TPU v7x, 8 devices: a whole 2x2x1 slice. The times are simulated.
8 devices in a mesh: dp: 1 (over z), tp: 8 (over y, x, core).
Axes of the slice: x: 2, y: 2, z: 1, core: 2. Of those that a mesh axis runs over, the one named last changes fastest.
Arguments:
- x_in: bfloat16 [3, 1536, 4096], P('dp', 'tp')
- positions: int32 [3, 1536], P('dp')
- prefix_len: int32 [3], P('dp')
- w_qkv: bfloat16 [4096, 12288], P(None, 'tp')
- b_qkv: bfloat16 [12288], P('tp')
- w_out: bfloat16 [4096, 4096], P('tp')
- b_out: bfloat16 [4096], replicated
- ln1_gain: bfloat16 [4096], replicated
- ln1_bias: bfloat16 [4096], replicated
- w_up: bfloat16 [4096, 28672], P(None, 'tp')
- b_up: bfloat16 [28672], P('tp')
- w_down: bfloat16 [14336, 4096], P('tp')
- b_down: bfloat16 [4096], replicated
- ln2_gain: bfloat16 [4096], replicated
- ln2_bias: bfloat16 [4096], replicated
Outputs:
- output: bfloat16 [3, 1536, 4096], P('dp', 'tp')
All inputs are finite; a program needn't handle non-finite values.
Results may differ from a plain program's by a relative error of at most 0.0193589.
Values are sent between devices in bfloat16 or wider.
A program may use at most 1 GiB of HBM per device.

v0:
```python
import math
import jax
import jax.numpy as jnp
from jax import lax
from jax.sharding import PartitionSpec as P

HEAD_DIM = 128
GLU_BLOCK = 128
DEEPNORM_ALPHA = math.sqrt(2.0 * 70)
LN_EPS = 1e-5
ROPE_BASE = 10000.0


def layer_norm(resid, ln_gain, ln_bias):
    mean_val = jnp.mean(resid, axis=-1, keepdims=True)
    centered = resid - mean_val
    var_val = jnp.mean(centered * centered, axis=-1, keepdims=True)
    return centered * lax.rsqrt(var_val + LN_EPS) * ln_gain.astype(jnp.float32) + ln_bias.astype(jnp.float32)


def rope_tables(positions):
    inv_freq = ROPE_BASE ** (jnp.arange(HEAD_DIM // 2, dtype=jnp.float32) * (-2.0 / HEAD_DIM))
    angles = positions.astype(jnp.float32)[:, :, None] * inv_freq
    return jnp.cos(angles)[:, :, None, :], jnp.sin(angles)[:, :, None, :]


def apply_rope(head_vec, cos_t, sin_t):
    half_dim = HEAD_DIM // 2
    lower_half = head_vec[..., :half_dim].astype(jnp.float32)
    upper_half = head_vec[..., half_dim:].astype(jnp.float32)
    rotated = jnp.concatenate([lower_half * cos_t - upper_half * sin_t, upper_half * cos_t + lower_half * sin_t], axis=-1)
    return rotated.astype(jnp.bfloat16)


def attention(q_rot, k_rot, v_all, prefix_len):
    batch_size, seq_len, num_heads, _ = q_rot.shape
    q_block = min(seq_len, 256)
    key_idx = jnp.arange(seq_len)
    attn_scale = HEAD_DIM ** -0.5

    def attend(blk_idx):
        q_start = blk_idx * q_block
        q_blk = lax.dynamic_slice_in_dim(q_rot, q_start, q_block, axis=1)
        scores = jnp.einsum('bqnd,bknd->bnqk', q_blk, k_rot, preferred_element_type=jnp.float32) * attn_scale
        q_idx = q_start + jnp.arange(q_block)
        visible = (key_idx[None, None, :] < prefix_len[:, None, None]) | (key_idx[None, None, :] <= q_idx[None, :, None])
        scores = jnp.where(visible[:, None, :, :], scores, -1e30)
        attn_probs = jax.nn.softmax(scores, axis=-1).astype(jnp.bfloat16)
        context = jnp.einsum('bnqk,bknd->bqnd', attn_probs, v_all, preferred_element_type=jnp.float32)
        return context.astype(jnp.bfloat16).reshape(batch_size, q_block, num_heads * HEAD_DIM)

    return lax.map(attend, jnp.arange(seq_len // q_block))


def glu_units(up_proj):
    lead_shape = up_proj.shape[:-1]
    paired = up_proj.reshape(lead_shape + (up_proj.shape[-1] // (2 * GLU_BLOCK), 2, GLU_BLOCK))
    value_part = paired[..., 0, :].astype(jnp.float32)
    gate_part = paired[..., 1, :].astype(jnp.float32)
    glu_out = (value_part * jax.nn.gelu(gate_part, approximate=True)).astype(jnp.bfloat16)
    return glu_out.reshape(lead_shape + (up_proj.shape[-1] // 2,))


def solution(mesh):
    def local_layer(x_loc, positions, prefix_len, w_qkv, b_qkv, w_out, b_out, ln1_gain, ln1_bias, w_up, b_up, w_down, b_down, ln2_gain, ln2_bias):
        batch_size, seq_loc, model_dim = x_loc.shape
        local_heads = w_qkv.shape[1] // (3 * HEAD_DIM)
        x_full = lax.all_gather(x_loc, 'tp', axis=1, tiled=True)
        seq_len = x_full.shape[1]
        qkv_all = jnp.einsum('bsh,hc->bsc', x_full, w_qkv, preferred_element_type=jnp.float32) + b_qkv.astype(jnp.float32)
        qkv_all = qkv_all.astype(jnp.bfloat16).reshape(batch_size, seq_len, local_heads, 3, HEAD_DIM)
        cos_t, sin_t = rope_tables(positions)
        q_rot = apply_rope(qkv_all[:, :, :, 0], cos_t, sin_t)
        k_rot = apply_rope(qkv_all[:, :, :, 1], cos_t, sin_t)
        context = attention(q_rot, k_rot, qkv_all[:, :, :, 2], prefix_len)
        attn_part = jnp.einsum('ibqc,ch->biqh', context, w_out, preferred_element_type=jnp.float32)
        attn_part = attn_part.astype(jnp.bfloat16).reshape(batch_size, seq_len, model_dim)
        attn_loc = lax.psum_scatter(attn_part, 'tp', scatter_dimension=1, tiled=True)
        resid1 = DEEPNORM_ALPHA * x_loc.astype(jnp.float32) + attn_loc.astype(jnp.float32) + b_out.astype(jnp.float32)
        mid_loc = layer_norm(resid1, ln1_gain, ln1_bias).astype(jnp.bfloat16)
        mid_full = lax.all_gather(mid_loc, 'tp', axis=1, tiled=True)
        up_proj = jnp.einsum('bsh,hf->bsf', mid_full, w_up, preferred_element_type=jnp.float32) + b_up.astype(jnp.float32)
        glu_out = glu_units(up_proj.astype(jnp.bfloat16))
        ffn_part = jnp.einsum('bsf,fh->bsh', glu_out, w_down, preferred_element_type=jnp.float32).astype(jnp.bfloat16)
        ffn_loc = lax.psum_scatter(ffn_part, 'tp', scatter_dimension=1, tiled=True)
        resid2 = DEEPNORM_ALPHA * mid_loc.astype(jnp.float32) + ffn_loc.astype(jnp.float32) + b_down.astype(jnp.float32)
        return layer_norm(resid2, ln2_gain, ln2_bias).astype(jnp.bfloat16)

    in_specs = (P('dp', 'tp', None), P('dp', None), P('dp'), P(None, 'tp'), P('tp'), P('tp', None), P(), P(), P(), P(None, 'tp'), P('tp'), P('tp', None), P(), P(), P())
    return jax.shard_map(local_layer, mesh=mesh, in_specs=in_specs, out_specs=P('dp', 'tp', None), check_vma=False)
```

profile of v0, /device:TPU:0, one launch (start us, length us, event | category | flops | bytes accessed | tf_op | source)
XLA Modules:
  0.0 2104.9 jit_solution(12955204281918623150)
XLA Ops:
  6.5 0.7 all-gather.3.cloned.1.call-update
  7.3 0.7 convert_element_type.102
  8.0 0.7 convert_element_type.105
  8.8 10.0 multiply_cosine_fusion
  18.8 166.6 %all-gather.3.cloned.1.call-done = bf16[3,1536,4096]{2,1,0:T(8,128)(2,1)} async-done(((bf16[3,192,4096]{2,1,0:T(8,128)(2,1)}), bf16[3,1536,4096]{2,1,0:T(8,128)(2,1)}) %all-gather.3.cloned.1.call-update) | async-done | bytes 37748752 | tf_op jit(solution)/shard_map/all_gather | solution.py:68
  185.4 68.3 %add_convert_fusion.1 = bf16[3,1536,1536]{1,2,0:T(8,128)(2,1)} fusion(bf16[3,1536,4096]{2,1,0:T(8,128)(2,1)} %all-gather.3.cloned.1.call-done, f32[1536]{0:T(1024)S(1)} %convert_element_type.102, bf16[4096,1536]{1,0:T(8,128)(2,1)} %param.20), kind=kOutput, calls=%fused_computation.41 | convolution fusion | flops 57996214272 | bytes 64493568 | tf_op jit(solution)/shard_map/bsh,hc->bsc/dot_general | solution.py:70
  253.6 11.0 slice_bitcast_fusion
  264.6 6.8 copy.31
  271.4 6.7 copy.32
  278.1 13.2 fusion.48
  291.3 7.1 pad_maximum_fusion
  298.4 148.5 %while.12 = (s32[]{:T(128)}, bf16[6,3,256,512]{2,3,1,0:T(8,128)(2,1)}, s32[3]{0:T(128)S(1)}, s32[6]{0:T(128)S(1)}, bf16[3,1536,4,128]{3,1,2,0:T(8,128)(2,1)}, /*...) while((s32[]{:T(128)}, ...), condition=%wide.region_3.4_spmd.clone.clone, body=%wide.region_0.3_spmd.clone.clone.sunk | while | flops 2446203136 | bytes 53513912 | solution.py:52
  300.4 12.5 fusion.80
  313.0 9.2 fusion.81
  322.2 0.9 constant_dynamic-update-slice_fusion.2
  325.2 12.6 fusion.80
  337.7 9.2 fusion.81
  347.0 0.9 constant_dynamic-update-slice_fusion.2
  349.9 12.6 fusion.80
  362.5 9.2 fusion.81
  371.7 0.9 constant_dynamic-update-slice_fusion.2
  374.7 12.6 fusion.80
  387.3 9.2 fusion.81
  396.5 0.9 constant_dynamic-update-slice_fusion.2
  399.5 12.6 fusion.80
  412.0 9.2 fusion.81
  421.2 0.9 constant_dynamic-update-slice_fusion.2
  424.2 12.6 fusion.80
  436.8 9.2 fusion.81
  446.0 0.9 constant_dynamic-update-slice_fusion.2
  446.9 27.8 %convert_bitcast_fusion = bf16[3,6,256,4096]{3,2,0,1:T(8,128)(2,1)} fusion(bf16[6,3,256,512]{2,3,1,0:T(8,128)(2,1)} %get-tuple-element.50, bf16[512,4096]{1,0:T(8,128)(2,1)} %param.22), kind=kOutput, calls=%fused_computation.26 | convolution fusion | flops 19346227200 | bytes 46661632 | tf_op jit(solution)/shard_map/ibqc,ch->biqh/dot_general | solution.py:76
  474.7 25.7 %copy.26 = bf16[3,6,256,4096]{3,2,1,0:T(8,128)(2,1)} copy(bf16[3,6,256,4096]{3,2,0,1:T(8,128)(2,1)} %convert_bitcast_fusion) | data formatting | bytes 75497472 | tf_op jit(solution)/shard_map/convert_element_type | solution.py:77
  501.1 215.7 %reduce-scatter.3.cloned.1.call-done = bf16[3,192,4096]{2,1,0:T(8,128)(2,1)} async-done(((bf16[3,1536,4096]{2,1,0:T(8,128)(2,1)}), bf16[3,192,4096]{2,1,0:T(8,128)(2,1)}) %reduce-scatter.3.cloned.1.call-update) | async-done | bytes 4718608 | tf_op jit(solution)/shard_map/reduce_scatter | solution.py:78
  716.9 5.8 fusion.51
  722.7 5.0 multiply_reduce_fusion.1
  727.8 4.9 add_convert_fusion.3
  732.8 173.3 %all-gather.5.cloned.1.call-done = bf16[3,1536,4096]{2,1,0:T(8,128)(2,1)} async-done(((bf16[3,192,4096]{2,1,0:T(8,128)(2,1)}), bf16[3,1536,4096]{2,1,0:T(8,128)(2,1)}) %all-gather.5.cloned.1.call-update) | async-done | bytes 37748752 | tf_op jit(solution)/shard_map/all_gather | solution.py:81
  906.1 147.2 %add_convert_fusion = bf16[3,1536,3584]{2,1,0:T(8,128)(2,1)} fusion(bf16[3,1536,4096]{2,1,0:T(8,128)(2,1)} %all-gather.5.cloned.1.call-done, f32[3584]{0:T(1024)S(1)} %convert_element_type.117, bf16[4096,3584]{1,0:T(8,128)(2,1)} %param.26), kind=kOutput, calls=%fused_computation.24 | convolution fusion | flops 135324499968 | bytes 100153344 | tf_op jit(solution)/shard_map/bsh,hf->bsf/dot_general | solution.py:82
  1053.3 63.2 %reshape.130 = bf16[3,1536,14,2,128]{4,3,2,1,0:T(2,128)(2,1)} reshape(bf16[3,1536,3584]{2,1,0:T(8,128)(2,1)} %add_convert_fusion) | data formatting | bytes 66060288 | tf_op jit(solution)/shard_map/reshape | solution.py:57
  1116.5 288.3 %fusion.34 = f32[3,1536,14,128]{3,2,1,0:T(8,128)} fusion(bf16[3,1536,14,2,128]{4,3,2,1,0:T(2,128)(2,1)} %reshape.130), kind=kLoop, calls=%fused_computation.39 | loop fusion | flops 8257536 | bytes 49545216 | tf_op jit(solution)/shard_map/convert_element_type | solution.py:58
  1404.8 305.1 %fusion.33 = f32[3,1536,14,128]{3,2,1,0:T(8,128)} fusion(bf16[3,1536,14,2,128]{4,3,2,1,0:T(2,128)(2,1)} %reshape.130), kind=kLoop, calls=%fused_computation.37 | loop fusion | flops 8257536 | bytes 49545216 | tf_op jit(solution)/shard_map/convert_element_type | solution.py:59
  1709.9 36.3 %reshape.131 = f32[3,1536,1792]{2,1,0:T(8,128)} reshape(f32[3,1536,14,128]{3,2,1,0:T(8,128)} %fusion.34) | data formatting | bytes 66060288 | tf_op jit(solution)/shard_map/convert_element_type | solution.py:58
  1746.2 36.5 %reshape.132 = f32[3,1536,1792]{2,1,0:T(8,128)} reshape(f32[3,1536,14,128]{3,2,1,0:T(8,128)} %fusion.33) | data formatting | bytes 66060288 | tf_op jit(solution)/shard_map/convert_element_type | solution.py:59
  1782.7 83.0 %convolution_convert_fusion = bf16[3,1536,4096]{2,1,0:T(8,128)(2,1)} fusion(f32[3,1536,1792]{2,1,0:T(8,128)} %reshape.131, f32[3,1536,1792]{2,1,0:T(8,128)} %reshape.132, bf16[1792,4096]{1,0:T(8,128)(2,1)} %param.28), kind=kOutput, calls=%fused_computation.42 | convolution fusion | flops 67747184640 | bytes 118489088 | tf_op jit(solution)/shard_map/bsf,fh->bsh/dot_general | solution.py:84
  1866.4 215.8 %reduce-scatter.5.cloned.1.call-done = bf16[3,192,4096]{2,1,0:T(8,128)(2,1)} async-done(((bf16[3,1536,4096]{2,1,0:T(8,128)(2,1)}), bf16[3,192,4096]{2,1,0:T(8,128)(2,1)}) %reduce-scatter.5.cloned.1.call-update) | async-done | bytes 4718608 | tf_op jit(solution)/shard_map/reduce_scatter | solution.py:85
  2082.2 5.8 fusion.52
  2088.0 5.0 multiply_reduce_fusion
  2093.1 4.9 add_convert_fusion.2
  (83 shorter events, 10.4 us)
Async XLA Ops:
  6.5 178.8 %all-gather.3.cloned.1.call-start = ((), (), s32[]{:S(2)}) async-start(), calls=%async_computation.2 | async-start | bytes 42467328 | tf_op jit(solution)/shard_map/all_gather | solution.py:68
  7.3 709.6 %reduce-scatter.3.cloned.1.call-start = ((), (), s32[]{:S(2)}) async-start(), calls=%async_computation.3 | async-start | bytes 42467328 | tf_op jit(solution)/shard_map/reduce_scatter | solution.py:78
  264.6 13.5 copy-start.2
  291.3 7.1 copy-start.3
  500.4 0.7 copy-start.4
  500.4 0.7 copy-start.5
  500.4 0.7 copy-start.6
  500.4 405.6 %all-gather.5.cloned.1.call-start = ((), (), s32[]{:S(2)}) async-start(), calls=%async_computation.4 | async-start | bytes 42467328 | tf_op jit(solution)/shard_map/all_gather | solution.py:81
  501.1 226.6 %slice-start.2 = ((s8[4718592]{0:T(1024)(128)(4,1)}), s8[524288]{0:T(1024)(128)(4,1)S(1)}, s32[]{:S(2)}) async-start(s8[4718592]{0:T(1024)(128)(4,1)} %bitcast.46), calls=%async_computation.8 | async-start | bytes 1048576
  716.9 5.8 copy-start
  722.7 5.1 slice-start.3
  727.8 5.0 copy-start.7
  732.7 1349.5 %reduce-scatter.5.cloned.1.call-start = ((), (), s32[]{:S(2)}) async-start(), calls=%async_computation.5 | async-start | bytes 42467328 | tf_op jit(solution)/shard_map/reduce_scatter | solution.py:85
  1865.7 0.7 copy-start.8
  1865.7 0.7 copy-start.9
  1865.7 0.7 copy-start.10
  1866.4 226.7 %slice-start = ((s8[4718592]{0:T(1024)(128)(4,1)}), s8[524288]{0:T(1024)(128)(4,1)S(1)}, s32[]{:S(2)}) async-start(s8[4718592]{0:T(1024)(128)(4,1)} %bitcast.44), calls=%async_computation.6 | async-start | bytes 1048576
  2082.2 5.8 copy-start.1
  2088.0 5.1 slice-start.1
Sparse Core Ops, SparseCore 0:
  9.2 176.1 all-gather.2
  500.6 216.2 reduce-scatter.2
  732.8 173.2 all-gather.4
  1865.8 216.3 reduce-scatter.4
where the time goes:
time: 2120 us; the launch traced here: 2100 us
  waiting for transfers between devices  772 us (36%)
  other arithmetic  662 us (31%)
  matrix products  457 us (22%)
  local copies, waits for them, and re-layouts  197 us (9%)
    convert_element_type x1, other arithmetic, glu_units(): gate_part = paired[..., 1, :].astype(jnp.float32)  305 us
    convert_element_type x1, other arithmetic, glu_units(): value_part = paired[..., 0, :].astype(jnp.float32)  288 us
    reduce_scatter x1, waiting for transfers between devices, local_layer(): ffn_loc = lax.psum_scatter(ffn_part, 'tp', scatter_dimension=1, tiled=True)  216 us
    reduce_scatter x1, waiting for transfers between devices, local_layer(): lax.psum_scatter(attn_part, 'tp', scatter_dimension=1, tiled=True)  216 us
    all_gather x1, waiting for transfers between devices, local_layer(): mid_full = lax.all_gather(mid_loc, 'tp', axis=1, tiled=True)  173 us
    all_gather x1, waiting for transfers between devices, local_layer(): x_full = lax.all_gather(x_loc, 'tp', axis=1, tiled=True)  167 us
    dot_general x1, matrix products, local_layer(): jnp.einsum('bsh,hf->bsf', mid_full, w_up, preferred_element_type=jnp.floa...  147 us
    dot_general x1, matrix products, local_layer(): jnp.einsum('bsf,fh->bsh', glu_out, w_down, preferred_element_type=jnp.flo...  83 us
  transfers between devices with their start and end apart: 4, of which 4 were waited for; matrix products, arithmetic and copies ran while one was open for 1% of the time, Pallas kernels for 0%

commit v1 on v0

v1 whole, which is shorter than its diff:
```python
import functools
import math
import jax
import jax.numpy as jnp
from jax import lax
from jax.experimental import pallas as pl
from jax.experimental.pallas import tpu as pltpu
from jax.sharding import PartitionSpec as P

HEAD_DIM = 128
GLU_BLOCK = 128
DEEPNORM_ALPHA = math.sqrt(2.0 * 70)
LN_EPS = 1e-5
ROPE_BASE = 10000.0
F32 = jnp.float32
BF16 = jnp.bfloat16


def layer_norm(resid, ln_gain, ln_bias):
    mean_val = jnp.mean(resid, axis=-1, keepdims=True)
    centered = resid - mean_val
    var_val = jnp.mean(centered * centered, axis=-1, keepdims=True)
    return centered * lax.rsqrt(var_val + LN_EPS) * ln_gain.astype(F32) + ln_bias.astype(F32)


def rope_tables(positions):
    inv_freq = ROPE_BASE ** (jnp.arange(HEAD_DIM // 2, dtype=F32) * (-2.0 / HEAD_DIM))
    angles = positions.astype(F32)[:, :, None] * inv_freq
    cos_t, sin_t = jnp.cos(angles), jnp.sin(angles)
    return jnp.concatenate([cos_t, cos_t], axis=-1), jnp.concatenate([-sin_t, sin_t], axis=-1)


def rotate(vec, cos_t, sin_t):
    wide = vec.astype(F32)
    return (wide * cos_t + pltpu.roll(wide, HEAD_DIM // 2, 1) * sin_t).astype(BF16)


def attn_kernel(rows, seq_len, key_block, info, qkv_ref, cos_ref, sin_ref, mine_ref, other_ref, k_ref):
    q_blk = pl.program_id(1)
    prefix, core = info[0], info[1]
    q_rows = 2 * rows

    @pl.when(q_blk == 0)
    def _():
        k_ref[...] = rotate(qkv_ref[:, HEAD_DIM:2 * HEAD_DIM], cos_ref[...], sin_ref[...])

    q_start = pl.multiple_of(q_blk * q_rows, q_rows)
    limit = jnp.maximum(prefix, q_start + q_rows)
    need = lax.div(limit + (key_block - 1), key_block)
    exp_scale = HEAD_DIM ** -0.5 * math.log2(math.e)

    def half(which, keys):
        at = pl.multiple_of(q_start + which * rows, rows)
        here = pl.ds(at, rows)
        q_rot = rotate(qkv_ref[here, 0:HEAD_DIM], cos_ref[here, :], sin_ref[here, :])
        scores = lax.dot_general(q_rot, k_ref[0:keys, :], (((1,), (1,)), ((), ())), preferred_element_type=F32)
        row_last = jnp.maximum(lax.broadcasted_iota(jnp.int32, (rows, 1), 0) + at, prefix - 1)
        key_idx = lax.broadcasted_iota(jnp.int32, (rows, keys), 1)
        scores = jnp.where(key_idx <= row_last, scores, -1e30)
        top = jnp.max(scores, axis=-1, keepdims=True)
        probs = jnp.exp2(scores * exp_scale - top * exp_scale)
        inv_sum = 1.0 / jnp.sum(probs, axis=-1, keepdims=True)
        probs = (probs * inv_sum).astype(BF16)
        v_all = qkv_ref[0:keys, 2 * HEAD_DIM:3 * HEAD_DIM]
        return jnp.dot(probs, v_all, preferred_element_type=F32)

    for blocks in range(1, seq_len // key_block + 1):
        @pl.when(need == blocks)
        def _(keys=blocks * key_block):
            first, second = half(0, keys), half(1, keys)
            mine_ref[...] = jnp.where(core == 0, first, second).astype(BF16)
            other_ref[...] = jnp.where(core == 0, second, first).astype(BF16)


def attention(info, qkv, cos_t, sin_t, rows):
    seq_len, width = qkv.shape
    heads = width // (3 * HEAD_DIM)
    half_len = seq_len // 2
    key_block = 2 * rows
    out = jax.ShapeDtypeStruct((half_len, heads * HEAD_DIM), BF16)
    out_spec = pl.BlockSpec((rows, HEAD_DIM), lambda h, i, info: (i, h))
    return pl.pallas_call(
        functools.partial(attn_kernel, rows, seq_len, key_block),
        out_shape=(out, out),
        grid_spec=pltpu.PrefetchScalarGridSpec(
            num_scalar_prefetch=1,
            grid=(heads, seq_len // (2 * rows)),
            in_specs=[
                pl.BlockSpec((seq_len, 3 * HEAD_DIM), lambda h, i, info: (0, h)),
                pl.BlockSpec((seq_len, HEAD_DIM), lambda h, i, info: (0, 0)),
                pl.BlockSpec((seq_len, HEAD_DIM), lambda h, i, info: (0, 0)),
            ],
            out_specs=[out_spec, out_spec],
            scratch_shapes=[pltpu.VMEM((seq_len, HEAD_DIM), BF16)],
        ),
        compiler_params=pltpu.CompilerParams(vmem_limit_bytes=40 << 20),
        cost_estimate=pl.CostEstimate(flops=24 * 10 ** 9, bytes_accessed=12 << 20, transcendentals=heads * seq_len * seq_len),
        name='attention',
    )(info, qkv, cos_t, sin_t)


def split_kernel(w_ref, value_ref, gate_ref):
    value_ref[...] = w_ref[:, :GLU_BLOCK]
    gate_ref[...] = w_ref[:, GLU_BLOCK:]


def split_pairs(w_up):
    depth, width = w_up.shape
    out = jax.ShapeDtypeStruct((depth, width // 2), w_up.dtype)
    spec = pl.BlockSpec((depth, GLU_BLOCK), lambda j: (0, j))
    return pl.pallas_call(
        split_kernel,
        out_shape=(out, out),
        grid=(width // (2 * GLU_BLOCK),),
        in_specs=[pl.BlockSpec((depth, 2 * GLU_BLOCK), lambda j: (0, j))],
        out_specs=[spec, spec],
        compiler_params=pltpu.CompilerParams(vmem_limit_bytes=24 << 20),
        cost_estimate=pl.CostEstimate(flops=18 * 10 ** 9, bytes_accessed=4 * depth * width, transcendentals=0),
        name='split_pairs',
    )(w_up)


def mm(lhs, rhs):
    return jnp.dot(lhs, rhs, preferred_element_type=F32)


def glu(rows, w_pair, b_pair):
    value = (mm(rows, w_pair[0]) + b_pair[0].astype(F32)).astype(BF16)
    gate = (mm(rows, w_pair[1]) + b_pair[1].astype(F32)).astype(BF16)
    return (value.astype(F32) * jax.nn.gelu(gate.astype(F32), approximate=True)).astype(BF16)


def two_part_sum(lhs_pair, rhs_pair):
    first = mm(lhs_pair[0], rhs_pair[0]).astype(BF16)
    second = mm(lhs_pair[1], rhs_pair[1]).astype(BF16)
    return (first.astype(F32) + second.astype(F32)).astype(BF16)


def solution(mesh):
    tp = mesh.shape['tp']
    swap = [(i, i ^ 1) for i in range(tp)]
    same_core = [list(range(0, tp, 2)), list(range(1, tp, 2))]

    def partner(val):
        return lax.ppermute(val, 'tp', swap)

    def local_layer(x_loc, positions, prefix_len, w_qkv, b_qkv, w_out, b_out, ln1_gain, ln1_bias, w_up, b_up, w_down, b_down, ln2_gain, ln2_bias):
        batch_size, seq_loc, model_dim = x_loc.shape
        core = lax.axis_index('tp') % 2
        gathered = [lax.all_gather(x_loc[b], 'tp', axis=0, tiled=True) for b in range(batch_size)]
        cos_t, sin_t = rope_tables(positions)
        w_pair = split_pairs(w_up)
        b_rows = b_up.reshape(-1, 2, GLU_BLOCK)
        b_pair = (b_rows[:, 0].reshape(-1), b_rows[:, 1].reshape(-1))
        outs_w = (w_out, partner(w_out))
        down_w = (w_down, partner(w_down))
        up_w = (w_pair, (partner(w_pair[0]), partner(w_pair[1])))
        b_other = partner(jnp.stack(b_pair))
        up_b = (b_pair, (b_other[0], b_other[1]))

        attn_loc = []
        for b in range(batch_size):
            qkv = (mm(gathered[b], w_qkv) + b_qkv.astype(F32)).astype(BF16)
            info = jnp.stack([prefix_len[b], core]).astype(jnp.int32)
            mine, other = attention(info, qkv, cos_t[b], sin_t[b], seq_loc)
            part = two_part_sum((mine, partner(other)), outs_w)
            attn_loc.append(lax.psum_scatter(part, 'tp', scatter_dimension=0, axis_index_groups=same_core, tiled=True))

        mids, fulls = [], []
        for b in range(batch_size):
            resid1 = DEEPNORM_ALPHA * x_loc[b].astype(F32) + attn_loc[b].astype(F32) + b_out.astype(F32)
            mids.append(layer_norm(resid1, ln1_gain, ln1_bias).astype(BF16))
            fulls.append(lax.all_gather(mids[b], 'tp', axis=0, axis_index_groups=same_core, tiled=True))

        outs = []
        for b in range(batch_size):
            acts = tuple(glu(fulls[b], up_w[i], up_b[i]) for i in range(2))
            part = two_part_sum(acts, down_w)
            ffn_loc = lax.psum_scatter(part, 'tp', scatter_dimension=0, axis_index_groups=same_core, tiled=True)
            resid2 = DEEPNORM_ALPHA * mids[b].astype(F32) + ffn_loc.astype(F32) + b_down.astype(F32)
            outs.append(layer_norm(resid2, ln2_gain, ln2_bias).astype(BF16))
        return jnp.stack(outs)

    in_specs = (P('dp', 'tp', None), P('dp', None), P('dp'), P(None, 'tp'), P('tp'), P('tp', None), P(), P(), P(), P(None, 'tp'), P('tp'), P('tp', None), P(), P(), P())
    return jax.shard_map(local_layer, mesh=mesh, in_specs=in_specs, out_specs=P('dp', 'tp', None), check_vma=False)
```

time: 2120 us -> 917 us (0.43)
  other arithmetic: 662 us -> 45.9 us
  waiting for transfers between devices: 772 us -> 297 us
  local copies, waits for them, and re-layouts: 197 us -> 13.9 us
  Pallas kernels: 0 us -> 96.9 us
    convert_element_type x13 -> x10, other arithmetic: 605 us -> 5.99 us  [the longest x1 5.92 us: local_layer(): mids.append(layer_norm(resid1, ln1_gain, ln1_bias).astype(BF16))]
    all_gather x2 -> x6, waiting for transfers between devices: 340 us -> 76.7 us  [the longest x3 61.1 us: local_layer(): lax.all_gather(x_loc[b], 'tp', axis=0, tiled=True)]
    reduce_scatter x2 -> x6, waiting for transfers between devices: 432 us -> 197 us  [local_layer(): lax.psum_scatter(part, 'tp', scatter_dimension=0, axis_index_groups=same_...]
    convert_element_type x3 -> x0, local copies, waits for them, and re-layouts: 98.5 us -> none  [the longest x1 36.5 us: glu_units(): gate_part = paired[..., 1, :].astype(jnp.float32)]
    pallas_call x0 -> x4, Pallas kernels: none -> 96.9 us  [the longest x3 76.7 us: attention(): pl.pallas_call(functools.partial(attn_kernel, rows, seq_len, key_block),...]
    sub x6 -> x0, matrix products: 75.3 us -> none  [attend(): attn_probs = jax.nn.softmax(scores, axis=-1).astype(jnp.bfloat16)]
    reshape x1, local copies, waits for them, and re-layouts: 63.2 us -> 0.02 us  [local_layer(): b_rows = b_up.reshape(-1, 2, GLU_BLOCK)]
    dot_general x10 -> x24, matrix products: 381 us -> 437 us  [mm(): return jnp.dot(lhs, rhs, preferred_element_type=F32)]
  transfers between devices with their start and end apart: 4 -> 20, of which waited for: 4 -> 9; matrix products, arithmetic and copies ran while one was open for 1% -> 50% of each run, Pallas kernels for 0% -> 11%
where the time goes in v1:
time: 917 us; the launch traced here: 909 us
  matrix products  437 us (48%)
  waiting for transfers between devices  297 us (32%)
  Pallas kernels  96.9 us (11%)
  other arithmetic  45.9 us (5%)
  between operations  14.8 us (2%)
  local copies, waits for them, and re-layouts  13.9 us (2%)
    dot_general x24, matrix products, mm(): return jnp.dot(lhs, rhs, preferred_element_type=F32)  437 us
    reduce_scatter x6, waiting for transfers between devices, local_layer(): lax.psum_scatter(part, 'tp', scatter_dimension=0, axis_index_groups=same_...  197 us
    pallas_call x3, Pallas kernels, attention(): pl.pallas_call(functools.partial(attn_kernel, rows, seq_len, key_block),...  76.7 us
    all_gather x3, waiting for transfers between devices, local_layer(): lax.all_gather(x_loc[b], 'tp', axis=0, tiled=True)  61.1 us
    ppermute x8, waiting for transfers between devices, partner(): return lax.ppermute(val, 'tp', swap)  21 us
    pallas_call x1, Pallas kernels, split_pairs(): pl.pallas_call(split_kernel, out_shape=(out, out), grid=(width // (2 * GL...  20.1 us
  transfers between devices with their start and end apart: 20, of which 9 were waited for; matrix products, arithmetic and copies ran while one was open for 50% of the time, Pallas kernels for 11%

profile of v1, /device:TPU:0, one launch (start us, length us, event | category | flops | bytes accessed | tf_op | source)
XLA Modules:
  0.0 908.8 jit_solution(15964521918911079426)
XLA Ops:
  6.5 4.7 fusion.109
  15.1 8.4 fusion.94
  23.4 2.5 fusion.87
  25.9 54.6 %all-gather.16.cloned.1.call-done = bf16[1,1536,4096]{2,1,0:T(8,128)(2,1)} async-done(((bf16[1,192,4096]{2,1,0:T(8,128)(2,1)}), bf16[1,1536,4096]{2,1,0:T(8,128)(2,1)}) %all-gather.16.cloned.1.call-update) | async-done | bytes 12582928 | tf_op jit(solution)/shard_map/all_gather | solution.py:150
  80.5 26.1 %fusion.21.qkv_ref = bf16[1536,1536]{1,0:T(8,128)(2,1)S(1)} fusion(bf16[4096,1536]{1,0:T(8,128)(2,1)} %param.18, bf16[1,1536,4096]{2,1,0:T(8,128)(2,1)} %all-gather.16.cloned.1.call-done, f32[1536]{0:T(1024)S(1)} %convert_element_type.314), kind=kOutput, calls=%fused_computation.41 | convolution fusion | flops 19332071424 | bytes 29890560 | tf_op jit(solution)/shard_map/dot_general | solution.py:124
  106.7 25.3 %attention.3 = (bf16[768,512]{1,0:T(8,128)(2,1)S(1)}, bf16[768,512]{1,0:T(8,128)(2,1)S(1)}) custom-call(s32[2]{0:T(128)S(1)} %pad_add_fusion.info, bf16[1536,1536]{1,0:T(8,128)(2,1)S(1)} %fusion.21.qkv_ref, f32[1536,128]{1,0:T(8,128)S(1)} %copy-done.1, f32[1536,128]{1,0:T(8,128)S(1)} %copy-done), custom_call_target="tpu_custom_call" | custom-call | flops 24000000000 | bytes 12582912 | tf_op jit(solution)/shard_map/attention/pallas_call | solution.py:82
  132.4 3.6 convolution_convert_fusion.5
  136.0 7.5 add_convert_fusion.5
  144.3 4.3 all-gather.18.cloned.1.call-done
  148.7 26.2 %fusion.18.qkv_ref = bf16[1536,1536]{1,0:T(8,128)(2,1)S(1)} fusion(bf16[4096,1536]{1,0:T(8,128)(2,1)} %param.18, bf16[1,1536,4096]{2,1,0:T(8,128)(2,1)} %all-gather.18.cloned.1.call-done, f32[1536]{0:T(1024)S(1)} %convert_element_type.314), kind=kOutput, calls=%fused_computation.40 | convolution fusion | flops 19332071424 | bytes 29890560 | tf_op jit(solution)/shard_map/dot_general | solution.py:124
  174.9 27.4 %attention.4 = (bf16[768,512]{1,0:T(8,128)(2,1)S(1)}, bf16[768,512]{1,0:T(8,128)(2,1)S(1)}) custom-call(s32[2]{0:T(128)S(1)} %pad_add_fusion.1.info, bf16[1536,1536]{1,0:T(8,128)(2,1)S(1)} %fusion.18.qkv_ref, f32[1536,128]{1,0:T(8,128)S(1)} %get-tuple-element.58.cos_ref, f32[1536,128]{1,0:T(8,128)S(1)} %get-tuple-element.40.sin_ref), custom_call_target="tpu_custom_call" | custom-call | flops 24000000000 | bytes 12582912 | tf_op jit(solution)/shard_map/attention/pallas_call | solution.py:82
  202.6 3.6 convolution_convert_fusion.3
  206.3 7.7 add_convert_fusion.3
  214.8 2.2 all-gather.20.cloned.1.call-done
  216.9 26.0 %fusion.15.qkv_ref = bf16[1536,1536]{1,0:T(8,128)(2,1)S(1)} fusion(bf16[4096,1536]{1,0:T(8,128)(2,1)} %param.18, bf16[1,1536,4096]{2,1,0:T(8,128)(2,1)} %all-gather.20.cloned.1.call-done, f32[1536]{0:T(1024)S(1)} %convert_element_type.314), kind=kOutput, calls=%fused_computation.39 | convolution fusion | flops 19332071424 | bytes 29890560 | tf_op jit(solution)/shard_map/dot_general | solution.py:124
  243.0 23.9 %attention.5 = (bf16[768,512]{1,0:T(8,128)(2,1)S(1)}, bf16[768,512]{1,0:T(8,128)(2,1)S(1)}) custom-call(s32[2]{0:T(128)S(1)} %pad_add_fusion.2.info, bf16[1536,1536]{1,0:T(8,128)(2,1)S(1)} %fusion.15.qkv_ref, f32[1536,128]{1,0:T(8,128)S(1)} %get-tuple-element.59.cos_ref, f32[1536,128]{1,0:T(8,128)S(1)} %get-tuple-element.39.sin_ref), custom_call_target="tpu_custom_call" | custom-call | flops 24000000000 | bytes 12582912 | tf_op jit(solution)/shard_map/attention/pallas_call | solution.py:82
  267.2 3.6 convolution_convert_fusion.1
  270.8 7.9 add_convert_fusion.1
  279.5 4.5 reduce-scatter.7.cloned.1.call-done
  284.0 2.6 fusion.78
  286.6 64.5 %reduce-scatter.11.cloned.1.call-done = bf16[192,4096]{1,0:T(8,128)(2,1)} async-done(((bf16[768,4096]{1,0:T(8,128)(2,1)}), bf16[192,4096]{1,0:T(8,128)(2,1)}) %reduce-scatter.11.cloned.1.call-update) | async-done | bytes 1572880 | tf_op jit(solution)/shard_map/reduce_scatter | solution.py:167
  351.1 67.1 %reduce-scatter.15.cloned.1.call-done = bf16[192,4096]{1,0:T(8,128)(2,1)} async-done(((bf16[768,4096]{1,0:T(8,128)(2,1)}), bf16[192,4096]{1,0:T(8,128)(2,1)}) %reduce-scatter.15.cloned.1.call-update) | async-done | bytes 1572880 | tf_op jit(solution)/shard_map/reduce_scatter | solution.py:167
  418.2 4.9 multiply_reduce_fusion.5
  423.2 3.7 multiply_reduce_fusion.3
  426.9 5.9 add_convert_fusion.23
  433.7 20.1 %split_pairs.1 = (bf16[4096,1792]{1,0:T(8,128)(2,1)}, bf16[4096,1792]{1,0:T(8,128)(2,1)S(1)}) custom-call(bf16[4096,3584]{1,0:T(8,128)(2,1)} %w_ref.1), custom_call_target="tpu_custom_call" | custom-call | flops 17999998976 | bytes 58720256 | tf_op jit(solution)/shard_map/split_pairs/pallas_call | solution.py:111
  453.8 5.1 copy-done.2
  460.1 21.0 %collective-permute-done.3 = bf16[2,1792]{1,0:T(2,128)(2,1)S(1)} collective-permute-done((bf16[2,1792]{1,0:T(2,128)(2,1)S(1)}, bf16[2,1792]{1,0:T(2,128)(2,1)S(1)}, u32[]{:S(2)}, u32[]{:S(2)}) %collective-permute-start.3) | collective-permute-done | bytes 7200 | tf_op jit(solution)/shard_map/ppermute | solution.py:145
  481.8 15.5 %all-gather.10.cloned.1.call-done = bf16[768,4096]{1,0:T(8,128)(2,1)} async-done(((bf16[192,4096]{1,0:T(8,128)(2,1)}), bf16[768,4096]{1,0:T(8,128)(2,1)}) %all-gather.10.cloned.1.call-update) | async-done | bytes 6291472 | tf_op jit(solution)/shard_map/all_gather | solution.py:173
  497.3 17.8 %add_convert_fusion.17 = bf16[768,1792]{1,0:T(8,128)(2,1)S(1)} fusion(bf16[768,4096]{1,0:T(8,128)(2,1)} %all-gather.10.cloned.1.call-done, bf16[4096,1792]{1,0:T(8,128)(2,1)} %get-tuple-element.15, f32[1792]{0:T(1024)S(1)} %bitcast.127), kind=kOutput, calls=%fused_computation.107 | convolution fusion | flops 11277041664 | bytes 23731200 | tf_op jit(solution)/shard_map/dot_general | solution.py:124
  515.2 37.3 %convolution_convert_fusion.11 = bf16[768,4096]{1,0:T(8,128)(2,1)} fusion(bf16[1792,4096]{1,0:T(8,128)(2,1)} %param.26, bf16[768,1792]{1,0:T(8,128)(2,1)S(1)} %add_convert_fusion.17, bf16[768,4096]{1,0:T(8,128)(2,1)} %all-gather.10.cloned.1.call-done, bf16[4096,1792]{1,0:T(8,128)(2,1)} %copy-done.2, f32[1792]{0:T(1024)S(1)} %bitcast.124), kind=kOutput, calls=%fused_computation.53 | convolution fusion | flops 22570991616 | bytes 44702720 | tf_op jit(solution)/shard_map/dot_general | solution.py:124
  552.5 18.2 %add_convert_fusion.15 = bf16[768,1792]{1,0:T(8,128)(2,1)S(1)} fusion(bf16[768,4096]{1,0:T(8,128)(2,1)} %all-gather.10.cloned.1.call-done, bf16[4096,1792]{1,0:T(8,128)(2,1)} %collective-permute-done.2, f32[1792]{0:T(1024)S(1)} %copy-done.26), kind=kOutput, calls=%fused_computation.105 | convolution fusion | flops 11277041664 | bytes 23731200 | tf_op jit(solution)/shard_map/dot_general | solution.py:124
  570.8 18.1 %fusion.37 = bf16[768,1792]{1,0:T(8,128)(2,1)S(1)} fusion(bf16[768,1792]{1,0:T(8,128)(2,1)S(1)} %add_convert_fusion.15, bf16[768,4096]{1,0:T(8,128)(2,1)S(1)} %copy-done.32, bf16[4096,1792]{1,0:T(8,128)(2,1)} %collective-permute-done.4, f32[1792]{0:T(1024)S(1)} %copy-done.20), kind=kOutput, calls=%fused_computation.67 | convolution fusion | flops 11293556736 | bytes 26483712 | tf_op jit(solution)/shard_map/dot_general | solution.py:124
  588.9 17.0 %add_convert_fusion.4 = bf16[768,4096]{1,0:T(8,128)(2,1)} fusion(bf16[768,4096]{1,0:T(8,128)(2,1)S(1)} %bitcast.131, bf16[768,1792]{1,0:T(8,128)(2,1)S(1)} %fusion.37, bf16[1792,4096]{1,0:T(8,128)(2,1)} %collective-permute-done.5), kind=kOutput, calls=%fused_computation.10 | convolution fusion | flops 11290017792 | bytes 30015488 | tf_op jit(solution)/shard_map/dot_general | solution.py:124
  606.6 17.8 %add_convert_fusion.13 = bf16[768,1792]{1,0:T(8,128)(2,1)S(1)} fusion(bf16[768,4096]{1,0:T(8,128)(2,1)} %all-gather.12.cloned.1.call-done, bf16[4096,1792]{1,0:T(8,128)(2,1)} %get-tuple-element.15, f32[1792]{0:T(1024)S(1)} %bitcast.128), kind=kOutput, calls=%fused_computation.103 | convolution fusion | flops 11277041664 | bytes 23731200 | tf_op jit(solution)/shard_map/dot_general | solution.py:124
  624.4 37.2 %convolution_convert_fusion.9 = bf16[768,4096]{1,0:T(8,128)(2,1)} fusion(bf16[1792,4096]{1,0:T(8,128)(2,1)} %param.26, bf16[768,1792]{1,0:T(8,128)(2,1)S(1)} %add_convert_fusion.13, bf16[768,4096]{1,0:T(8,128)(2,1)} %all-gather.12.cloned.1.call-done, bf16[4096,1792]{1,0:T(8,128)(2,1)} %copy-done.2, f32[1792]{0:T(1024)S(1)} %bitcast.125), kind=kOutput, calls=%fused_computation.51 | convolution fusion | flops 22570991616 | bytes 44702720 | tf_op jit(solution)/shard_map/dot_general | solution.py:124
  661.7 18.2 %add_convert_fusion.11 = bf16[768,1792]{1,0:T(8,128)(2,1)S(1)} fusion(bf16[768,4096]{1,0:T(8,128)(2,1)} %all-gather.12.cloned.1.call-done, bf16[4096,1792]{1,0:T(8,128)(2,1)} %collective-permute-done.2, f32[1792]{0:T(1024)S(1)} %copy-done.27), kind=kOutput, calls=%fused_computation.101 | convolution fusion | flops 11277041664 | bytes 23731200 | tf_op jit(solution)/shard_map/dot_general | solution.py:124
  679.9 18.1 %fusion.51 = bf16[768,1792]{1,0:T(8,128)(2,1)S(1)} fusion(bf16[768,1792]{1,0:T(8,128)(2,1)S(1)} %add_convert_fusion.11, bf16[768,4096]{1,0:T(8,128)(2,1)S(1)} %copy-done.31, bf16[4096,1792]{1,0:T(8,128)(2,1)} %collective-permute-done.4, f32[1792]{0:T(1024)S(1)} %copy-done.21), kind=kOutput, calls=%fused_computation.81 | convolution fusion | flops 11293556736 | bytes 26483712 | tf_op jit(solution)/shard_map/dot_general | solution.py:124
  698.0 17.0 %add_convert_fusion.2 = bf16[768,4096]{1,0:T(8,128)(2,1)} fusion(bf16[768,4096]{1,0:T(8,128)(2,1)S(1)} %bitcast.135, bf16[768,1792]{1,0:T(8,128)(2,1)S(1)} %fusion.51, bf16[1792,4096]{1,0:T(8,128)(2,1)} %collective-permute-done.5), kind=kOutput, calls=%fused_computation.8 | convolution fusion | flops 11290017792 | bytes 30015488 | tf_op jit(solution)/shard_map/dot_general | solution.py:124
  715.8 17.8 %add_convert_fusion.9 = bf16[768,1792]{1,0:T(8,128)(2,1)S(1)} fusion(bf16[768,4096]{1,0:T(8,128)(2,1)} %all-gather.14.cloned.1.call-done, bf16[4096,1792]{1,0:T(8,128)(2,1)} %get-tuple-element.15, f32[1792]{0:T(1024)S(1)} %bitcast.129), kind=kOutput, calls=%fused_computation.99 | convolution fusion | flops 11277041664 | bytes 23731200 | tf_op jit(solution)/shard_map/dot_general | solution.py:124
  733.6 37.1 %convolution_convert_fusion.7 = bf16[768,4096]{1,0:T(8,128)(2,1)} fusion(bf16[1792,4096]{1,0:T(8,128)(2,1)} %param.26, bf16[768,1792]{1,0:T(8,128)(2,1)S(1)} %add_convert_fusion.9, bf16[768,4096]{1,0:T(8,128)(2,1)} %all-gather.14.cloned.1.call-done, bf16[4096,1792]{1,0:T(8,128)(2,1)} %copy-done.2, f32[1792]{0:T(1024)S(1)} %bitcast.126), kind=kOutput, calls=%fused_computation.49 | convolution fusion | flops 22570991616 | bytes 44702720 | tf_op jit(solution)/shard_map/dot_general | solution.py:124
  770.8 18.2 %add_convert_fusion.7 = bf16[768,1792]{1,0:T(8,128)(2,1)S(1)} fusion(bf16[768,4096]{1,0:T(8,128)(2,1)} %all-gather.14.cloned.1.call-done, bf16[4096,1792]{1,0:T(8,128)(2,1)} %collective-permute-done.2, f32[1792]{0:T(1024)S(1)} %copy-done.28), kind=kOutput, calls=%fused_computation.97 | convolution fusion | flops 11277041664 | bytes 23731200 | tf_op jit(solution)/shard_map/dot_general | solution.py:124
  789.0 18.1 %fusion.65 = bf16[768,1792]{1,0:T(8,128)(2,1)S(1)} fusion(bf16[768,1792]{1,0:T(8,128)(2,1)S(1)} %add_convert_fusion.7, bf16[768,4096]{1,0:T(8,128)(2,1)S(1)} %copy-done.33, bf16[4096,1792]{1,0:T(8,128)(2,1)} %collective-permute-done.4, f32[1792]{0:T(1024)S(1)} %copy-done.22), kind=kOutput, calls=%fused_computation.95 | convolution fusion | flops 11293556736 | bytes 26483712 | tf_op jit(solution)/shard_map/dot_general | solution.py:124
  807.1 16.8 %add_convert_fusion = bf16[768,4096]{1,0:T(8,128)(2,1)} fusion(bf16[768,4096]{1,0:T(8,128)(2,1)S(1)} %bitcast.133, bf16[768,1792]{1,0:T(8,128)(2,1)S(1)} %fusion.65, bf16[1792,4096]{1,0:T(8,128)(2,1)} %collective-permute-done.5), kind=kOutput, calls=%fused_computation.6 | convolution fusion | flops 11290017792 | bytes 30015488 | tf_op jit(solution)/shard_map/dot_general | solution.py:124
  827.6 60.9 %reduce-scatter.17.cloned.1.call-done = bf16[192,4096]{1,0:T(8,128)(2,1)} async-done(((bf16[768,4096]{1,0:T(8,128)(2,1)}), bf16[192,4096]{1,0:T(8,128)(2,1)}) %reduce-scatter.17.cloned.1.call-update) | async-done | bytes 1572880 | tf_op jit(solution)/shard_map/reduce_scatter | solution.py:179
  888.5 5.1 multiply_reduce_fusion.4
  895.4 3.6 fusion.81
  899.0 2.5 pad_maximum_fusion
  (163 shorter events, 16.3 us)
Async XLA Ops:
  6.5 7.1 copy-start.30
  6.5 7.1 copy-start.12
  6.5 7.2 copy-start.29
  6.5 74.0 %all-gather.16.cloned.1.call-start = ((), (), s32[]{:S(2)}) async-start(), calls=%async_computation.15 | async-start | bytes 14155776 | tf_op jit(solution)/shard_map/all_gather | solution.py:150
  11.3 137.4 %all-gather.18.cloned.1.call-start = ((), (), s32[]{:S(2)}) async-start(), calls=%async_computation.16 | async-start | bytes 14155776 | tf_op jit(solution)/shard_map/all_gather | solution.py:150
  12.0 204.9 %all-gather.20.cloned.1.call-start = ((), (), s32[]{:S(2)}) async-start(), calls=%async_computation.17 | async-start | bytes 14155776 | tf_op jit(solution)/shard_map/all_gather | solution.py:150
  12.7 271.3 %reduce-scatter.7.cloned.1.call-start = ((), (), s32[]{:S(2)}) async-start(), calls=%async_computation.6 | async-start | bytes 7864320 | tf_op jit(solution)/shard_map/reduce_scatter | solution.py:167
  12.8 123.2 %collective-permute-start.1 = (bf16[512,4096]{1,0:T(8,128)(2,1)}, bf16[512,4096]{1,0:T(8,128)(2,1)}, u32[]{:S(2)}, u32[]{:S(2)}) collective-permute-start(bf16[512,4096]{1,0:T(8,128)(2,1)} %param.20), channel_id=1, source_target_pairs={{0,1},{1,0},{2,3},{3,2},{4,5},{5,4},{6,7},{7,6}} | collective-permute-start | bytes 12582920 | tf_op jit(solution)/shard_map/ppermute | solution.py:145
  80.5 26.2 %copy-start = (f32[1536,128]{1,0:T(8,128)S(1)}, f32[1536,128]{1,0:T(8,128)}, u32[]{:S(2)}) copy-start(f32[1536,128]{1,0:T(8,128)} %get-tuple-element.38.sin_ref) | copy-start | bytes 2359300
  80.5 26.2 %copy-start.1 = (f32[1536,128]{1,0:T(8,128)S(1)}, f32[1536,128]{1,0:T(8,128)}, u32[]{:S(2)}) copy-start(f32[1536,128]{1,0:T(8,128)} %get-tuple-element.60.cos_ref) | copy-start | bytes 2359300
  106.7 25.6 %copy-start.34 = (bf16[512,4096]{1,0:T(8,128)(2,1)S(1)}, bf16[512,4096]{1,0:T(8,128)(2,1)}, u32[]{:S(2)}) copy-start(bf16[512,4096]{1,0:T(8,128)(2,1)} %param.20) | copy-start | bytes 12582916
  132.1 3.9 collective-permute-start
  143.5 207.6 %reduce-scatter.11.cloned.1.call-start = ((), (), s32[]{:S(2)}) async-start(), calls=%async_computation.9 | async-start | bytes 7864320 | tf_op jit(solution)/shard_map/reduce_scatter | solution.py:167
  174.9 27.7 %copy-start.35 = (bf16[512,4096]{1,0:T(8,128)(2,1)S(1)}, bf16[512,4096]{1,0:T(8,128)(2,1)}, u32[]{:S(2)}) copy-start(bf16[512,4096]{1,0:T(8,128)(2,1)} %param.20) | copy-start | bytes 12582916
  202.4 3.9 collective-permute-start.6
  214.0 204.2 %reduce-scatter.15.cloned.1.call-start = ((), (), s32[]{:S(2)}) async-start(), calls=%async_computation.12 | async-start | bytes 7864320 | tf_op jit(solution)/shard_map/reduce_scatter | solution.py:167
  243.0 24.2 %copy-start.36 = (bf16[512,4096]{1,0:T(8,128)(2,1)S(1)}, bf16[512,4096]{1,0:T(8,128)(2,1)}, u32[]{:S(2)}) copy-start(bf16[512,4096]{1,0:T(8,128)(2,1)} %param.20) | copy-start | bytes 12582916
  266.9 3.9 collective-permute-start.7
  278.8 218.5 %all-gather.10.cloned.1.call-start = ((), (), s32[]{:S(2)}) async-start(), calls=%async_computation.7 | async-start | bytes 7864320 | tf_op jit(solution)/shard_map/all_gather | solution.py:173
  351.1 72.1 %copy-start.8 = (bf16[192,4096]{1,0:T(8,128)(2,1)S(1)}, bf16[192,4096]{1,0:T(8,128)(2,1)}, u32[]{:S(2)}) copy-start(bf16[192,4096]{1,0:T(8,128)(2,1)} %reduce-scatter.11.cloned.1.call-done) | copy-start | bytes 4718596
  432.9 173.1 %all-gather.12.cloned.1.call-start = ((), (), s32[]{:S(2)}) async-start(), calls=%async_computation.10 | async-start | bytes 7864320 | tf_op jit(solution)/shard_map/all_gather | solution.py:173
  433.6 25.3 %copy-start.19 = (bf16[3584]{0:T(1024)(128)(2,1)S(1)}, bf16[3584]{0:T(1024)(128)(2,1)}, u32[]{:S(2)}) copy-start(bf16[3584]{0:T(1024)(128)(2,1)} %param.25) | copy-start | bytes 21508
  433.6 281.5 %all-gather.14.cloned.1.call-start = ((), (), s32[]{:S(2)}) async-start(), calls=%async_computation.13 | async-start | bytes 7864320 | tf_op jit(solution)/shard_map/all_gather | solution.py:173
  458.9 93.5 %collective-permute-start.2 = (bf16[4096,1792]{1,0:T(8,128)(2,1)}, bf16[4096,1792]{1,0:T(8,128)(2,1)}, u32[]{:S(2)}, u32[]{:S(2)}) collective-permute-start(bf16[4096,1792]{1,0:T(8,128)(2,1)} %get-tuple-element.15), channel_id=1, source_target_pairs={{0,1},{1,0},{2,3},{3,2},{4,5},{5,4},{6,7},{7,6}} | collective-permute-start | bytes 44040200 | tf_op jit(solution)/shard_map/ppermute | solution.py:145
  459.0 22.1 %collective-permute-start.3 = (bf16[2,1792]{1,0:T(2,128)(2,1)S(1)}, bf16[2,1792]{1,0:T(2,128)(2,1)S(1)}, u32[]{:S(2)}, u32[]{:S(2)}) collective-permute-start(bf16[2,1792]{1,0:T(2,128)(2,1)S(1)} %pad_maximum_fusion.3), channel_id=1, source_target_pairs={{0,1},{1,0},{2,3},{3,2},{4,5},{5,4},{6,7},{7,6}} | collective-permute-start | bytes 21512 | tf_op jit(solution)/shard_map/ppermute | solution.py:145
  459.6 111.2 %collective-permute-start.4 = (bf16[4096,1792]{1,0:T(8,128)(2,1)}, bf16[4096,1792]{1,0:T(8,128)(2,1)}, u32[]{:S(2)}, u32[]{:S(2)}) collective-permute-start(bf16[4096,1792]{1,0:T(8,128)(2,1)} %copy-done.2), channel_id=1, source_target_pairs={{0,1},{1,0},{2,3},{3,2},{4,5},{5,4},{6,7},{7,6}} | collective-permute-start | bytes 44040200 | tf_op jit(solution)/shard_map/ppermute | solution.py:145
  459.6 129.3 %collective-permute-start.5 = (bf16[1792,4096]{1,0:T(8,128)(2,1)}, bf16[1792,4096]{1,0:T(8,128)(2,1)}, u32[]{:S(2)}, u32[]{:S(2)}) collective-permute-start(bf16[1792,4096]{1,0:T(8,128)(2,1)} %param.26), channel_id=1, source_target_pairs={{0,1},{1,0},{2,3},{3,2},{4,5},{5,4},{6,7},{7,6}} | collective-permute-start | bytes 44040200 | tf_op jit(solution)/shard_map/ppermute | solution.py:145
  460.1 55.1 %copy-start.23 = (f32[14,128]{1,0:T(8,128)}, f32[14,128]{1,0:T(8,128)S(1)}, u32[]{:S(2)}) copy-start(f32[14,128]{1,0:T(8,128)S(1)} %get-tuple-element.34) | copy-start | bytes 21508
  481.8 342.9 %reduce-scatter.9.cloned.1.call-start = ((), (), s32[]{:S(2)}) async-start(), calls=%async_computation.8 | async-start | bytes 7864320 | tf_op jit(solution)/shard_map/reduce_scatter | solution.py:179
  515.2 37.3 %copy-start.26 = (f32[1792]{0:T(1024)S(1)}, f32[1792]{0:T(1024)}, u32[]{:S(2)}) copy-start(f32[1792]{0:T(1024)} %get-tuple-element.32) | copy-start | bytes 21508
  552.5 18.2 %copy-start.20 = (f32[1792]{0:T(1024)S(1)}, f32[1792]{0:T(1024)}, u32[]{:S(2)}) copy-start(f32[1792]{0:T(1024)} %get-tuple-element.31) | copy-start | bytes 21508
  552.5 18.2 %copy-start.32 = (bf16[768,4096]{1,0:T(8,128)(2,1)S(1)}, bf16[768,4096]{1,0:T(8,128)(2,1)}, u32[]{:S(2)}) copy-start(bf16[768,4096]{1,0:T(8,128)(2,1)} %all-gather.10.cloned.1.call-done) | copy-start | bytes 18874372
  552.5 36.4 %slice-start = ((s8[6291456]{0:T(1024)(128)(4,1)}), s8[4194304]{0:T(1024)(128)(4,1)S(1)}, s32[]{:S(2)}) async-start(s8[6291456]{0:T(1024)(128)(4,1)} %bitcast.130), calls=%async_computation.18 | async-start | bytes 8388608
  570.7 18.1 %slice-start.1 = ((s8[6291456]{0:T(1024)(128)(4,1)}), s8[2097152]{0:T(1024)(128)(4,1)S(1)}, s32[]{:S(2)}) async-start(s8[6291456]{0:T(1024)(128)(4,1)} %bitcast.130), calls=%async_computation.19 | async-start | bytes 4194304
  605.9 221.6 %reduce-scatter.13.cloned.1.call-start = ((), (), s32[]{:S(2)}) async-start(), calls=%async_computation.11 | async-start | bytes 7864320 | tf_op jit(solution)/shard_map/reduce_scatter | solution.py:179
  624.4 37.2 %copy-start.27 = (f32[1792]{0:T(1024)S(1)}, f32[1792]{0:T(1024)}, u32[]{:S(2)}) copy-start(f32[1792]{0:T(1024)} %get-tuple-element.32) | copy-start | bytes 21508
  661.7 18.2 %copy-start.21 = (f32[1792]{0:T(1024)S(1)}, f32[1792]{0:T(1024)}, u32[]{:S(2)}) copy-start(f32[1792]{0:T(1024)} %get-tuple-element.31) | copy-start | bytes 21508
  661.7 18.2 %copy-start.31 = (bf16[768,4096]{1,0:T(8,128)(2,1)S(1)}, bf16[768,4096]{1,0:T(8,128)(2,1)}, u32[]{:S(2)}) copy-start(bf16[768,4096]{1,0:T(8,128)(2,1)} %all-gather.12.cloned.1.call-done) | copy-start | bytes 18874372
  661.7 36.3 %slice-start.4 = ((s8[6291456]{0:T(1024)(128)(4,1)}), s8[4194304]{0:T(1024)(128)(4,1)S(1)}, s32[]{:S(2)}) async-start(s8[6291456]{0:T(1024)(128)(4,1)} %bitcast.134), calls=%async_computation.22 | async-start | bytes 8388608
  679.9 18.1 %slice-start.5 = ((s8[6291456]{0:T(1024)(128)(4,1)}), s8[2097152]{0:T(1024)(128)(4,1)S(1)}, s32[]{:S(2)}) async-start(s8[6291456]{0:T(1024)(128)(4,1)} %bitcast.134), calls=%async_computation.23 | async-start | bytes 4194304
  715.1 173.4 %reduce-scatter.17.cloned.1.call-start = ((), (), s32[]{:S(2)}) async-start(), calls=%async_computation.14 | async-start | bytes 7864320 | tf_op jit(solution)/shard_map/reduce_scatter | solution.py:179
  733.6 37.2 %copy-start.28 = (f32[1792]{0:T(1024)S(1)}, f32[1792]{0:T(1024)}, u32[]{:S(2)}) copy-start(f32[1792]{0:T(1024)} %get-tuple-element.32) | copy-start | bytes 21508
  770.8 18.2 %copy-start.22 = (f32[1792]{0:T(1024)S(1)}, f32[1792]{0:T(1024)}, u32[]{:S(2)}) copy-start(f32[1792]{0:T(1024)} %get-tuple-element.31) | copy-start | bytes 21508
  770.8 18.2 %copy-start.33 = (bf16[768,4096]{1,0:T(8,128)(2,1)S(1)}, bf16[768,4096]{1,0:T(8,128)(2,1)}, u32[]{:S(2)}) copy-start(bf16[768,4096]{1,0:T(8,128)(2,1)} %all-gather.14.cloned.1.call-done) | copy-start | bytes 18874372
  770.8 36.3 %slice-start.2 = ((s8[6291456]{0:T(1024)(128)(4,1)}), s8[4194304]{0:T(1024)(128)(4,1)S(1)}, s32[]{:S(2)}) async-start(s8[6291456]{0:T(1024)(128)(4,1)} %bitcast.132), calls=%async_computation.20 | async-start | bytes 8388608
  789.0 18.1 %slice-start.3 = ((s8[6291456]{0:T(1024)(128)(4,1)}), s8[2097152]{0:T(1024)(128)(4,1)S(1)}, s32[]{:S(2)}) async-start(s8[6291456]{0:T(1024)(128)(4,1)} %bitcast.132), calls=%async_computation.21 | async-start | bytes 4194304
  824.0 64.5 %copy-start.4 = (bf16[192,4096]{1,0:T(8,128)(2,1)S(1)}, bf16[192,4096]{1,0:T(8,128)(2,1)}, u32[]{:S(2)}) copy-start(bf16[192,4096]{1,0:T(8,128)(2,1)} %get-tuple-element.36) | copy-start | bytes 4718596
  888.5 5.2 copy-start.10
  (15 other events, 33.1 us)
Sparse Core Ops, SparseCore 0:
  11.4 69.1 all-gather.15
  82.4 66.2 all-gather.17
  150.5 66.3 all-gather.19
  219.7 64.2 reduce-scatter.6
  286.8 64.2 reduce-scatter.10
  353.9 64.2 reduce-scatter.14
  433.0 64.3 all-gather.9
  499.1 64.3 all-gather.11
  565.2 64.3 all-gather.13
  632.4 64.2 reduce-scatter.8
  715.2 64.2 reduce-scatter.12
  824.1 64.2 reduce-scatter.16

commit v2 on v1

--- a/solution.py
+++ b/solution.py
@@ -99,87 +99,221 @@
     )(info, qkv, cos_t, sin_t)
 
 
-def split_kernel(w_ref, value_ref, gate_ref):
-    value_ref[...] = w_ref[:, :GLU_BLOCK]
-    gate_ref[...] = w_ref[:, GLU_BLOCK:]
-
-
-def split_pairs(w_up):
-    depth, width = w_up.shape
-    out = jax.ShapeDtypeStruct((depth, width // 2), w_up.dtype)
-    spec = pl.BlockSpec((depth, GLU_BLOCK), lambda j: (0, j))
+def norm_kernel(x_ref, part_ref, bias_ref, gain_ref, shift_ref, *out_refs):
+    resid = DEEPNORM_ALPHA * x_ref[...].astype(F32) + part_ref[...].astype(F32) + bias_ref[...].astype(F32)
+    out_refs[-1][...] = layer_norm(resid, gain_ref[...], shift_ref[...]).astype(BF16)
+
+
+def norm_rows(x_rows, x_at, part, bias, gain, shift, out_rows=None, out_at=None, into=None):
+    rows, width = part.shape
+    step = 64
+    spec = pl.BlockSpec((step, width), lambda i: (i, 0))
+    vec = pl.BlockSpec((1, width), lambda i: (0, 0))
+    x_spec = spec if x_at is None else pl.BlockSpec((None, step, width), lambda i: (x_at, i, 0))
+    args = [x_rows, part, bias.reshape(1, -1), gain.reshape(1, -1), shift.reshape(1, -1)]
+    in_specs = [x_spec, spec, vec, vec, vec]
+    alias = {}
+    if out_rows is None:
+        out, out_spec = jax.ShapeDtypeStruct((rows, width), BF16), spec
+    else:
+        out = jax.ShapeDtypeStruct((out_rows, rows, width), BF16)
+        out_spec = pl.BlockSpec((None, step, width), lambda i: (out_at, i, 0))
+    if into is not None:
+        args.append(into)
+        in_specs.append(pl.BlockSpec(memory_space=pl.ANY))
+        alias = {5: 0}
     return pl.pallas_call(
-        split_kernel,
-        out_shape=(out, out),
-        grid=(width // (2 * GLU_BLOCK),),
-        in_specs=[pl.BlockSpec((depth, 2 * GLU_BLOCK), lambda j: (0, j))],
-        out_specs=[spec, spec],
+        norm_kernel,
+        out_shape=out,
+        grid=(rows // step,),
+        in_specs=in_specs,
+        out_specs=out_spec,
+        input_output_aliases=alias,
         compiler_params=pltpu.CompilerParams(vmem_limit_bytes=24 << 20),
-        cost_estimate=pl.CostEstimate(flops=18 * 10 ** 9, bytes_accessed=4 * depth * width, transcendentals=0),
-        name='split_pairs',
-    )(w_up)
+        cost_estimate=pl.CostEstimate(flops=3 * 10 ** 9, bytes_accessed=6 * rows * width, transcendentals=0),
+        name='norm_rows',
+    )(*args)
+
+
+UP_TILE = 512
+UP_ROWS = 384
+
+
+def up_kernel(tiles, own_rows, info, own_ref, x_ref, y_ref, far_a_ref, far_b_ref, w_own, w_other, b_ref, m_ref, h_buf, w_buf, h_sem, w_sem):
+    step = pl.program_id(0)
+    chip = info[2]
+    half = own_rows // 2
+
+    def weight_copy(at, start):
+        slot = lax.rem(at, 2)
+
+        def go(src, tile):
+            cols = pl.ds(pl.multiple_of(tile * UP_TILE, UP_TILE), UP_TILE)
+            copy = pltpu.make_async_copy(src.at[:, cols], w_buf.at[slot], w_sem.at[slot])
+            copy.start() if start else copy.wait()
+
+        if not start:
+            go(w_own, 0)
+            return
+
+        @pl.when(at < tiles)
+        def _():
+            go(w_own, at)
+
+        @pl.when(at >= tiles)
+        def _():
+            go(w_other, at - tiles)
+
+    def row_copies():
+        parts = ((own_ref, 0, 0, own_rows), (x_ref, 1, 0, own_rows), (y_ref, 2, 0, own_rows), (far_a_ref, 3, 0, half), (far_b_ref, 3, half, half))
+        for k, (src, flip, shift, size) in enumerate(parts):
+            at = pl.multiple_of(jnp.bitwise_xor(chip, flip) * own_rows + shift, half)
+            yield pltpu.make_async_copy(src, h_buf.at[pl.ds(at, size), :], h_sem.at[k])
+
+    @pl.when(step == 0)
+    def _():
+        weight_copy(step, True)
+        for copy in row_copies():
+            copy.start()
+
+    @pl.when(step + 1 < 2 * tiles)
+    def _():
+        weight_copy(step + 1, True)
+
+    weight_copy(step, False)
+
+    @pl.when(step == 0)
+    def _():
+        for copy in row_copies():
+            copy.wait()
+
+    slot = lax.rem(step, 2)
+    bias = b_ref[...].astype(F32)
+
+    @pl.loop(0, h_buf.shape[0] // UP_ROWS)
+    def _(block):
+        here = pl.ds(pl.multiple_of(block * UP_ROWS, UP_ROWS), UP_ROWS)
+        up = jnp.dot(h_buf[here, :], w_buf[slot], preferred_element_type=F32)
+        up = (up + bias).astype(BF16).astype(F32)
+        for pair in range(UP_TILE // (2 * GLU_BLOCK)):
+            base = 2 * GLU_BLOCK * pair
+            value, gate = up[:, base:base + GLU_BLOCK], up[:, base + GLU_BLOCK:base + 2 * GLU_BLOCK]
+            m_ref[here, GLU_BLOCK * pair:GLU_BLOCK * (pair + 1)] = (value * jax.nn.gelu(gate, approximate=True)).astype(BF16)
+
+
+def up_glu(info, row_parts, w_own, w_other, b_all):
+    own_rows, depth = row_parts[0].shape
+    rows = 4 * own_rows
+    width = w_own.shape[1]
+    tiles = width // UP_TILE
+    hbm = pl.BlockSpec(memory_space=pl.ANY)
+    return pl.pallas_call(
+        functools.partial(up_kernel, tiles, own_rows),
+        out_shape=jax.ShapeDtypeStruct((rows, width), BF16),
+        grid_spec=pltpu.PrefetchScalarGridSpec(
+            num_scalar_prefetch=1,
+            grid=(2 * tiles,),
+            in_specs=[hbm] * 7 + [pl.BlockSpec((1, UP_TILE), lambda j, info: (0, j))],
+            out_specs=pl.BlockSpec((rows, UP_TILE // 2), lambda j, info: (0, j)),
+            scratch_shapes=[
+                pltpu.VMEM((rows, depth), BF16),
+                pltpu.VMEM((2, depth, UP_TILE), BF16),
+                pltpu.SemaphoreType.DMA((5,)),
+                pltpu.SemaphoreType.DMA((2,)),
+            ],
+        ),
+        compiler_params=pltpu.CompilerParams(vmem_limit_bytes=32 << 20),
+        cost_estimate=pl.CostEstimate(flops=4 * rows * depth * width, bytes_accessed=4 * depth * width, transcendentals=rows * width),
+        name='up_glu',
+    )(info, *row_parts, w_own, w_other, b_all)
+
+
+def pair_kernel(a_ref, b_ref, wa_ref, wb_ref, out_ref):
+    first = jnp.dot(a_ref[...], wa_ref[...], preferred_element_type=F32).astype(BF16)
+    second = jnp.dot(b_ref[...], wb_ref[...], preferred_element_type=F32).astype(BF16)
+    out_ref[...] = (first.astype(F32) + second.astype(F32)).astype(BF16)
+
+
+def pair_product(lhs, w_own, w_other, tile, row_tile):
+    depth, width = w_own.shape
+    rows = lhs[0].shape[0]
+    second = 1 if lhs[0] is lhs[1] else 0
+    w_spec = pl.BlockSpec((depth, tile), lambda j, i: (0, j))
+    return pl.pallas_call(
+        pair_kernel,
+        out_shape=jax.ShapeDtypeStruct((rows, width), BF16),
+        grid=(width // tile, rows // row_tile),
+        in_specs=[
+            pl.BlockSpec((row_tile, depth), lambda j, i: (i, 0)),
+            pl.BlockSpec((row_tile, depth), lambda j, i: (i, second)),
+            w_spec,
+            w_spec,
+        ],
+        out_specs=pl.BlockSpec((row_tile, tile), lambda j, i: (i, j)),
+        compiler_params=pltpu.CompilerParams(vmem_limit_bytes=32 << 20),
+        cost_estimate=pl.CostEstimate(flops=4 * rows * depth * width, bytes_accessed=4 * depth * width, transcendentals=0),
+    )(*lhs, w_own, w_other)
 
 
 def mm(lhs, rhs):
     return jnp.dot(lhs, rhs, preferred_element_type=F32)
 
 
-def glu(rows, w_pair, b_pair):
-    value = (mm(rows, w_pair[0]) + b_pair[0].astype(F32)).astype(BF16)
-    gate = (mm(rows, w_pair[1]) + b_pair[1].astype(F32)).astype(BF16)
-    return (value.astype(F32) * jax.nn.gelu(gate.astype(F32), approximate=True)).astype(BF16)
-
-
-def two_part_sum(lhs_pair, rhs_pair):
-    first = mm(lhs_pair[0], rhs_pair[0]).astype(BF16)
-    second = mm(lhs_pair[1], rhs_pair[1]).astype(BF16)
-    return (first.astype(F32) + second.astype(F32)).astype(BF16)
-
-
 def solution(mesh):
     tp = mesh.shape['tp']
-    swap = [(i, i ^ 1) for i in range(tp)]
     same_core = [list(range(0, tp, 2)), list(range(1, tp, 2))]
 
-    def partner(val):
-        return lax.ppermute(val, 'tp', swap)
-
-    def local_layer(x_loc, positions, prefix_len, w_qkv, b_qkv, w_out, b_out, ln1_gain, ln1_bias, w_up, b_up, w_down, b_down, ln2_gain, ln2_bias):
-        batch_size, seq_loc, model_dim = x_loc.shape
-        core = lax.axis_index('tp') % 2
+    def from_peer(val, flip):
+        return lax.ppermute(val, 'tp', [(i, i ^ flip) for i in range(tp)])
+
+    def layer(x_loc, positions, prefix_len, w_qkv, b_qkv, w_out, b_out, ln1_gain, ln1_bias, w_up, b_up, w_down, b_down, ln2_gain, ln2_bias):
+        batch_size, seq_loc, _ = x_loc.shape
+        me = lax.axis_index('tp')
+        half = seq_loc // 2
         gathered = [lax.all_gather(x_loc[b], 'tp', axis=0, tiled=True) for b in range(batch_size)]
         cos_t, sin_t = rope_tables(positions)
-        w_pair = split_pairs(w_up)
-        b_rows = b_up.reshape(-1, 2, GLU_BLOCK)
-        b_pair = (b_rows[:, 0].reshape(-1), b_rows[:, 1].reshape(-1))
-        outs_w = (w_out, partner(w_out))
-        down_w = (w_down, partner(w_down))
-        up_w = (w_pair, (partner(w_pair[0]), partner(w_pair[1])))
-        b_other = partner(jnp.stack(b_pair))
-        up_b = (b_pair, (b_other[0], b_other[1]))
+        infos = [jnp.stack([prefix_len[b], me % 2, me // 2]).astype(jnp.int32) for b in range(batch_size)]
+        out_other, up_other, down_other = from_peer(w_out, 1), from_peer(w_up, 1), from_peer(w_down, 1)
+        b_all = jnp.concatenate([b_up, from_peer(b_up, 1)]).reshape(1, -1)
 
         attn_loc = []
         for b in range(batch_size):
+            if b == batch_size - 1:
+                gathered[b], up_other, down_other = lax.optimization_barrier((gathered[b], up_other, down_other))
             qkv = (mm(gathered[b], w_qkv) + b_qkv.astype(F32)).astype(BF16)
-            info = jnp.stack([prefix_len[b], core]).astype(jnp.int32)
-            mine, other = attention(info, qkv, cos_t[b], sin_t[b], seq_loc)
-            part = two_part_sum((mine, partner(other)), outs_w)
+            mine, other = attention(infos[b], qkv, cos_t[b], sin_t[b], seq_loc)
+            part = pair_product((mine, from_peer(other, 1)), w_out, out_other, 1024, 768)
             attn_loc.append(lax.psum_scatter(part, 'tp', scatter_dimension=0, axis_index_groups=same_core, tiled=True))
 
-        mids, fulls = [], []
+        def first_norm(b):
+            return norm_rows(x_loc, b, attn_loc[b], b_out, ln1_gain, ln1_bias)
+
+        def near_rows(mid):
+            return from_peer(mid, 2), from_peer(mid, 4)
+
+        def far_rows(near):
+            return from_peer(near[1][:half], 2), from_peer(near[0][half:], 4)
+
+        result = None
+        mid = first_norm(0)
+        near = near_rows(mid)
+        far = far_rows(near)
         for b in range(batch_size):
-            resid1 = DEEPNORM_ALPHA * x_loc[b].astype(F32) + attn_loc[b].astype(F32) + b_out.astype(F32)
-            mids.append(layer_norm(resid1, ln1_gain, ln1_bias).astype(BF16))
-            fulls.append(lax.all_gather(mids[b], 'tp', axis=0, axis_index_groups=same_core, tiled=True))
-
-        outs = []
-        for b in range(batch_size):
-            acts = tuple(glu(fulls[b], up_w[i], up_b[i]) for i in range(2))
-            part = two_part_sum(acts, down_w)
+            parts = (mid, *near, *far)
+            last = b == batch_size - 1
+            if not last:
+                parts, next_mid = lax.optimization_barrier((parts, first_norm(b + 1)))
+                next_near = near_rows(next_mid)
+            acts = up_glu(infos[b], parts, w_up, up_other, b_all)
+            if not last:
+                acts, next_near = lax.optimization_barrier((acts, next_near))
+                next_far = far_rows(next_near)
+            part = pair_product((acts, acts), w_down, down_other, 512, 768)
             ffn_loc = lax.psum_scatter(part, 'tp', scatter_dimension=0, axis_index_groups=same_core, tiled=True)
-            resid2 = DEEPNORM_ALPHA * mids[b].astype(F32) + ffn_loc.astype(F32) + b_down.astype(F32)
-            outs.append(layer_norm(resid2, ln2_gain, ln2_bias).astype(BF16))
-        return jnp.stack(outs)
+            result = norm_rows(mid, None, ffn_loc, b_down, ln2_gain, ln2_bias, batch_size, b, result)
+            if not last:
+                mid, near, far = next_mid, next_near, next_far
+        return result
 
     in_specs = (P('dp', 'tp', None), P('dp', None), P('dp'), P(None, 'tp'), P('tp'), P('tp', None), P(), P(), P(), P(None, 'tp'), P('tp'), P('tp', None), P(), P(), P())
-    return jax.shard_map(local_layer, mesh=mesh, in_specs=in_specs, out_specs=P('dp', 'tp', None), check_vma=False)
+    return jax.shard_map(layer, mesh=mesh, in_specs=in_specs, out_specs=P('dp', 'tp', None), check_vma=False)

time: 917 us -> 857 us (0.935)
  matrix products: 437 us -> 78.9 us
  Pallas kernels: 96.9 us -> 371 us
  local copies, waits for them, and re-layouts: 13.9 us -> 61.6 us
  other arithmetic: 45.9 us -> 12.9 us
  starting transfers between devices: 3.19 us -> 14.1 us
    dot_general x24 -> x3, matrix products: 437 us -> 78.9 us  [mm(): return jnp.dot(lhs, rhs, preferred_element_type=F32)]
    pallas_call x1 -> x15, Pallas kernels: 20.1 us -> 294 us  [the longest x3 172 us: up_glu(): pl.pallas_call(functools.partial(up_kernel, tiles, own_rows), out_shape=j...]
    ppermute x8 -> x19, waiting for transfers between devices: 21 us -> 148 us  [from_peer(): return lax.ppermute(val, 'tp', [(i, i ^ flip) for i in range(tp)])]
    reduce_scatter x6, waiting for transfers between devices: 197 us -> 85.6 us  [layer(): lax.psum_scatter(part, 'tp', scatter_dimension=0, axis_index_groups=same_...]
    unnamed x86 -> x110, local copies, waits for them, and re-layouts: 8.49 us -> 48.9 us
    reduce_sum x6 -> x0, other arithmetic: 20.1 us -> none  [the longest x4 15.4 us: layer_norm(): var_val = jnp.mean(centered * centered, axis=-1, keepdims=True)]
    all_gather x6 -> x3, waiting for transfers between devices: 76.7 us -> 60.3 us  [layer(): lax.all_gather(x_loc[b], 'tp', axis=0, tiled=True)]
    ppermute x8 -> x19, starting transfers between devices: 2.74 us -> 13.8 us  [from_peer(): return lax.ppermute(val, 'tp', [(i, i ^ flip) for i in range(tp)])]
  transfers between devices with their start and end apart: 20 -> 28, of which waited for: 9 -> 16; matrix products, arithmetic and copies ran while one was open for 50% -> 12% of each run, Pallas kernels for 11% -> 43%
where the time goes in v2:
time: 857 us; the launch traced here: 848 us
  Pallas kernels  371 us (43%)
  waiting for transfers between devices  295 us (34%)
  matrix products  78.9 us (9%)
  local copies, waits for them, and re-layouts  61.6 us (7%)
  between operations  14.2 us (2%)
  starting transfers between devices  14.1 us (2%)
  other arithmetic  12.9 us (2%)
    pallas_call x3, Pallas kernels, up_glu(): pl.pallas_call(functools.partial(up_kernel, tiles, own_rows), out_shape=j...  172 us
    ppermute x19, waiting for transfers between devices, from_peer(): return lax.ppermute(val, 'tp', [(i, i ^ flip) for i in range(tp)])  148 us
    pallas_call x6, Pallas kernels, pair_product(): pl.pallas_call(pair_kernel, out_shape=jax.ShapeDtypeStruct((rows, width),...  108 us
    reduce_scatter x6, waiting for transfers between devices, layer(): lax.psum_scatter(part, 'tp', scatter_dimension=0, axis_index_groups=same_...  85.6 us
    dot_general x3, matrix products, mm(): return jnp.dot(lhs, rhs, preferred_element_type=F32)  78.9 us
    pallas_call x3, Pallas kernels, attention(): pl.pallas_call(functools.partial(attn_kernel, rows, seq_len, key_block),...  76.6 us
    all_gather x3, waiting for transfers between devices, layer(): lax.all_gather(x_loc[b], 'tp', axis=0, tiled=True)  60.3 us
    unnamed x110, local copies, waits for them, and re-layouts  48.9 us
  transfers between devices with their start and end apart: 28, of which 16 were waited for; matrix products, arithmetic and copies ran while one was open for 12% of the time, Pallas kernels for 43%

profile of v2, /device:TPU:0, one launch (start us, length us, event | category | flops | bytes accessed | tf_op | source)
XLA Modules:
  0.0 847.6 jit_solution(13026984497501684399)
XLA Ops:
  6.5 4.7 fusion.28
  15.0 8.4 multiply_sine_fusion
  23.4 2.4 fusion.25
  25.8 54.8 %all-gather.7.cloned.1.call-done = bf16[1,1536,4096]{2,1,0:T(8,128)(2,1)} async-done(((bf16[1,192,4096]{2,1,0:T(8,128)(2,1)}), bf16[1,1536,4096]{2,1,0:T(8,128)(2,1)}) %all-gather.7.cloned.1.call-update) | async-done | bytes 12582928 | tf_op jit(solution)/shard_map/all_gather | solution.py:273
  80.7 26.4 %fusion.14.qkv_ref = bf16[1536,1536]{1,0:T(8,128)(2,1)S(1)} fusion(bf16[4096,1536]{1,0:T(8,128)(2,1)} %param.18, bf16[1,1536,4096]{2,1,0:T(8,128)(2,1)} %all-gather.7.cloned.1.call-done, f32[1536]{0:T(1024)S(1)} %convert_element_type.17), kind=kOutput, calls=%fused_computation.9 | convolution fusion | flops 19332071424 | bytes 29890560 | tf_op jit(solution)/shard_map/dot_general | solution.py:259
  107.1 25.2 %attention.3 = (bf16[768,512]{1,0:T(8,128)(2,1)S(1)}, bf16[768,512]{1,0:T(8,128)(2,1)S(1)}) custom-call(s32[3]{0:T(128)S(1)} %add_add_fusion.info, bf16[1536,1536]{1,0:T(8,128)(2,1)S(1)} %fusion.14.qkv_ref, f32[1536,128]{1,0:T(8,128)S(1)} %copy-done.12, f32[1536,128]{1,0:T(8,128)S(1)} %copy-done.11), custom_call_target="tpu_custom_call" | custom-call | flops 24000000000 | bytes 12582912 | tf_op jit(solution)/shard_map/attention/pallas_call | solution.py:82
  132.5 2.1 collective-permute-done.b_ref
  134.6 9.2 %shard_map.145 = bf16[768,4096]{1,0:T(8,128)(2,1)S(1)} custom-call(bf16[768,512]{1,0:T(8,128)(2,1)S(1)} %get-tuple-element.32.a_ref, bf16[768,512]{1,0:T(8,128)(2,1)S(1)} %collective-permute-done.b_ref, bf16[512,4096]{1,0:T(8,128)(2,1)S(1)} %copy-done.31, bf16[512,4096]{1,0:T(8,128)(2,1)} %collective-permute-done.1.wb_ref), custom_call_target="tpu_custom_call" | custom-call | flops 6442450944 | bytes 8388608 | tf_op jit(solution)/shard_map/pallas_call | solution.py:242
  143.9 2.7 copy-done.3
  147.5 2.4 all-gather.9.cloned.1.call-done
  149.9 26.3 %fusion.11.qkv_ref = bf16[1536,1536]{1,0:T(8,128)(2,1)S(1)} fusion(bf16[4096,1536]{1,0:T(8,128)(2,1)} %param.18, bf16[1,1536,4096]{2,1,0:T(8,128)(2,1)} %all-gather.9.cloned.1.call-done, f32[1536]{0:T(1024)S(1)} %convert_element_type.17), kind=kOutput, calls=%fused_computation.8 | convolution fusion | flops 19332071424 | bytes 29890560 | tf_op jit(solution)/shard_map/dot_general | solution.py:259
  176.2 23.9 %attention.4 = (bf16[768,512]{1,0:T(8,128)(2,1)S(1)}, bf16[768,512]{1,0:T(8,128)(2,1)S(1)}) custom-call(s32[3]{0:T(128)S(1)} %add_add_fusion.1.info, bf16[1536,1536]{1,0:T(8,128)(2,1)S(1)} %fusion.11.qkv_ref, f32[1536,128]{1,0:T(8,128)S(1)} %get-tuple-element.75.cos_ref, f32[1536,128]{1,0:T(8,128)S(1)} %get-tuple-element.60.sin_ref), custom_call_target="tpu_custom_call" | custom-call | flops 24000000000 | bytes 12582912 | tf_op jit(solution)/shard_map/attention/pallas_call | solution.py:82
  200.4 2.1 collective-permute-done.6.b_ref
  202.5 9.1 %shard_map.146 = bf16[768,4096]{1,0:T(8,128)(2,1)S(1)} custom-call(bf16[768,512]{1,0:T(8,128)(2,1)S(1)} %get-tuple-element.34.a_ref, bf16[768,512]{1,0:T(8,128)(2,1)S(1)} %collective-permute-done.6.b_ref, bf16[512,4096]{1,0:T(8,128)(2,1)S(1)} %copy-done.32, bf16[512,4096]{1,0:T(8,128)(2,1)} %collective-permute-done.1.wb_ref), custom_call_target="tpu_custom_call" | custom-call | flops 6442450944 | bytes 8388608 | tf_op jit(solution)/shard_map/pallas_call | solution.py:242
  211.6 2.7 copy-done.2
  215.1 3.1 all-gather.11.cloned.1.call-done
  218.2 26.2 %fusion.10.qkv_ref = bf16[1536,1536]{1,0:T(8,128)(2,1)S(1)} fusion(bf16[1536,4096]{1,0:T(8,128)(2,1)} %bitcast.33, bf16[4096,1536]{1,0:T(8,128)(2,1)} %param.18, f32[1536]{0:T(1024)S(1)} %convert_element_type.17), kind=kOutput, calls=%fused_computation.7 | convolution fusion | flops 19332071424 | bytes 29890560 | tf_op jit(solution)/shard_map/dot_general | solution.py:259
  244.4 27.4 %attention.5 = (bf16[768,512]{1,0:T(8,128)(2,1)S(1)}, bf16[768,512]{1,0:T(8,128)(2,1)S(1)}) custom-call(s32[3]{0:T(128)S(1)} %add_add_fusion.2.info, bf16[1536,1536]{1,0:T(8,128)(2,1)S(1)} %fusion.10.qkv_ref, f32[1536,128]{1,0:T(8,128)S(1)} %get-tuple-element.76.cos_ref, f32[1536,128]{1,0:T(8,128)S(1)} %get-tuple-element.59.sin_ref), custom_call_target="tpu_custom_call" | custom-call | flops 24000000000 | bytes 12582912 | tf_op jit(solution)/shard_map/attention/pallas_call | solution.py:82
  272.1 2.0 collective-permute-done.14.b_ref
  274.2 9.1 %shard_map.147 = bf16[768,4096]{1,0:T(8,128)(2,1)S(1)} custom-call(bf16[768,512]{1,0:T(8,128)(2,1)S(1)} %get-tuple-element.46.a_ref, bf16[768,512]{1,0:T(8,128)(2,1)S(1)} %collective-permute-done.14.b_ref, bf16[512,4096]{1,0:T(8,128)(2,1)S(1)} %copy-done.33, bf16[512,4096]{1,0:T(8,128)(2,1)} %collective-permute-done.1.wb_ref), custom_call_target="tpu_custom_call" | custom-call | flops 6442450944 | bytes 8388608 | tf_op jit(solution)/shard_map/pallas_call | solution.py:242
  283.3 2.7 copy-done
  286.8 2.3 copy-done.6
  290.5 2.1 norm_rows.6.own_ref.x_ref
  294.6 66.8 %collective-permute-done.3.y_ref = bf16[192,4096]{1,0:T(8,128)(2,1)S(1)} collective-permute-done((bf16[192,4096]{1,0:T(8,128)(2,1)S(1)}, bf16[192,4096]{1,0:T(8,128)(2,1)S(1)}, u32[]{:S(2)}, u32[]{:S(2)}) %collective-permute-start.3) | collective-permute-done | bytes 1572896 | tf_op jit(solution)/shard_map/ppermute | solution.py:267
  368.8 32.7 %reduce-scatter.9.cloned.1.call-done.part_ref = bf16[192,4096]{1,0:T(8,128)(2,1)} async-done(((bf16[768,4096]{1,0:T(8,128)(2,1)}), bf16[192,4096]{1,0:T(8,128)(2,1)}) %reduce-scatter.9.cloned.1.call-update) | async-done | bytes 1572880 | tf_op jit(solution)/shard_map/reduce_scatter | solution.py:286
  401.5 2.3 copy-done.7
  405.3 1.9 norm_rows.7.own_ref.x_ref
  413.3 57.0 %up_glu.3.a_ref.b_ref = bf16[768,3584]{1,0:T(8,128)(2,1)S(1)} custom-call(s32[3]{0:T(128)S(1)} %copy-done.28, bf16[192,4096]{1,0:T(8,128)(2,1)S(1)} %copy-done.35, bf16[192,4096]{1,0:T(8,128)(2,1)S(1)} %copy-done.20, bf16[192,4096]{1,0:T(8,128)(2,1)S(1)} %copy-done.18, bf16[96,4096]{1,0:T(8,128)(2,1)S(1)} %copy-done.42, bf16[96,4096]{1,0:T(8,128)(2,1)S(1)} %copy-done.44, ...), custom_call_target="tpu_custom_call" | custom-call | flops 45097156608 | bytes 58720256 | tf_op jit(solution)/shard_map/up_glu/pallas_call | solution.py:210
  470.3 7.2 collective-permute-done.11.y_ref
  478.7 26.7 %shard_map.150 = bf16[768,4096]{1,0:T(8,128)(2,1)S(1)} custom-call(bf16[768,3584]{1,0:T(8,128)(2,1)S(1)} %up_glu.3.a_ref.b_ref, bf16[768,3584]{1,0:T(8,128)(2,1)S(1)} %up_glu.3.a_ref.b_ref, bf16[1792,4096]{1,0:T(8,128)(2,1)} %wa_ref.11, bf16[1792,4096]{1,0:T(8,128)(2,1)} %collective-permute-done.8.wb_ref), custom_call_target="tpu_custom_call" | custom-call | flops 22548578304 | bytes 29360128 | tf_op jit(solution)/shard_map/pallas_call | solution.py:242
  505.4 2.6 copy-done.1
  508.1 2.1 slice.66
  513.1 2.3 copy-done.8
  516.9 1.9 norm_rows.8.own_ref.x_ref
  518.7 29.1 %collective-permute-done.12.far_a_ref = bf16[96,4096]{1,0:T(8,128)(2,1)} collective-permute-done((bf16[96,4096]{1,0:T(8,128)(2,1)}, bf16[96,4096]{1,0:T(8,128)(2,1)}, u32[]{:S(2)}, u32[]{:S(2)}) %collective-permute-start.12) | collective-permute-done | bytes 786464 | tf_op jit(solution)/shard_map/ppermute | solution.py:267
  552.9 57.7 %up_glu.4.a_ref.b_ref = bf16[768,3584]{1,0:T(8,128)(2,1)S(1)} custom-call(s32[3]{0:T(128)S(1)} %copy-done.30, bf16[192,4096]{1,0:T(8,128)(2,1)S(1)} %norm_rows.7.own_ref.x_ref, bf16[192,4096]{1,0:T(8,128)(2,1)S(1)} %copy-done.16, bf16[192,4096]{1,0:T(8,128)(2,1)S(1)} %copy-done.14, bf16[96,4096]{1,0:T(8,128)(2,1)} %collective-permute-done.12.far_a_ref, ...), custom_call_target="tpu_custom_call" | custom-call | flops 45097156608 | bytes 58720256 | tf_op jit(solution)/shard_map/up_glu/pallas_call | solution.py:210
  614.7 26.7 %shard_map.149 = bf16[768,4096]{1,0:T(8,128)(2,1)S(1)} custom-call(bf16[768,3584]{1,0:T(8,128)(2,1)S(1)} %up_glu.4.a_ref.b_ref, bf16[768,3584]{1,0:T(8,128)(2,1)S(1)} %up_glu.4.a_ref.b_ref, bf16[1792,4096]{1,0:T(8,128)(2,1)} %wa_ref.11, bf16[1792,4096]{1,0:T(8,128)(2,1)} %collective-permute-done.8.wb_ref), custom_call_target="tpu_custom_call" | custom-call | flops 22548578304 | bytes 29360128 | tf_op jit(solution)/shard_map/pallas_call | solution.py:242
  641.5 2.7 copy-done.4
  648.7 32.0 %collective-permute-done.17.far_a_ref = bf16[96,4096]{1,0:T(8,128)(2,1)S(1)} collective-permute-done((bf16[96,4096]{1,0:T(8,128)(2,1)S(1)}, bf16[96,4096]{1,0:T(8,128)(2,1)S(1)}, u32[]{:S(2)}, u32[]{:S(2)}) %collective-permute-start.17) | collective-permute-done | bytes 786464 | tf_op jit(solution)/shard_map/ppermute | solution.py:267
  680.7 1.9 collective-permute-done.18.far_b_ref
  685.7 57.4 %up_glu.5.a_ref.b_ref = bf16[768,3584]{1,0:T(8,128)(2,1)S(1)} custom-call(s32[3]{0:T(128)S(1)} %copy-done.26, bf16[192,4096]{1,0:T(8,128)(2,1)S(1)} %norm_rows.8.own_ref.x_ref, bf16[192,4096]{1,0:T(8,128)(2,1)S(1)} %copy-done.24, bf16[192,4096]{1,0:T(8,128)(2,1)S(1)} %copy-done.22, bf16[96,4096]{1,0:T(8,128)(2,1)S(1)} %collective-permute-done.17.far_a_ref, ...), custom_call_target="tpu_custom_call" | custom-call | flops 45097156608 | bytes 58720256 | tf_op jit(solution)/shard_map/up_glu/pallas_call | solution.py:210
  743.2 26.7 %shard_map.148 = bf16[768,4096]{1,0:T(8,128)(2,1)S(1)} custom-call(bf16[768,3584]{1,0:T(8,128)(2,1)S(1)} %up_glu.5.a_ref.b_ref, bf16[768,3584]{1,0:T(8,128)(2,1)S(1)} %up_glu.5.a_ref.b_ref, bf16[1792,4096]{1,0:T(8,128)(2,1)} %wa_ref.11, bf16[1792,4096]{1,0:T(8,128)(2,1)} %collective-permute-done.8.wb_ref), custom_call_target="tpu_custom_call" | custom-call | flops 22548578304 | bytes 29360128 | tf_op jit(solution)/shard_map/pallas_call | solution.py:242
  769.9 2.6 copy-done.5
  774.7 1.9 copy-done.38
  776.6 2.8 norm_rows.9.out_refs_0_
  780.8 2.8 norm_rows.10.out_refs_0_
  783.6 52.8 %reduce-scatter.13.cloned.1.call-done.part_ref = bf16[192,4096]{1,0:T(8,128)(2,1)} async-done(((bf16[768,4096]{1,0:T(8,128)(2,1)}), bf16[192,4096]{1,0:T(8,128)(2,1)}) %reduce-scatter.13.cloned.1.call-update) | async-done | bytes 1572880 | tf_op jit(solution)/shard_map/reduce_scatter | solution.py:312
  837.8 2.8 norm_rows.11
  (172 shorter events, 52.5 us)
Async XLA Ops:
  6.5 74.1 %all-gather.7.cloned.1.call-start = ((), (), s32[]{:S(2)}) async-start(), calls=%async_computation.12 | async-start | bytes 14155776 | tf_op jit(solution)/shard_map/all_gather | solution.py:273
  11.3 138.6 %all-gather.9.cloned.1.call-start = ((), (), s32[]{:S(2)}) async-start(), calls=%async_computation.13 | async-start | bytes 14155776 | tf_op jit(solution)/shard_map/all_gather | solution.py:273
  12.0 206.1 %all-gather.11.cloned.1.call-start = ((), (), s32[]{:S(2)}) async-start(), calls=%async_computation.14 | async-start | bytes 14155776 | tf_op jit(solution)/shard_map/all_gather | solution.py:273
  12.8 274.0 %reduce-scatter.7.cloned.1.call-start = ((), (), s32[]{:S(2)}) async-start(), calls=%async_computation.6 | async-start | bytes 7864320 | tf_op jit(solution)/shard_map/reduce_scatter | solution.py:286
  12.8 205.4 %collective-permute-start.7 = (bf16[4096,3584]{1,0:T(8,128)(2,1)}, bf16[4096,3584]{1,0:T(8,128)(2,1)}, u32[]{:S(2)}, u32[]{:S(2)}) collective-permute-start(bf16[4096,3584]{1,0:T(8,128)(2,1)} %w_own.5), channel_id=1, source_target_pairs={{0,1},{1,0},{2,3},{3,2},{4,5},{5,4},{6,7},{7,6}} | collective-permute-start | bytes 88080392 | tf_op jit(solution)/shard_map/ppermute | solution.py:267
  13.7 118.9 %collective-permute-start.1 = (bf16[512,4096]{1,0:T(8,128)(2,1)}, bf16[512,4096]{1,0:T(8,128)(2,1)}, u32[]{:S(2)}, u32[]{:S(2)}) collective-permute-start(bf16[512,4096]{1,0:T(8,128)(2,1)} %wa_ref.8), channel_id=1, source_target_pairs={{0,1},{1,0},{2,3},{3,2},{4,5},{5,4},{6,7},{7,6}} | collective-permute-start | bytes 12582920 | tf_op jit(solution)/shard_map/ppermute | solution.py:267
  15.0 92.1 %copy-start.27 = (s32[3]{0:T(128)}, s32[3]{0:T(128)S(1)}, u32[]{:S(2)}) copy-start(s32[3]{0:T(128)S(1)} %add_add_fusion.info) | copy-start | bytes 40
  80.6 26.4 %copy-start.11 = (f32[1536,128]{1,0:T(8,128)S(1)}, f32[1536,128]{1,0:T(8,128)}, u32[]{:S(2)}) copy-start(f32[1536,128]{1,0:T(8,128)} %get-tuple-element.61.sin_ref) | copy-start | bytes 2359300
  80.6 26.4 %copy-start.12 = (f32[1536,128]{1,0:T(8,128)S(1)}, f32[1536,128]{1,0:T(8,128)}, u32[]{:S(2)}) copy-start(f32[1536,128]{1,0:T(8,128)} %get-tuple-element.74.cos_ref) | copy-start | bytes 2359300
  107.1 27.5 %copy-start.31 = (bf16[512,4096]{1,0:T(8,128)(2,1)S(1)}, bf16[512,4096]{1,0:T(8,128)(2,1)}, u32[]{:S(2)}) copy-start(bf16[512,4096]{1,0:T(8,128)(2,1)} %wa_ref.8) | copy-start | bytes 12582916
  132.3 2.3 collective-permute-start
  143.9 2.7 copy-start.3
  146.6 254.9 %reduce-scatter.9.cloned.1.call-start = ((), (), s32[]{:S(2)}) async-start(), calls=%async_computation.7 | async-start | bytes 7864320 | tf_op jit(solution)/shard_map/reduce_scatter | solution.py:286
  146.6 68.5 %collective-permute-start.8 = (bf16[1792,4096]{1,0:T(8,128)(2,1)}, bf16[1792,4096]{1,0:T(8,128)(2,1)}, u32[]{:S(2)}, u32[]{:S(2)}) collective-permute-start(bf16[1792,4096]{1,0:T(8,128)(2,1)} %wa_ref.11), channel_id=1, source_target_pairs={{0,1},{1,0},{2,3},{3,2},{4,5},{5,4},{6,7},{7,6}} | collective-permute-start | bytes 44040200 | tf_op jit(solution)/shard_map/ppermute | solution.py:267
  147.5 28.7 %copy-start.29 = (s32[3]{0:T(128)}, s32[3]{0:T(128)S(1)}, u32[]{:S(2)}) copy-start(s32[3]{0:T(128)S(1)} %add_add_fusion.1.info) | copy-start | bytes 40
  176.2 26.3 %copy-start.32 = (bf16[512,4096]{1,0:T(8,128)(2,1)S(1)}, bf16[512,4096]{1,0:T(8,128)(2,1)}, u32[]{:S(2)}) copy-start(bf16[512,4096]{1,0:T(8,128)(2,1)} %wa_ref.8) | copy-start | bytes 12582916
  200.2 2.3 collective-permute-start.6
  211.6 2.7 copy-start.2
  214.4 298.8 %reduce-scatter.11.cloned.1.call-start = ((), (), s32[]{:S(2)}) async-start(), calls=%async_computation.8 | async-start | bytes 7864320 | tf_op jit(solution)/shard_map/reduce_scatter | solution.py:286
  215.1 29.3 %copy-start.25 = (s32[3]{0:T(128)}, s32[3]{0:T(128)S(1)}, u32[]{:S(2)}) copy-start(s32[3]{0:T(128)S(1)} %add_add_fusion.2.info) | copy-start | bytes 40
  244.4 29.8 %copy-start.33 = (bf16[512,4096]{1,0:T(8,128)(2,1)S(1)}, bf16[512,4096]{1,0:T(8,128)(2,1)}, u32[]{:S(2)}) copy-start(bf16[512,4096]{1,0:T(8,128)(2,1)} %wa_ref.8) | copy-start | bytes 12582916
  271.9 2.3 collective-permute-start.14
  286.0 487.3 %reduce-scatter.17.cloned.1.call-start = ((), (), s32[]{:S(2)}) async-start(), calls=%async_computation.11 | async-start | bytes 7864320 | tf_op jit(solution)/shard_map/reduce_scatter | solution.py:312
  290.5 77.0 %copy-start.52 = (bf16[3584]{0:T(1024)(128)(2,1)S(1)}, bf16[3584]{0:T(1024)(128)(2,1)}, u32[]{:S(2)}) copy-start(bf16[3584]{0:T(1024)(128)(2,1)} %param.25) | copy-start | bytes 21508
  292.6 76.1 %copy-start.34 = (bf16[192,4096]{1,0:T(8,128)(2,1)}, bf16[192,4096]{1,0:T(8,128)(2,1)S(1)}, u32[]{:S(2)}) copy-start(bf16[192,4096]{1,0:T(8,128)(2,1)S(1)} %norm_rows.6.own_ref.x_ref) | copy-start | bytes 4718596
  292.6 68.8 %collective-permute-start.3 = (bf16[192,4096]{1,0:T(8,128)(2,1)S(1)}, bf16[192,4096]{1,0:T(8,128)(2,1)S(1)}, u32[]{:S(2)}, u32[]{:S(2)}) collective-permute-start(bf16[192,4096]{1,0:T(8,128)(2,1)S(1)} %norm_rows.6.own_ref.x_ref), channel_id=1, source_target_pairs={{0,4},{1,5},{2,6},{3,7},{4,0},{5,1},{6,2},{7,3}} | collective-permute-start | bytes 4718600 | tf_op jit(solution)/shard_map/ppermute | solution.py:267
  293.5 71.4 %collective-permute-start.2 = (bf16[192,4096]{1,0:T(8,128)(2,1)S(1)}, bf16[192,4096]{1,0:T(8,128)(2,1)S(1)}, u32[]{:S(2)}, u32[]{:S(2)}) collective-permute-start(bf16[192,4096]{1,0:T(8,128)(2,1)S(1)} %norm_rows.6.own_ref.x_ref), channel_id=1, source_target_pairs={{0,2},{1,3},{2,0},{3,1},{4,6},{5,7},{6,4},{7,5}} | collective-permute-start | bytes 4718600 | tf_op jit(solution)/shard_map/ppermute | solution.py:267
  363.4 43.7 %collective-permute-start.4 = (bf16[96,4096]{1,0:T(8,128)(2,1)}, bf16[96,4096]{1,0:T(8,128)(2,1)S(1)}, u32[]{:S(2)}, u32[]{:S(2)}) collective-permute-start(bf16[96,4096]{1,0:T(8,128)(2,1)} %slice.76), channel_id=1, source_target_pairs={{0,2},{1,3},{2,0},{3,1},{4,6},{5,7},{6,4},{7,5}} | collective-permute-start | bytes 2359304 | tf_op jit(solution)/shard_map/ppermute | solution.py:267
  367.0 41.1 %collective-permute-start.5 = (bf16[96,4096]{1,0:T(8,128)(2,1)}, bf16[96,4096]{1,0:T(8,128)(2,1)S(1)}, u32[]{:S(2)}, u32[]{:S(2)}) collective-permute-start(bf16[96,4096]{1,0:T(8,128)(2,1)} %slice.77), channel_id=1, source_target_pairs={{0,4},{1,5},{2,6},{3,7},{4,0},{5,1},{6,2},{7,3}} | collective-permute-start | bytes 2359304 | tf_op jit(solution)/shard_map/ppermute | solution.py:267
  367.6 1.2 collective-permute-start.9
  405.3 5.7 copy-start.18
  405.3 5.7 copy-start.20
  405.3 5.7 copy-start.28
  405.3 5.7 copy-start.35
  408.9 68.5 %collective-permute-start.11 = (bf16[192,4096]{1,0:T(8,128)(2,1)S(1)}, bf16[192,4096]{1,0:T(8,128)(2,1)S(1)}, u32[]{:S(2)}, u32[]{:S(2)}) collective-permute-start(bf16[192,4096]{1,0:T(8,128)(2,1)S(1)} %norm_rows.7.own_ref.x_ref), channel_id=1, source_target_pairs={{0,4},{1,5},{2,6},{3,7},{4,0},{5,1},{6,2},{7,3}} | collective-permute-start | bytes 4718600 | tf_op jit(solution)/shard_map/ppermute | solution.py:267
  409.5 68.0 %collective-permute-start.10 = (bf16[192,4096]{1,0:T(8,128)(2,1)S(1)}, bf16[192,4096]{1,0:T(8,128)(2,1)S(1)}, u32[]{:S(2)}, u32[]{:S(2)}) collective-permute-start(bf16[192,4096]{1,0:T(8,128)(2,1)S(1)} %norm_rows.7.own_ref.x_ref), channel_id=1, source_target_pairs={{0,2},{1,3},{2,0},{3,1},{4,6},{5,7},{6,4},{7,5}} | collective-permute-start | bytes 4718600 | tf_op jit(solution)/shard_map/ppermute | solution.py:267
  477.5 32.7 %copy-start.13 = (bf16[192,4096]{1,0:T(8,128)(2,1)}, bf16[192,4096]{1,0:T(8,128)(2,1)S(1)}, u32[]{:S(2)}) copy-start(bf16[192,4096]{1,0:T(8,128)(2,1)S(1)} %collective-permute-done.11.y_ref) | copy-start | bytes 4718596
  508.0 271.4 %reduce-scatter.15.cloned.1.call-start = ((), (), s32[]{:S(2)}) async-start(), calls=%async_computation.10 | async-start | bytes 7864320 | tf_op jit(solution)/shard_map/reduce_scatter | solution.py:312
  510.1 41.4 %copy-start.30 = (s32[3]{0:T(128)S(1)}, s32[3]{0:T(128)}, u32[]{:S(2)}) copy-start(s32[3]{0:T(128)} %copy-done.29) | copy-start | bytes 40
  511.1 36.7 %collective-permute-start.12 = (bf16[96,4096]{1,0:T(8,128)(2,1)}, bf16[96,4096]{1,0:T(8,128)(2,1)}, u32[]{:S(2)}, u32[]{:S(2)}) collective-permute-start(bf16[96,4096]{1,0:T(8,128)(2,1)} %slice.65), channel_id=1, source_target_pairs={{0,2},{1,3},{2,0},{3,1},{4,6},{5,7},{6,4},{7,5}} | collective-permute-start | bytes 2359304 | tf_op jit(solution)/shard_map/ppermute | solution.py:267
  512.6 37.1 %collective-permute-start.13 = (bf16[96,4096]{1,0:T(8,128)(2,1)}, bf16[96,4096]{1,0:T(8,128)(2,1)}, u32[]{:S(2)}, u32[]{:S(2)}) collective-permute-start(bf16[96,4096]{1,0:T(8,128)(2,1)} %slice.66), channel_id=1, source_target_pairs={{0,4},{1,5},{2,6},{3,7},{4,0},{5,1},{6,2},{7,3}} | collective-permute-start | bytes 2359304 | tf_op jit(solution)/shard_map/ppermute | solution.py:267
  516.9 34.6 %copy-start.14 = (bf16[192,4096]{1,0:T(8,128)(2,1)S(1)}, bf16[192,4096]{1,0:T(8,128)(2,1)}, u32[]{:S(2)}) copy-start(bf16[192,4096]{1,0:T(8,128)(2,1)} %copy-done.13) | copy-start | bytes 4718596
  549.7 62.8 %collective-permute-start.16 = (bf16[192,4096]{1,0:T(8,128)(2,1)S(1)}, bf16[192,4096]{1,0:T(8,128)(2,1)S(1)}, u32[]{:S(2)}, u32[]{:S(2)}) collective-permute-start(bf16[192,4096]{1,0:T(8,128)(2,1)S(1)} %norm_rows.8.own_ref.x_ref), channel_id=1, source_target_pairs={{0,4},{1,5},{2,6},{3,7},{4,0},{5,1},{6,2},{7,3}} | collective-permute-start | bytes 4718600 | tf_op jit(solution)/shard_map/ppermute | solution.py:267
  550.2 63.4 %collective-permute-start.15 = (bf16[192,4096]{1,0:T(8,128)(2,1)S(1)}, bf16[192,4096]{1,0:T(8,128)(2,1)S(1)}, u32[]{:S(2)}, u32[]{:S(2)}) collective-permute-start(bf16[192,4096]{1,0:T(8,128)(2,1)S(1)} %norm_rows.8.own_ref.x_ref), channel_id=1, source_target_pairs={{0,2},{1,3},{2,0},{3,1},{4,6},{5,7},{6,4},{7,5}} | collective-permute-start | bytes 4718600 | tf_op jit(solution)/shard_map/ppermute | solution.py:267
  644.1 38.5 %copy-start.26 = (s32[3]{0:T(128)S(1)}, s32[3]{0:T(128)}, u32[]{:S(2)}) copy-start(s32[3]{0:T(128)} %copy-done.25) | copy-start | bytes 40
  644.2 192.3 %reduce-scatter.13.cloned.1.call-start = ((), (), s32[]{:S(2)}) async-start(), calls=%async_computation.9 | async-start | bytes 7864320 | tf_op jit(solution)/shard_map/reduce_scatter | solution.py:312
  646.6 34.1 %collective-permute-start.17 = (bf16[96,4096]{1,0:T(8,128)(2,1)S(1)}, bf16[96,4096]{1,0:T(8,128)(2,1)S(1)}, u32[]{:S(2)}, u32[]{:S(2)}) collective-permute-start(bf16[96,4096]{1,0:T(8,128)(2,1)S(1)} %slice.70), channel_id=1, source_target_pairs={{0,2},{1,3},{2,0},{3,1},{4,6},{5,7},{6,4},{7,5}} | collective-permute-start | bytes 2359304 | tf_op jit(solution)/shard_map/ppermute | solution.py:267
  647.9 34.7 %collective-permute-start.18 = (bf16[96,4096]{1,0:T(8,128)(2,1)S(1)}, bf16[96,4096]{1,0:T(8,128)(2,1)S(1)}, u32[]{:S(2)}, u32[]{:S(2)}) collective-permute-start(bf16[96,4096]{1,0:T(8,128)(2,1)S(1)} %slice.71), channel_id=1, source_target_pairs={{0,4},{1,5},{2,6},{3,7},{4,0},{5,1},{6,2},{7,3}} | collective-permute-start | bytes 2359304 | tf_op jit(solution)/shard_map/ppermute | solution.py:267
  (35 other events, 53.9 us)
Sparse Core Ops, SparseCore 0:
  11.4 69.2 all-gather.6
  82.5 67.3 all-gather.8
  151.7 66.3 all-gather.10
  220.9 64.4 reduce-scatter.6
  288.2 113.2 reduce-scatter.8
  404.3 98.0 reduce-scatter.10
  508.1 108.6 reduce-scatter.16
  644.3 78.5 reduce-scatter.14
  772.7 63.7 reduce-scatter.12

commit v3 on v2

--- a/solution.py
+++ b/solution.py
@@ -7,11 +7,13 @@
 from jax.experimental.pallas import tpu as pltpu
 from jax.sharding import PartitionSpec as P
 
+
 HEAD_DIM = 128
 GLU_BLOCK = 128
 DEEPNORM_ALPHA = math.sqrt(2.0 * 70)
 LN_EPS = 1e-5
 ROPE_BASE = 10000.0
+VMEM_LIMIT = 60 << 20
 F32 = jnp.float32
 BF16 = jnp.bfloat16
 
@@ -93,7 +95,7 @@
             out_specs=[out_spec, out_spec],
             scratch_shapes=[pltpu.VMEM((seq_len, HEAD_DIM), BF16)],
         ),
-        compiler_params=pltpu.CompilerParams(vmem_limit_bytes=40 << 20),
+        compiler_params=pltpu.CompilerParams(vmem_limit_bytes=VMEM_LIMIT),
         cost_estimate=pl.CostEstimate(flops=24 * 10 ** 9, bytes_accessed=12 << 20, transcendentals=heads * seq_len * seq_len),
         name='attention',
     )(info, qkv, cos_t, sin_t)
@@ -129,10 +131,76 @@
         in_specs=in_specs,
         out_specs=out_spec,
         input_output_aliases=alias,
-        compiler_params=pltpu.CompilerParams(vmem_limit_bytes=24 << 20),
+        compiler_params=pltpu.CompilerParams(vmem_limit_bytes=VMEM_LIMIT),
         cost_estimate=pl.CostEstimate(flops=3 * 10 ** 9, bytes_accessed=6 * rows * width, transcendentals=0),
         name='norm_rows',
     )(*args)
+
+
+QKV_TILE = 512
+ROW_BLOCK = 384
+
+
+def qkv_kernel(pieces, info, *refs):
+    piece_refs, (w_ref, b_ref, out_ref, x_buf, x_sem) = refs[:len(pieces)], refs[len(pieces):]
+    first = pl.program_id(0) == 0
+    in_order = pieces[0] is None
+    bias = b_ref[...].astype(F32)
+
+    def piece_copy(k):
+        if in_order:
+            return pltpu.make_async_copy(
+                piece_refs[0].at[pl.ds(k * ROW_BLOCK, ROW_BLOCK), :], x_buf.at[pl.ds(k * ROW_BLOCK, ROW_BLOCK), :], x_sem.at[k])
+        flip, other, shift, size, whole = pieces[k]
+        device = 2 * jnp.bitwise_xor(info[2], flip) + jnp.bitwise_xor(info[1], other)
+        at = pl.multiple_of(device * whole + shift, size)
+        return pltpu.make_async_copy(piece_refs[k], x_buf.at[pl.ds(at, size), :], x_sem.at[k])
+
+    blocks = x_buf.shape[0] // ROW_BLOCK
+    copies = blocks if in_order else len(pieces)
+
+    @pl.when(first)
+    def _():
+        for k in range(copies):
+            piece_copy(k).start()
+        if not in_order:
+            for k in range(copies):
+                piece_copy(k).wait()
+
+    @pl.loop(0, blocks)
+    def _(block):
+        here = pl.ds(pl.multiple_of(block * ROW_BLOCK, ROW_BLOCK), ROW_BLOCK)
+        if in_order:
+            @pl.when(first)
+            def _():
+                pltpu.make_async_copy(piece_refs[0].at[here, :], x_buf.at[here, :], x_sem.at[block]).wait()
+        out_ref[here, :] = (jnp.dot(x_buf[here, :], w_ref[...], preferred_element_type=F32) + bias).astype(BF16)
+
+
+def qkv_product(info, row_refs, pieces, w_qkv, b_qkv):
+    depth, width = w_qkv.shape
+    rows = sum(r.shape[0] for r in row_refs)
+    hbm = pl.BlockSpec(memory_space=pl.ANY)
+    return pl.pallas_call(
+        functools.partial(qkv_kernel, pieces),
+        out_shape=jax.ShapeDtypeStruct((rows, width), BF16),
+        grid_spec=pltpu.PrefetchScalarGridSpec(
+            num_scalar_prefetch=1,
+            grid=(width // QKV_TILE,),
+            in_specs=[hbm] * len(row_refs) + [
+                pl.BlockSpec((depth, QKV_TILE), lambda j, info: (0, j)),
+                pl.BlockSpec((1, QKV_TILE), lambda j, info: (0, j)),
+            ],
+            out_specs=pl.BlockSpec((rows, QKV_TILE), lambda j, info: (0, j)),
+            scratch_shapes=[
+                pltpu.VMEM((rows, depth), BF16),
+                pltpu.SemaphoreType.DMA((max(len(pieces), rows // ROW_BLOCK),)),
+            ],
+        ),
+        compiler_params=pltpu.CompilerParams(vmem_limit_bytes=VMEM_LIMIT),
+        cost_estimate=pl.CostEstimate(flops=2 * rows * depth * width, bytes_accessed=2 * depth * (rows + width), transcendentals=0),
+        name='qkv',
+    )(info, *row_refs, w_qkv, b_qkv.reshape(1, -1))
 
 
 UP_TILE = 512
@@ -222,7 +290,7 @@
                 pltpu.SemaphoreType.DMA((2,)),
             ],
         ),
-        compiler_params=pltpu.CompilerParams(vmem_limit_bytes=32 << 20),
+        compiler_params=pltpu.CompilerParams(vmem_limit_bytes=VMEM_LIMIT),
         cost_estimate=pl.CostEstimate(flops=4 * rows * depth * width, bytes_accessed=4 * depth * width, transcendentals=rows * width),
         name='up_glu',
     )(info, *row_parts, w_own, w_other, b_all)
@@ -250,13 +318,9 @@
             w_spec,
         ],
         out_specs=pl.BlockSpec((row_tile, tile), lambda j, i: (i, j)),
-        compiler_params=pltpu.CompilerParams(vmem_limit_bytes=32 << 20),
+        compiler_params=pltpu.CompilerParams(vmem_limit_bytes=VMEM_LIMIT),
         cost_estimate=pl.CostEstimate(flops=4 * rows * depth * width, bytes_accessed=4 * depth * width, transcendentals=0),
     )(*lhs, w_own, w_other)
-
-
-def mm(lhs, rhs):
-    return jnp.dot(lhs, rhs, preferred_element_type=F32)
 
 
 def solution(mesh):
@@ -270,29 +334,46 @@
         batch_size, seq_loc, _ = x_loc.shape
         me = lax.axis_index('tp')
         half = seq_loc // 2
-        gathered = [lax.all_gather(x_loc[b], 'tp', axis=0, tiled=True) for b in range(batch_size)]
+        gathered = [lax.all_gather(x_loc[0], 'tp', axis=0, tiled=True)]
         cos_t, sin_t = rope_tables(positions)
         infos = [jnp.stack([prefix_len[b], me % 2, me // 2]).astype(jnp.int32) for b in range(batch_size)]
         out_other, up_other, down_other = from_peer(w_out, 1), from_peer(w_up, 1), from_peer(w_down, 1)
         b_all = jnp.concatenate([b_up, from_peer(b_up, 1)]).reshape(1, -1)
 
+        def near_rows(rows):
+            return from_peer(rows, 2), from_peer(rows, 4)
+
+        def far_rows(near):
+            return from_peer(near[1][:half], 2), from_peer(near[0][half:], 4)
+
+        last_row = batch_size - 1
+        x_late, cos_t, sin_t = lax.optimization_barrier((x_loc, cos_t, sin_t))
+        for b in range(1, last_row):
+            gathered.append(lax.all_gather(x_late[b], 'tp', axis=0, tiled=True))
+        gathered[0], x_last = lax.optimization_barrier((gathered[0], x_late[last_row]))
+        near_x = near_rows(x_last)
+
         attn_loc = []
         for b in range(batch_size):
-            if b == batch_size - 1:
-                gathered[b], up_other, down_other = lax.optimization_barrier((gathered[b], up_other, down_other))
-            qkv = (mm(gathered[b], w_qkv) + b_qkv.astype(F32)).astype(BF16)
+            if b < last_row:
+                row_refs, pieces = (gathered[b],), (None,)
+            else:
+                row_refs = (x_last, *near_x, *far_x)
+                swapped = tuple(from_peer(r, 1) for r in row_refs)
+                swapped, up_other, down_other = lax.optimization_barrier((swapped, up_other, down_other))
+                row_refs = (*row_refs, *swapped)
+                pieces = tuple((flip, other, shift, size, seq_loc) for other in (0, 1) for flip, shift, size in (
+                    (0, 0, seq_loc), (1, 0, seq_loc), (2, 0, seq_loc), (3, 0, half), (3, half, half)))
+            qkv = qkv_product(infos[b], row_refs, pieces, w_qkv, b_qkv)
             mine, other = attention(infos[b], qkv, cos_t[b], sin_t[b], seq_loc)
+            if b == 0:
+                mine, near_x = lax.optimization_barrier((mine, near_x))
+                far_x = far_rows(near_x)
             part = pair_product((mine, from_peer(other, 1)), w_out, out_other, 1024, 768)
             attn_loc.append(lax.psum_scatter(part, 'tp', scatter_dimension=0, axis_index_groups=same_core, tiled=True))
 
         def first_norm(b):
             return norm_rows(x_loc, b, attn_loc[b], b_out, ln1_gain, ln1_bias)
-
-        def near_rows(mid):
-            return from_peer(mid, 2), from_peer(mid, 4)
-
-        def far_rows(near):
-            return from_peer(near[1][:half], 2), from_peer(near[0][half:], 4)
 
         result = None
         mid = first_norm(0)

time: 857 us -> 898 us (1.048)
  Pallas kernels: 371 us -> 504 us
  matrix products: 78.9 us -> 0 us
  local copies, waits for them, and re-layouts: 61.6 us -> 27.3 us
  waiting for transfers between devices: 295 us -> 312 us
    pallas_call x0 -> x3, Pallas kernels: none -> 87.4 us  [qkv_product(): pl.pallas_call(functools.partial(qkv_kernel, pieces), out_shape=jax.Shape...]
    dot_general x3 -> x0, matrix products: 78.9 us -> none  [mm(): return jnp.dot(lhs, rhs, preferred_element_type=F32)]
    ppermute x19 -> x28, waiting for transfers between devices: 148 us -> 194 us  [from_peer(): return lax.ppermute(val, 'tp', [(i, i ^ flip) for i in range(tp)])]
    unnamed x110 -> x68, local copies, waits for them, and re-layouts: 48.9 us -> 10 us
    reduce_scatter x6, waiting for transfers between devices: 85.6 us -> 51.9 us  [layer(): lax.psum_scatter(part, 'tp', scatter_dimension=0, axis_index_groups=same_...]
    pallas_call x6, Pallas kernels: 14.2 us -> 28.7 us  [norm_rows(): pl.pallas_call(norm_kernel, out_shape=out, grid=(rows // step,), in_specs...]
    pallas_call x6, Pallas kernels: 108 us -> 121 us  [pair_product(): pl.pallas_call(pair_kernel, out_shape=jax.ShapeDtypeStruct((rows, width),...]
    pallas_call x3, Pallas kernels: 172 us -> 185 us  [up_glu(): pl.pallas_call(functools.partial(up_kernel, tiles, own_rows), out_shape=j...]
  transfers between devices with their start and end apart: 28 -> 36, of which waited for: 16 -> 18; matrix products, arithmetic and copies ran while one was open for 12% -> 3% of each run, Pallas kernels for 43% -> 56%
where the time goes in v3:
time: 898 us; the launch traced here: 892 us
  Pallas kernels  504 us (56%)
  waiting for transfers between devices  312 us (35%)
  local copies, waits for them, and re-layouts  27.3 us (3%)
  starting transfers between devices  19.8 us (2%)
  other arithmetic  14.6 us (2%)
  between operations  14.1 us (2%)
    ppermute x28, waiting for transfers between devices, from_peer(): return lax.ppermute(val, 'tp', [(i, i ^ flip) for i in range(tp)])  194 us
    pallas_call x3, Pallas kernels, up_glu(): pl.pallas_call(functools.partial(up_kernel, tiles, own_rows), out_shape=j...  185 us
    pallas_call x6, Pallas kernels, pair_product(): pl.pallas_call(pair_kernel, out_shape=jax.ShapeDtypeStruct((rows, width),...  121 us
    pallas_call x3, Pallas kernels, qkv_product(): pl.pallas_call(functools.partial(qkv_kernel, pieces), out_shape=jax.Shape...  87.4 us
    pallas_call x3, Pallas kernels, attention(): pl.pallas_call(functools.partial(attn_kernel, rows, seq_len, key_block),...  82.2 us
    reduce_scatter x6, waiting for transfers between devices, layer(): lax.psum_scatter(part, 'tp', scatter_dimension=0, axis_index_groups=same_...  51.9 us
    all_gather x1, waiting for transfers between devices, layer(): gathered = [lax.all_gather(x_loc[0], 'tp', axis=0, tiled=True)]  49 us
    pallas_call x6, Pallas kernels, norm_rows(): pl.pallas_call(norm_kernel, out_shape=out, grid=(rows // step,), in_specs...  28.7 us
  transfers between devices with their start and end apart: 36, of which 18 were waited for; matrix products, arithmetic and copies ran while one was open for 3% of the time, Pallas kernels for 56%

profile of v3, /device:TPU:0, one launch (start us, length us, event | category | flops | bytes accessed | tf_op | source)
XLA Modules:
  0.0 891.7 jit_solution(1848146068989026344)
XLA Ops:
  6.5 2.7 slice.61
  9.4 8.4 fusion
  17.8 2.7 pad_maximum_fusion
  20.5 1.9 fusion.1
  24.8 1.2 add_add_fusion.info
  26.0 3.1 slice_bitcast_fusion.2
  29.1 1.5 slice_bitcast_fusion.1
  30.6 49.0 %all-gather.5.cloned.1.call-done = bf16[1,1536,4096]{2,1,0:T(8,128)(2,1)} async-done(((bf16[1,192,4096]{2,1,0:T(8,128)(2,1)}), bf16[1,1536,4096]{2,1,0:T(8,128)(2,1)}) %all-gather.5.cloned.1.call-update) | async-done | bytes 12582928 | tf_op jit(solution)/shard_map/all_gather | solution.py:337
  79.9 1.7 collective-permute-start
  81.6 28.7 %qkv.3.qkv_ref = bf16[1536,1536]{1,0:T(8,128)(2,1)} custom-call(s32[3]{0:T(128)} %add_add_fusion.info, bf16[1536,4096]{1,0:T(8,128)(2,1)} %bitcast.21, bf16[4096,1536]{1,0:T(8,128)(2,1)} %refs_10_.1, bf16[1,1536]{1,0:T(2,128)(2,1)} %reshape.44.refs_2_.refs_11_), custom_call_target="tpu_custom_call" | custom-call | flops 19327352832 | bytes 25165824 | tf_op jit(solution)/shard_map/qkv/pallas_call | solution.py:184
  110.3 26.9 %attention.3 = (bf16[768,512]{1,0:T(8,128)(2,1)}, bf16[768,512]{1,0:T(8,128)(2,1)}) custom-call(s32[3]{0:T(128)} %add_add_fusion.info, bf16[1536,1536]{1,0:T(8,128)(2,1)} %qkv.3.qkv_ref, f32[1536,128]{1,0:T(8,128)} %get-tuple-element.90.cos_ref, f32[1536,128]{1,0:T(8,128)} %get-tuple-element.87.sin_ref), custom_call_target="tpu_custom_call" | custom-call | flops 24000000000 | bytes 12582912 | tf_op jit(solution)/shard_map/attention/pallas_call | solution.py:84
  140.6 10.9 %shard_map.145 = bf16[768,4096]{1,0:T(8,128)(2,1)} custom-call(bf16[768,512]{1,0:T(8,128)(2,1)} %get-tuple-element.50.a_ref, bf16[768,512]{1,0:T(8,128)(2,1)} %copy-done.28, bf16[512,4096]{1,0:T(8,128)(2,1)} %wa_ref.8, bf16[512,4096]{1,0:T(8,128)(2,1)} %collective-permute-done.3.wb_ref), custom_call_target="tpu_custom_call" | custom-call | flops 6442450944 | bytes 8388608 | tf_op jit(solution)/shard_map/pallas_call | solution.py:310
  153.5 16.6 %all-gather.7.cloned.1.call-done = bf16[1,1536,4096]{2,1,0:T(8,128)(2,1)} async-done(((bf16[1,192,4096]{2,1,0:T(8,128)(2,1)}), bf16[1,1536,4096]{2,1,0:T(8,128)(2,1)}) %all-gather.7.cloned.1.call-update) | async-done | bytes 12582928 | tf_op jit(solution)/shard_map/all_gather | solution.py:352
  170.0 27.9 %qkv.4.qkv_ref = bf16[1536,1536]{1,0:T(8,128)(2,1)} custom-call(s32[3]{0:T(128)} %add_add_fusion.1.info, bf16[1536,4096]{1,0:T(8,128)(2,1)} %bitcast.20, bf16[4096,1536]{1,0:T(8,128)(2,1)} %refs_10_.1, bf16[1,1536]{1,0:T(2,128)(2,1)} %reshape.44.refs_2_.refs_11_), custom_call_target="tpu_custom_call" | custom-call | flops 19327352832 | bytes 25165824 | tf_op jit(solution)/shard_map/qkv/pallas_call | solution.py:184
  198.0 25.9 %attention.4 = (bf16[768,512]{1,0:T(8,128)(2,1)}, bf16[768,512]{1,0:T(8,128)(2,1)}) custom-call(s32[3]{0:T(128)} %add_add_fusion.1.info, bf16[1536,1536]{1,0:T(8,128)(2,1)} %qkv.4.qkv_ref, f32[1536,128]{1,0:T(8,128)} %get-tuple-element.89.cos_ref, f32[1536,128]{1,0:T(8,128)} %get-tuple-element.86.sin_ref), custom_call_target="tpu_custom_call" | custom-call | flops 24000000000 | bytes 12582912 | tf_op jit(solution)/shard_map/attention/pallas_call | solution.py:84
  224.1 2.2 collective-permute-done.8.b_ref
  227.2 10.9 %shard_map.146 = bf16[768,4096]{1,0:T(8,128)(2,1)} custom-call(bf16[768,512]{1,0:T(8,128)(2,1)} %get-tuple-element.52.a_ref, bf16[768,512]{1,0:T(8,128)(2,1)} %copy-done.31, bf16[512,4096]{1,0:T(8,128)(2,1)} %wa_ref.8, bf16[512,4096]{1,0:T(8,128)(2,1)} %collective-permute-done.3.wb_ref), custom_call_target="tpu_custom_call" | custom-call | flops 6442450944 | bytes 8388608 | tf_op jit(solution)/shard_map/pallas_call | solution.py:310
  241.2 1.5 collective-permute-start.12
  243.8 32.6 %collective-permute-done.12.refs_3_ = bf16[96,4096]{1,0:T(8,128)(2,1)S(1)} collective-permute-done((bf16[96,4096]{1,0:T(8,128)(2,1)S(1)}, bf16[96,4096]{1,0:T(8,128)(2,1)S(1)}, u32[]{:S(2)}, u32[]{:S(2)}) %collective-permute-start.12) | collective-permute-done | bytes 786464 | tf_op jit(solution)/shard_map/ppermute | solution.py:331
  276.5 2.3 collective-permute-done.14.refs_4_
  283.7 30.8 %qkv.5.qkv_ref = bf16[1536,1536]{1,0:T(8,128)(2,1)} custom-call(s32[3]{0:T(128)} %add_add_fusion.2.info, bf16[192,4096]{1,0:T(8,128)(2,1)} %get-tuple-element.49.refs_0_, bf16[192,4096]{1,0:T(8,128)(2,1)} %collective-permute-done.refs_1_, bf16[192,4096]{1,0:T(8,128)(2,1)} %copy-done.1, bf16[96,4096]{1,0:T(8,128)(2,1)} %copy-done.20, ...), custom_call_target="tpu_custom_call" | custom-call | flops 19327352832 | bytes 25165824 | tf_op jit(solution)/shard_map/qkv/pallas_call | solution.py:184
  314.5 29.5 %attention.5 = (bf16[768,512]{1,0:T(8,128)(2,1)}, bf16[768,512]{1,0:T(8,128)(2,1)}) custom-call(s32[3]{0:T(128)} %add_add_fusion.2.info, bf16[1536,1536]{1,0:T(8,128)(2,1)} %qkv.5.qkv_ref, f32[1536,128]{1,0:T(8,128)} %get-tuple-element.88.cos_ref, f32[1536,128]{1,0:T(8,128)} %get-tuple-element.85.sin_ref), custom_call_target="tpu_custom_call" | custom-call | flops 24000000000 | bytes 12582912 | tf_op jit(solution)/shard_map/attention/pallas_call | solution.py:84
  344.0 2.5 collective-permute-done.23.b_ref
  347.3 10.8 %shard_map.147 = bf16[768,4096]{1,0:T(8,128)(2,1)} custom-call(bf16[768,512]{1,0:T(8,128)(2,1)} %get-tuple-element.70.a_ref, bf16[768,512]{1,0:T(8,128)(2,1)} %copy-done.30, bf16[512,4096]{1,0:T(8,128)(2,1)} %wa_ref.8, bf16[512,4096]{1,0:T(8,128)(2,1)} %collective-permute-done.3.wb_ref), custom_call_target="tpu_custom_call" | custom-call | flops 6442450944 | bytes 8388608 | tf_op jit(solution)/shard_map/pallas_call | solution.py:310
  360.7 4.8 norm_rows.6.own_ref.x_ref
  366.8 64.6 %collective-permute-done.5.y_ref = bf16[192,4096]{1,0:T(8,128)(2,1)S(1)} collective-permute-done((bf16[192,4096]{1,0:T(8,128)(2,1)}, bf16[192,4096]{1,0:T(8,128)(2,1)S(1)}, u32[]{:S(2)}, u32[]{:S(2)}) %collective-permute-start.5) | collective-permute-done | bytes 1572896 | tf_op jit(solution)/shard_map/ppermute | solution.py:331
  431.4 1.5 collective-permute-start.6
  435.3 4.6 norm_rows.7.own_ref.x_ref
  440.0 27.5 %collective-permute-done.6.far_a_ref = bf16[96,4096]{1,0:T(8,128)(2,1)S(1)} collective-permute-done((bf16[96,4096]{1,0:T(8,128)(2,1)S(1)}, bf16[96,4096]{1,0:T(8,128)(2,1)S(1)}, u32[]{:S(2)}, u32[]{:S(2)}) %collective-permute-start.6) | collective-permute-done | bytes 786464 | tf_op jit(solution)/shard_map/ppermute | solution.py:331
  468.0 1.5 collective-permute-start.19
  469.5 61.5 %up_glu.3.a_ref.b_ref = bf16[768,3584]{1,0:T(8,128)(2,1)} custom-call(s32[3]{0:T(128)} %add_add_fusion.info, bf16[192,4096]{1,0:T(8,128)(2,1)} %norm_rows.6.own_ref.x_ref, bf16[192,4096]{1,0:T(8,128)(2,1)} %copy-done.4, bf16[192,4096]{1,0:T(8,128)(2,1)} %copy-done.3, bf16[96,4096]{1,0:T(8,128)(2,1)} %copy-done.22, bf16[96,4096]{1,0:T(8,128)(2,1)} %copy-done.24, ...), custom_call_target="tpu_custom_call" | custom-call | flops 45097156608 | bytes 58720256 | tf_op jit(solution)/shard_map/up_glu/pallas_call | solution.py:278
  531.0 29.4 %shard_map.150 = bf16[768,4096]{1,0:T(8,128)(2,1)} custom-call(bf16[768,3584]{1,0:T(8,128)(2,1)} %up_glu.3.a_ref.b_ref, bf16[768,3584]{1,0:T(8,128)(2,1)} %up_glu.3.a_ref.b_ref, bf16[1792,4096]{1,0:T(8,128)(2,1)} %wa_ref.11, bf16[1792,4096]{1,0:T(8,128)(2,1)} %collective-permute-done.17.wb_ref), custom_call_target="tpu_custom_call" | custom-call | flops 22548578304 | bytes 29360128 | tf_op jit(solution)/shard_map/pallas_call | solution.py:310
  560.7 1.2 slice.74
  562.5 1.5 collective-permute-start.22
  564.0 5.0 norm_rows.8.own_ref.x_ref
  569.0 27.7 %collective-permute-done.21.far_a_ref = bf16[96,4096]{1,0:T(8,128)(2,1)S(1)} collective-permute-done((bf16[96,4096]{1,0:T(8,128)(2,1)S(1)}, bf16[96,4096]{1,0:T(8,128)(2,1)S(1)}, u32[]{:S(2)}, u32[]{:S(2)}) %collective-permute-start.21) | collective-permute-done | bytes 786464 | tf_op jit(solution)/shard_map/ppermute | solution.py:331
  598.1 2.1 collective-permute-start.25
  600.2 1.2 collective-permute-start.24
  601.5 61.6 %up_glu.4.a_ref.b_ref = bf16[768,3584]{1,0:T(8,128)(2,1)} custom-call(s32[3]{0:T(128)} %add_add_fusion.1.info, bf16[192,4096]{1,0:T(8,128)(2,1)} %norm_rows.7.own_ref.x_ref, bf16[192,4096]{1,0:T(8,128)(2,1)} %collective-permute-done.19.x_ref, bf16[192,4096]{1,0:T(8,128)(2,1)} %copy-done.2, bf16[96,4096]{1,0:T(8,128)(2,1)} %copy-done.25, ...), custom_call_target="tpu_custom_call" | custom-call | flops 45097156608 | bytes 58720256 | tf_op jit(solution)/shard_map/up_glu/pallas_call | solution.py:278
  663.1 30.1 %shard_map.149 = bf16[768,4096]{1,0:T(8,128)(2,1)} custom-call(bf16[768,3584]{1,0:T(8,128)(2,1)} %up_glu.4.a_ref.b_ref, bf16[768,3584]{1,0:T(8,128)(2,1)} %up_glu.4.a_ref.b_ref, bf16[1792,4096]{1,0:T(8,128)(2,1)} %wa_ref.11, bf16[1792,4096]{1,0:T(8,128)(2,1)} %collective-permute-done.17.wb_ref), custom_call_target="tpu_custom_call" | custom-call | flops 22548578304 | bytes 29360128 | tf_op jit(solution)/shard_map/pallas_call | solution.py:310
  694.5 28.1 %collective-permute-done.26.far_a_ref = bf16[96,4096]{1,0:T(8,128)(2,1)S(1)} collective-permute-done((bf16[96,4096]{1,0:T(8,128)(2,1)S(1)}, bf16[96,4096]{1,0:T(8,128)(2,1)S(1)}, u32[]{:S(2)}, u32[]{:S(2)}) %collective-permute-start.26) | collective-permute-done | bytes 786464 | tf_op jit(solution)/shard_map/ppermute | solution.py:331
  722.6 1.9 collective-permute-done.27.far_b_ref
  725.4 61.7 %up_glu.5.a_ref.b_ref = bf16[768,3584]{1,0:T(8,128)(2,1)} custom-call(s32[3]{0:T(128)} %add_add_fusion.2.info, bf16[192,4096]{1,0:T(8,128)(2,1)} %norm_rows.8.own_ref.x_ref, bf16[192,4096]{1,0:T(8,128)(2,1)} %copy-done.6, bf16[192,4096]{1,0:T(8,128)(2,1)} %copy-done.5, bf16[96,4096]{1,0:T(8,128)(2,1)} %copy-done.27, bf16[96,4096]{1,0:T(8,128)(2,1)} %copy-done.29, ...), custom_call_target="tpu_custom_call" | custom-call | flops 45097156608 | bytes 58720256 | tf_op jit(solution)/shard_map/up_glu/pallas_call | solution.py:278
  787.1 28.9 %shard_map.148 = bf16[768,4096]{1,0:T(8,128)(2,1)} custom-call(bf16[768,3584]{1,0:T(8,128)(2,1)} %up_glu.5.a_ref.b_ref, bf16[768,3584]{1,0:T(8,128)(2,1)} %up_glu.5.a_ref.b_ref, bf16[1792,4096]{1,0:T(8,128)(2,1)} %wa_ref.11, bf16[1792,4096]{1,0:T(8,128)(2,1)} %collective-permute-done.17.wb_ref), custom_call_target="tpu_custom_call" | custom-call | flops 22548578304 | bytes 29360128 | tf_op jit(solution)/shard_map/pallas_call | solution.py:310
  818.5 5.0 norm_rows.9.out_refs_0_
  823.5 4.6 norm_rows.10.out_refs_0_
  828.1 51.9 %reduce-scatter.13.cloned.1.call-done.part_ref = bf16[192,4096]{1,0:T(8,128)(2,1)} async-done(((bf16[768,4096]{1,0:T(8,128)(2,1)}), bf16[192,4096]{1,0:T(8,128)(2,1)}) %reduce-scatter.13.cloned.1.call-update) | async-done | bytes 1572880 | tf_op jit(solution)/shard_map/reduce_scatter | solution.py:393
  880.0 4.6 norm_rows.11
  (151 shorter events, 33.0 us)
Async XLA Ops:
  6.5 2.8 copy-start.7
  6.5 73.0 %all-gather.5.cloned.1.call-start = ((), (), s32[]{:S(2)}) async-start(), calls=%async_computation.12 | async-start | bytes 14155776 | tf_op jit(solution)/shard_map/all_gather | solution.py:337
  9.3 160.7 %all-gather.7.cloned.1.call-start = ((), (), s32[]{:S(2)}) async-start(), calls=%async_computation.13 | async-start | bytes 14155776 | tf_op jit(solution)/shard_map/all_gather | solution.py:352
  9.4 11.1 %slice-start = ((s8[4718592]{0:T(1024)(128)(4,1)}), s8[4194304]{0:T(1024)(128)(4,1)S(1)}, s32[]{:S(2)}) async-start(s8[4718592]{0:T(1024)(128)(4,1)} %bitcast.18), calls=%async_computation.14 | async-start | bytes 8388608
  17.8 2.7 slice-start.1
  20.5 3.1 copy-start.16
  20.5 3.7 copy-start.15
  22.4 338.3 %reduce-scatter.7.cloned.1.call-start = ((), (), s32[]{:S(2)}) async-start(), calls=%async_computation.6 | async-start | bytes 7864320 | tf_op jit(solution)/shard_map/reduce_scatter | solution.py:373
  22.7 259.8 %collective-permute-start.16 = (bf16[4096,3584]{1,0:T(8,128)(2,1)}, bf16[4096,3584]{1,0:T(8,128)(2,1)}, u32[]{:S(2)}, u32[]{:S(2)}) collective-permute-start(bf16[4096,3584]{1,0:T(8,128)(2,1)} %w_own.5), channel_id=1, source_target_pairs={{0,1},{1,0},{2,3},{3,2},{4,5},{5,4},{6,7},{7,6}} | collective-permute-start | bytes 88080392 | tf_op jit(solution)/shard_map/ppermute | solution.py:331
  23.6 115.7 %collective-permute-start.3 = (bf16[512,4096]{1,0:T(8,128)(2,1)}, bf16[512,4096]{1,0:T(8,128)(2,1)}, u32[]{:S(2)}, u32[]{:S(2)}) collective-permute-start(bf16[512,4096]{1,0:T(8,128)(2,1)} %wa_ref.8), channel_id=1, source_target_pairs={{0,1},{1,0},{2,3},{3,2},{4,5},{5,4},{6,7},{7,6}} | collective-permute-start | bytes 12582920 | tf_op jit(solution)/shard_map/ppermute | solution.py:331
  79.6 58.6 %collective-permute-start.1 = (bf16[192,4096]{1,0:T(8,128)(2,1)}, bf16[192,4096]{1,0:T(8,128)(2,1)S(1)}, u32[]{:S(2)}, u32[]{:S(2)}) collective-permute-start(bf16[192,4096]{1,0:T(8,128)(2,1)} %get-tuple-element.49.refs_0_), channel_id=1, source_target_pairs={{0,4},{1,5},{2,6},{3,7},{4,0},{5,1},{6,2},{7,3}} | collective-permute-start | bytes 4718600 | tf_op jit(solution)/shard_map/ppermute | solution.py:331
  79.9 59.3 %collective-permute-start = (bf16[192,4096]{1,0:T(8,128)(2,1)}, bf16[192,4096]{1,0:T(8,128)(2,1)}, u32[]{:S(2)}, u32[]{:S(2)}) collective-permute-start(bf16[192,4096]{1,0:T(8,128)(2,1)} %get-tuple-element.49.refs_0_), channel_id=1, source_target_pairs={{0,2},{1,3},{2,0},{3,1},{4,6},{5,7},{6,4},{7,5}} | collective-permute-start | bytes 4718600 | tf_op jit(solution)/shard_map/ppermute | solution.py:331
  137.2 2.5 collective-permute-start.2
  138.2 105.1 %copy-start.1 = (bf16[192,4096]{1,0:T(8,128)(2,1)}, bf16[192,4096]{1,0:T(8,128)(2,1)S(1)}, u32[]{:S(2)}) copy-start(bf16[192,4096]{1,0:T(8,128)(2,1)S(1)} %collective-permute-done.1.refs_2_) | copy-start | bytes 4718596
  151.5 283.9 %reduce-scatter.9.cloned.1.call-start = ((), (), s32[]{:S(2)}) async-start(), calls=%async_computation.7 | async-start | bytes 7864320 | tf_op jit(solution)/shard_map/reduce_scatter | solution.py:373
  152.0 91.3 %collective-permute-start.17 = (bf16[1792,4096]{1,0:T(8,128)(2,1)}, bf16[1792,4096]{1,0:T(8,128)(2,1)}, u32[]{:S(2)}, u32[]{:S(2)}) collective-permute-start(bf16[1792,4096]{1,0:T(8,128)(2,1)} %wa_ref.11), channel_id=1, source_target_pairs={{0,1},{1,0},{2,3},{3,2},{4,5},{5,4},{6,7},{7,6}} | collective-permute-start | bytes 44040200 | tf_op jit(solution)/shard_map/ppermute | solution.py:331
  223.8 2.5 collective-permute-start.8
  238.2 325.8 %reduce-scatter.11.cloned.1.call-start = ((), (), s32[]{:S(2)}) async-start(), calls=%async_computation.8 | async-start | bytes 7864320 | tf_op jit(solution)/shard_map/reduce_scatter | solution.py:373
  239.6 3.8 collective-permute-start.9
  241.2 35.3 %collective-permute-start.12 = (bf16[96,4096]{1,0:T(8,128)(2,1)S(1)}, bf16[96,4096]{1,0:T(8,128)(2,1)S(1)}, u32[]{:S(2)}, u32[]{:S(2)}) collective-permute-start(bf16[96,4096]{1,0:T(8,128)(2,1)S(1)} %slice.71), channel_id=1, source_target_pairs={{0,2},{1,3},{2,0},{3,1},{4,6},{5,7},{6,4},{7,5}} | collective-permute-start | bytes 2359304 | tf_op jit(solution)/shard_map/ppermute | solution.py:331
  242.7 36.1 %collective-permute-start.14 = (bf16[96,4096]{1,0:T(8,128)(2,1)S(1)}, bf16[96,4096]{1,0:T(8,128)(2,1)S(1)}, u32[]{:S(2)}, u32[]{:S(2)}) collective-permute-start(bf16[96,4096]{1,0:T(8,128)(2,1)S(1)} %slice.72), channel_id=1, source_target_pairs={{0,4},{1,5},{2,6},{3,7},{4,0},{5,1},{6,2},{7,3}} | collective-permute-start | bytes 2359304 | tf_op jit(solution)/shard_map/ppermute | solution.py:331
  243.3 37.8 %collective-permute-start.10 = (bf16[192,4096]{1,0:T(8,128)(2,1)}, bf16[192,4096]{1,0:T(8,128)(2,1)S(1)}, u32[]{:S(2)}, u32[]{:S(2)}) collective-permute-start(bf16[192,4096]{1,0:T(8,128)(2,1)} %collective-permute-done.refs_1_), channel_id=1, source_target_pairs={{0,1},{1,0},{2,3},{3,2},{4,5},{5,4},{6,7},{7,6}} | collective-permute-start | bytes 4718600 | tf_op jit(solution)/shard_map/ppermute | solution.py:331
  243.3 37.7 %copy-start.17 = (bf16[192,4096]{1,0:T(8,128)(2,1)}, bf16[192,4096]{1,0:T(8,128)(2,1)S(1)}, u32[]{:S(2)}) copy-start(bf16[192,4096]{1,0:T(8,128)(2,1)S(1)} %collective-permute-done.9.refs_5_) | copy-start | bytes 4718596
  243.3 37.7 %collective-permute-start.11 = (bf16[192,4096]{1,0:T(8,128)(2,1)S(1)}, bf16[192,4096]{1,0:T(8,128)(2,1)S(1)}, u32[]{:S(2)}, u32[]{:S(2)}) collective-permute-start(bf16[192,4096]{1,0:T(8,128)(2,1)S(1)} %collective-permute-done.1.refs_2_), channel_id=1, source_target_pairs={{0,1},{1,0},{2,3},{3,2},{4,5},{5,4},{6,7},{7,6}} | collective-permute-start | bytes 4718600 | tf_op jit(solution)/shard_map/ppermute | solution.py:331
  276.5 4.6 copy-start.20
  276.5 3.5 collective-permute-start.13
  278.8 2.3 collective-permute-start.15
  344.0 2.5 collective-permute-start.23
  358.2 460.3 %reduce-scatter.17.cloned.1.call-start = ((), (), s32[]{:S(2)}) async-start(), calls=%async_computation.11 | async-start | bytes 7864320 | tf_op jit(solution)/shard_map/reduce_scatter | solution.py:393
  365.5 68.0 %copy-start.14 = (bf16[3584]{0:T(1024)(128)(2,1)S(1)}, bf16[3584]{0:T(1024)(128)(2,1)}, u32[]{:S(2)}) copy-start(bf16[3584]{0:T(1024)(128)(2,1)} %param.25) | copy-start | bytes 21508
  365.6 65.8 %collective-permute-start.5 = (bf16[192,4096]{1,0:T(8,128)(2,1)}, bf16[192,4096]{1,0:T(8,128)(2,1)S(1)}, u32[]{:S(2)}, u32[]{:S(2)}) collective-permute-start(bf16[192,4096]{1,0:T(8,128)(2,1)} %norm_rows.6.own_ref.x_ref), channel_id=1, source_target_pairs={{0,4},{1,5},{2,6},{3,7},{4,0},{5,1},{6,2},{7,3}} | collective-permute-start | bytes 4718600 | tf_op jit(solution)/shard_map/ppermute | solution.py:331
  366.5 66.4 %collective-permute-start.4 = (bf16[192,4096]{1,0:T(8,128)(2,1)}, bf16[192,4096]{1,0:T(8,128)(2,1)S(1)}, u32[]{:S(2)}, u32[]{:S(2)}) collective-permute-start(bf16[192,4096]{1,0:T(8,128)(2,1)} %norm_rows.6.own_ref.x_ref), channel_id=1, source_target_pairs={{0,2},{1,3},{2,0},{3,1},{4,6},{5,7},{6,4},{7,5}} | collective-permute-start | bytes 4718600 | tf_op jit(solution)/shard_map/ppermute | solution.py:331
  431.4 36.0 %collective-permute-start.6 = (bf16[96,4096]{1,0:T(8,128)(2,1)S(1)}, bf16[96,4096]{1,0:T(8,128)(2,1)S(1)}, u32[]{:S(2)}, u32[]{:S(2)}) collective-permute-start(bf16[96,4096]{1,0:T(8,128)(2,1)S(1)} %slice.80), channel_id=1, source_target_pairs={{0,2},{1,3},{2,0},{3,1},{4,6},{5,7},{6,4},{7,5}} | collective-permute-start | bytes 2359304 | tf_op jit(solution)/shard_map/ppermute | solution.py:331
  433.0 34.5 %collective-permute-start.7 = (bf16[96,4096]{1,0:T(8,128)(2,1)S(1)}, bf16[96,4096]{1,0:T(8,128)(2,1)S(1)}, u32[]{:S(2)}, u32[]{:S(2)}) collective-permute-start(bf16[96,4096]{1,0:T(8,128)(2,1)S(1)} %slice.81), channel_id=1, source_target_pairs={{0,4},{1,5},{2,6},{3,7},{4,0},{5,1},{6,2},{7,3}} | collective-permute-start | bytes 2359304 | tf_op jit(solution)/shard_map/ppermute | solution.py:331
  433.5 1.2 collective-permute-start.18
  467.5 63.5 %collective-permute-start.20 = (bf16[192,4096]{1,0:T(8,128)(2,1)}, bf16[192,4096]{1,0:T(8,128)(2,1)S(1)}, u32[]{:S(2)}, u32[]{:S(2)}) collective-permute-start(bf16[192,4096]{1,0:T(8,128)(2,1)} %norm_rows.7.own_ref.x_ref), channel_id=1, source_target_pairs={{0,4},{1,5},{2,6},{3,7},{4,0},{5,1},{6,2},{7,3}} | collective-permute-start | bytes 4718600 | tf_op jit(solution)/shard_map/ppermute | solution.py:331
  468.0 63.0 %collective-permute-start.19 = (bf16[192,4096]{1,0:T(8,128)(2,1)}, bf16[192,4096]{1,0:T(8,128)(2,1)}, u32[]{:S(2)}, u32[]{:S(2)}) collective-permute-start(bf16[192,4096]{1,0:T(8,128)(2,1)} %norm_rows.7.own_ref.x_ref), channel_id=1, source_target_pairs={{0,2},{1,3},{2,0},{3,1},{4,6},{5,7},{6,4},{7,5}} | collective-permute-start | bytes 4718600 | tf_op jit(solution)/shard_map/ppermute | solution.py:331
  531.0 30.9 %copy-start.2 = (bf16[192,4096]{1,0:T(8,128)(2,1)}, bf16[192,4096]{1,0:T(8,128)(2,1)S(1)}, u32[]{:S(2)}) copy-start(bf16[192,4096]{1,0:T(8,128)(2,1)S(1)} %collective-permute-done.20.y_ref) | copy-start | bytes 4718596
  560.5 263.0 %reduce-scatter.15.cloned.1.call-start = ((), (), s32[]{:S(2)}) async-start(), calls=%async_computation.10 | async-start | bytes 7864320 | tf_op jit(solution)/shard_map/reduce_scatter | solution.py:393
  562.0 34.7 %collective-permute-start.21 = (bf16[96,4096]{1,0:T(8,128)(2,1)S(1)}, bf16[96,4096]{1,0:T(8,128)(2,1)S(1)}, u32[]{:S(2)}, u32[]{:S(2)}) collective-permute-start(bf16[96,4096]{1,0:T(8,128)(2,1)S(1)} %slice.73), channel_id=1, source_target_pairs={{0,2},{1,3},{2,0},{3,1},{4,6},{5,7},{6,4},{7,5}} | collective-permute-start | bytes 2359304 | tf_op jit(solution)/shard_map/ppermute | solution.py:331
  562.5 35.6 %collective-permute-start.22 = (bf16[96,4096]{1,0:T(8,128)(2,1)S(1)}, bf16[96,4096]{1,0:T(8,128)(2,1)}, u32[]{:S(2)}, u32[]{:S(2)}) collective-permute-start(bf16[96,4096]{1,0:T(8,128)(2,1)S(1)} %slice.74), channel_id=1, source_target_pairs={{0,4},{1,5},{2,6},{3,7},{4,0},{5,1},{6,2},{7,3}} | collective-permute-start | bytes 2359304 | tf_op jit(solution)/shard_map/ppermute | solution.py:331
  598.1 65.0 %collective-permute-start.25 = (bf16[192,4096]{1,0:T(8,128)(2,1)}, bf16[192,4096]{1,0:T(8,128)(2,1)S(1)}, u32[]{:S(2)}, u32[]{:S(2)}) collective-permute-start(bf16[192,4096]{1,0:T(8,128)(2,1)} %norm_rows.8.own_ref.x_ref), channel_id=1, source_target_pairs={{0,4},{1,5},{2,6},{3,7},{4,0},{5,1},{6,2},{7,3}} | collective-permute-start | bytes 4718600 | tf_op jit(solution)/shard_map/ppermute | solution.py:331
  600.2 62.8 %collective-permute-start.24 = (bf16[192,4096]{1,0:T(8,128)(2,1)}, bf16[192,4096]{1,0:T(8,128)(2,1)S(1)}, u32[]{:S(2)}, u32[]{:S(2)}) collective-permute-start(bf16[192,4096]{1,0:T(8,128)(2,1)} %norm_rows.8.own_ref.x_ref), channel_id=1, source_target_pairs={{0,2},{1,3},{2,0},{3,1},{4,6},{5,7},{6,4},{7,5}} | collective-permute-start | bytes 4718600 | tf_op jit(solution)/shard_map/ppermute | solution.py:331
  663.1 30.3 %copy-start.5 = (bf16[192,4096]{1,0:T(8,128)(2,1)}, bf16[192,4096]{1,0:T(8,128)(2,1)S(1)}, u32[]{:S(2)}) copy-start(bf16[192,4096]{1,0:T(8,128)(2,1)S(1)} %collective-permute-done.25.y_ref) | copy-start | bytes 4718596
  663.1 30.2 %copy-start.6 = (bf16[192,4096]{1,0:T(8,128)(2,1)}, bf16[192,4096]{1,0:T(8,128)(2,1)S(1)}, u32[]{:S(2)}) copy-start(bf16[192,4096]{1,0:T(8,128)(2,1)S(1)} %collective-permute-done.24.x_ref) | copy-start | bytes 4718596
  693.2 186.7 %reduce-scatter.13.cloned.1.call-start = ((), (), s32[]{:S(2)}) async-start(), calls=%async_computation.9 | async-start | bytes 7864320 | tf_op jit(solution)/shard_map/reduce_scatter | solution.py:393
  693.4 29.2 %collective-permute-start.26 = (bf16[96,4096]{1,0:T(8,128)(2,1)S(1)}, bf16[96,4096]{1,0:T(8,128)(2,1)S(1)}, u32[]{:S(2)}, u32[]{:S(2)}) collective-permute-start(bf16[96,4096]{1,0:T(8,128)(2,1)S(1)} %slice.78), channel_id=1, source_target_pairs={{0,2},{1,3},{2,0},{3,1},{4,6},{5,7},{6,4},{7,5}} | collective-permute-start | bytes 2359304 | tf_op jit(solution)/shard_map/ppermute | solution.py:331
  694.1 30.4 %collective-permute-start.27 = (bf16[96,4096]{1,0:T(8,128)(2,1)S(1)}, bf16[96,4096]{1,0:T(8,128)(2,1)S(1)}, u32[]{:S(2)}, u32[]{:S(2)}) collective-permute-start(bf16[96,4096]{1,0:T(8,128)(2,1)S(1)} %slice.79), channel_id=1, source_target_pairs={{0,4},{1,5},{2,6},{3,7},{4,0},{5,1},{6,2},{7,3}} | collective-permute-start | bytes 2359304 | tf_op jit(solution)/shard_map/ppermute | solution.py:331
  (22 other events, 30.0 us)
Sparse Core Ops, SparseCore 0:
  9.4 70.1 all-gather.4
  81.4 88.5 all-gather.6
  172.9 64.5 reduce-scatter.6
  240.3 79.6 reduce-scatter.8
  358.3 110.5 reduce-scatter.10
  560.6 106.5 reduce-scatter.16
  693.4 72.7 reduce-scatter.14
  816.2 63.7 reduce-scatter.12

commit v4 on v3

--- a/solution.py
+++ b/solution.py
@@ -106,20 +106,25 @@
     out_refs[-1][...] = layer_norm(resid, gain_ref[...], shift_ref[...]).astype(BF16)
 
 
-def norm_rows(x_rows, x_at, part, bias, gain, shift, out_rows=None, out_at=None, into=None):
+NORM_ROWS = 96
+
+
+def norm_rows(x_rows, x_at, part, bias, gain, shift, lo=0, out_shape=None, out_at=None, into=None):
     rows, width = part.shape
-    step = 64
-    spec = pl.BlockSpec((step, width), lambda i: (i, 0))
+    skip = lo // NORM_ROWS
     vec = pl.BlockSpec((1, width), lambda i: (0, 0))
-    x_spec = spec if x_at is None else pl.BlockSpec((None, step, width), lambda i: (x_at, i, 0))
+    if x_at is None:
+        x_spec = pl.BlockSpec((NORM_ROWS, width), lambda i: (skip + i, 0))
+    else:
+        x_spec = pl.BlockSpec((None, NORM_ROWS, width), lambda i: (x_at, skip + i, 0))
     args = [x_rows, part, bias.reshape(1, -1), gain.reshape(1, -1), shift.reshape(1, -1)]
-    in_specs = [x_spec, spec, vec, vec, vec]
+    in_specs = [x_spec, pl.BlockSpec((NORM_ROWS, width), lambda i: (i, 0)), vec, vec, vec]
     alias = {}
-    if out_rows is None:
-        out, out_spec = jax.ShapeDtypeStruct((rows, width), BF16), spec
+    if out_shape is None:
+        out, out_spec = jax.ShapeDtypeStruct((rows, width), BF16), in_specs[1]
     else:
-        out = jax.ShapeDtypeStruct((out_rows, rows, width), BF16)
-        out_spec = pl.BlockSpec((None, step, width), lambda i: (out_at, i, 0))
+        out = jax.ShapeDtypeStruct(out_shape, BF16)
+        out_spec = pl.BlockSpec((None, NORM_ROWS, width), lambda i: (out_at, skip + i, 0))
     if into is not None:
         args.append(into)
         in_specs.append(pl.BlockSpec(memory_space=pl.ANY))
@@ -127,7 +132,7 @@
     return pl.pallas_call(
         norm_kernel,
         out_shape=out,
-        grid=(rows // step,),
+        grid=(rows // NORM_ROWS,),
         in_specs=in_specs,
         out_specs=out_spec,
         input_output_aliases=alias,
@@ -207,10 +212,10 @@
 UP_ROWS = 384
 
 
-def up_kernel(tiles, own_rows, info, own_ref, x_ref, y_ref, far_a_ref, far_b_ref, w_own, w_other, b_ref, m_ref, h_buf, w_buf, h_sem, w_sem):
+def up_kernel(tiles, pieces, size, info, *refs):
+    piece_refs, (w_own, w_other, b_ref, m_ref, h_buf, w_buf, h_sem, w_sem) = refs[:len(pieces)], refs[len(pieces):]
     step = pl.program_id(0)
     chip = info[2]
-    half = own_rows // 2
 
     def weight_copy(at, start):
         slot = lax.rem(at, 2)
@@ -233,10 +238,9 @@
             go(w_other, at - tiles)
 
     def row_copies():
-        parts = ((own_ref, 0, 0, own_rows), (x_ref, 1, 0, own_rows), (y_ref, 2, 0, own_rows), (far_a_ref, 3, 0, half), (far_b_ref, 3, half, half))
-        for k, (src, flip, shift, size) in enumerate(parts):
-            at = pl.multiple_of(jnp.bitwise_xor(chip, flip) * own_rows + shift, half)
-            yield pltpu.make_async_copy(src, h_buf.at[pl.ds(at, size), :], h_sem.at[k])
+        for k, (flip, src_at, dst_at, count) in enumerate(pieces):
+            at = pl.multiple_of(jnp.bitwise_xor(chip, flip) * size + dst_at, NORM_ROWS)
+            yield pltpu.make_async_copy(piece_refs[k].at[pl.ds(src_at, count), :], h_buf.at[pl.ds(at, count), :], h_sem.at[k])
 
     @pl.when(step == 0)
     def _():
@@ -269,31 +273,38 @@
             m_ref[here, GLU_BLOCK * pair:GLU_BLOCK * (pair + 1)] = (value * jax.nn.gelu(gate, approximate=True)).astype(BF16)
 
 
-def up_glu(info, row_parts, w_own, w_other, b_all):
+def up_glu(info, row_parts, lo, size, w_own, w_other, b_all):
     own_rows, depth = row_parts[0].shape
-    rows = 4 * own_rows
+    half = own_rows // 2
+    refs = list(row_parts[:3])
+    pieces = [(flip, lo, 0, size) for flip in range(3)]
+    for part in range(2):
+        if lo <= part * half < lo + size:
+            refs.append(row_parts[3 + part])
+            pieces.append((3, 0, part * half - lo, half))
+    rows = 4 * size
     width = w_own.shape[1]
     tiles = width // UP_TILE
     hbm = pl.BlockSpec(memory_space=pl.ANY)
     return pl.pallas_call(
-        functools.partial(up_kernel, tiles, own_rows),
+        functools.partial(up_kernel, tiles, tuple(pieces), size),
         out_shape=jax.ShapeDtypeStruct((rows, width), BF16),
         grid_spec=pltpu.PrefetchScalarGridSpec(
             num_scalar_prefetch=1,
             grid=(2 * tiles,),
-            in_specs=[hbm] * 7 + [pl.BlockSpec((1, UP_TILE), lambda j, info: (0, j))],
+            in_specs=[hbm] * (len(refs) + 2) + [pl.BlockSpec((1, UP_TILE), lambda j, info: (0, j))],
             out_specs=pl.BlockSpec((rows, UP_TILE // 2), lambda j, info: (0, j)),
             scratch_shapes=[
                 pltpu.VMEM((rows, depth), BF16),
                 pltpu.VMEM((2, depth, UP_TILE), BF16),
-                pltpu.SemaphoreType.DMA((5,)),
+                pltpu.SemaphoreType.DMA((len(refs),)),
                 pltpu.SemaphoreType.DMA((2,)),
             ],
         ),
         compiler_params=pltpu.CompilerParams(vmem_limit_bytes=VMEM_LIMIT),
         cost_estimate=pl.CostEstimate(flops=4 * rows * depth * width, bytes_accessed=4 * depth * width, transcendentals=rows * width),
         name='up_glu',
-    )(info, *row_parts, w_own, w_other, b_all)
+    )(info, *refs, w_own, w_other, b_all)
 
 
 def pair_kernel(a_ref, b_ref, wa_ref, wb_ref, out_ref):
@@ -353,6 +364,9 @@
         gathered[0], x_last = lax.optimization_barrier((gathered[0], x_late[last_row]))
         near_x = near_rows(x_last)
 
+        def first_norm(b):
+            return norm_rows(x_loc, b, attn_loc[b], b_out, ln1_gain, ln1_bias)
+
         attn_loc = []
         for b in range(batch_size):
             if b < last_row:
@@ -360,7 +374,9 @@
             else:
                 row_refs = (x_last, *near_x, *far_x)
                 swapped = tuple(from_peer(r, 1) for r in row_refs)
-                swapped, up_other, down_other = lax.optimization_barrier((swapped, up_other, down_other))
+                mid = first_norm(0)
+                swapped, up_other, down_other, mid = lax.optimization_barrier((swapped, up_other, down_other, mid))
+                near = near_rows(mid)
                 row_refs = (*row_refs, *swapped)
                 pieces = tuple((flip, other, shift, size, seq_loc) for other in (0, 1) for flip, shift, size in (
                     (0, 0, seq_loc), (1, 0, seq_loc), (2, 0, seq_loc), (3, 0, half), (3, half, half)))
@@ -369,29 +385,28 @@
             if b == 0:
                 mine, near_x = lax.optimization_barrier((mine, near_x))
                 far_x = far_rows(near_x)
+            if b == last_row:
+                mine, near = lax.optimization_barrier((mine, near))
+                far = far_rows(near)
             part = pair_product((mine, from_peer(other, 1)), w_out, out_other, 1024, 768)
             attn_loc.append(lax.psum_scatter(part, 'tp', scatter_dimension=0, axis_index_groups=same_core, tiled=True))
 
-        def first_norm(b):
-            return norm_rows(x_loc, b, attn_loc[b], b_out, ln1_gain, ln1_bias)
-
         result = None
-        mid = first_norm(0)
-        near = near_rows(mid)
-        far = far_rows(near)
         for b in range(batch_size):
             parts = (mid, *near, *far)
-            last = b == batch_size - 1
+            last = b == last_row
             if not last:
                 parts, next_mid = lax.optimization_barrier((parts, first_norm(b + 1)))
                 next_near = near_rows(next_mid)
-            acts = up_glu(infos[b], parts, w_up, up_other, b_all)
-            if not last:
-                acts, next_near = lax.optimization_barrier((acts, next_near))
-                next_far = far_rows(next_near)
-            part = pair_product((acts, acts), w_down, down_other, 512, 768)
-            ffn_loc = lax.psum_scatter(part, 'tp', scatter_dimension=0, axis_index_groups=same_core, tiled=True)
-            result = norm_rows(mid, None, ffn_loc, b_down, ln2_gain, ln2_bias, batch_size, b, result)
+            size = half if last else seq_loc
+            for lo in range(0, seq_loc, size):
+                acts = up_glu(infos[b], parts, lo, size, w_up, up_other, b_all)
+                if not last:
+                    acts, next_near = lax.optimization_barrier((acts, next_near))
+                    next_far = far_rows(next_near)
+                part = pair_product((acts, acts), w_down, down_other, 512, 4 * size)
+                ffn_loc = lax.psum_scatter(part, 'tp', scatter_dimension=0, axis_index_groups=same_core, tiled=True)
+                result = norm_rows(mid, None, ffn_loc, b_down, ln2_gain, ln2_bias, lo, x_loc.shape, b, result)
             if not last:
                 mid, near, far = next_mid, next_near, next_far
         return result

time: 898 us -> 851 us (0.948)
  waiting for transfers between devices: 312 us -> 245 us
  Pallas kernels: 504 us -> 523 us
    ppermute x28, waiting for transfers between devices: 194 us -> 153 us  [from_peer(): return lax.ppermute(val, 'tp', [(i, i ^ flip) for i in range(tp)])]
    reduce_scatter x6 -> x7, waiting for transfers between devices: 51.9 us -> 26.4 us  [layer(): lax.psum_scatter(part, 'tp', scatter_dimension=0, axis_index_groups=same_...]
    pallas_call x9 -> x11, Pallas kernels: 213 us -> 223 us  [the longest x4 196 us: up_glu(): pl.pallas_call(functools.partial(up_kernel, tiles, tuple(pieces), size),...]
    pallas_call x6 -> x7, Pallas kernels: 121 us -> 130 us  [pair_product(): pl.pallas_call(pair_kernel, out_shape=jax.ShapeDtypeStruct((rows, width),...]
  transfers between devices with their start and end apart: 36 -> 37, of which waited for: 18 -> 17; matrix products, arithmetic and copies ran while one was open for 3% -> 4% of each run, Pallas kernels for 56% -> 62%
where the time goes in v4:
time: 851 us; the launch traced here: 845 us
  Pallas kernels  523 us (61%)
  waiting for transfers between devices  245 us (29%)
  local copies, waits for them, and re-layouts  26.7 us (3%)
  starting transfers between devices  20.6 us (2%)
  other arithmetic  14.8 us (2%)
  between operations  14.1 us (2%)
    pallas_call x4, Pallas kernels, up_glu(): pl.pallas_call(functools.partial(up_kernel, tiles, tuple(pieces), size),...  196 us
    ppermute x28, waiting for transfers between devices, from_peer(): return lax.ppermute(val, 'tp', [(i, i ^ flip) for i in range(tp)])  153 us
    pallas_call x7, Pallas kernels, pair_product(): pl.pallas_call(pair_kernel, out_shape=jax.ShapeDtypeStruct((rows, width),...  130 us
    pallas_call x3, Pallas kernels, qkv_product(): pl.pallas_call(functools.partial(qkv_kernel, pieces), out_shape=jax.Shape...  87.4 us
    pallas_call x3, Pallas kernels, attention(): pl.pallas_call(functools.partial(attn_kernel, rows, seq_len, key_block),...  82.1 us
    all_gather x1, waiting for transfers between devices, layer(): gathered = [lax.all_gather(x_loc[0], 'tp', axis=0, tiled=True)]  48.7 us
    pallas_call x7, Pallas kernels, norm_rows(): pl.pallas_call(norm_kernel, out_shape=out, grid=(rows // NORM_ROWS,), in_...  27.6 us
    reduce_scatter x7, waiting for transfers between devices, layer(): lax.psum_scatter(part, 'tp', scatter_dimension=0, axis_index_groups=same_...  26.4 us
  transfers between devices with their start and end apart: 37, of which 17 were waited for; matrix products, arithmetic and copies ran while one was open for 4% of the time, Pallas kernels for 62%

profile of v4, /device:TPU:0, one launch (start us, length us, event | category | flops | bytes accessed | tf_op | source)
XLA Modules:
  0.0 844.7 jit_solution(12737351811353529852)
XLA Ops:
  6.5 2.8 slice.60
  9.4 8.4 fusion
  17.8 2.7 pad_maximum_fusion
  20.5 1.9 fusion.1
  26.4 3.1 slice_bitcast_fusion.1
  30.9 48.7 %all-gather.5.cloned.1.call-done = bf16[1,1536,4096]{2,1,0:T(8,128)(2,1)} async-done(((bf16[1,192,4096]{2,1,0:T(8,128)(2,1)}), bf16[1,1536,4096]{2,1,0:T(8,128)(2,1)}) %all-gather.5.cloned.1.call-update) | async-done | bytes 12582928 | tf_op jit(solution)/shard_map/all_gather | solution.py:348
  79.6 1.5 collective-permute-start.1
  81.6 28.7 %qkv.3.qkv_ref = bf16[1536,1536]{1,0:T(8,128)(2,1)} custom-call(s32[3]{0:T(128)} %add_add_fusion.info, bf16[1536,4096]{1,0:T(8,128)(2,1)} %bitcast.21, bf16[4096,1536]{1,0:T(8,128)(2,1)} %refs_1_.3, bf16[1,1536]{1,0:T(2,128)(2,1)} %reshape.22.refs_2_.refs_11_), custom_call_target="tpu_custom_call" | custom-call | flops 19327352832 | bytes 25165824 | tf_op jit(solution)/shard_map/qkv/pallas_call | solution.py:189
  110.3 26.8 %attention.3 = (bf16[768,512]{1,0:T(8,128)(2,1)}, bf16[768,512]{1,0:T(8,128)(2,1)}) custom-call(s32[3]{0:T(128)} %add_add_fusion.info, bf16[1536,1536]{1,0:T(8,128)(2,1)} %qkv.3.qkv_ref, f32[1536,128]{1,0:T(8,128)} %get-tuple-element.98.cos_ref, f32[1536,128]{1,0:T(8,128)} %get-tuple-element.95.sin_ref), custom_call_target="tpu_custom_call" | custom-call | flops 24000000000 | bytes 12582912 | tf_op jit(solution)/shard_map/attention/pallas_call | solution.py:84
  138.4 2.5 collective-permute-done.2.refs_2_
  141.9 10.9 %shard_map.145 = bf16[768,4096]{1,0:T(8,128)(2,1)} custom-call(bf16[768,512]{1,0:T(8,128)(2,1)} %get-tuple-element.56.a_ref, bf16[768,512]{1,0:T(8,128)(2,1)} %copy-done.20, bf16[512,4096]{1,0:T(8,128)(2,1)} %wa_ref.9, bf16[512,4096]{1,0:T(8,128)(2,1)} %collective-permute-done.12.wb_ref), custom_call_target="tpu_custom_call" | custom-call | flops 6442450944 | bytes 8388608 | tf_op jit(solution)/shard_map/pallas_call | solution.py:321
  154.3 16.9 %all-gather.7.cloned.1.call-done = bf16[1,1536,4096]{2,1,0:T(8,128)(2,1)} async-done(((bf16[1,192,4096]{2,1,0:T(8,128)(2,1)}), bf16[1,1536,4096]{2,1,0:T(8,128)(2,1)}) %all-gather.7.cloned.1.call-update) | async-done | bytes 12582928 | tf_op jit(solution)/shard_map/all_gather | solution.py:363
  171.2 27.9 %qkv.5.qkv_ref = bf16[1536,1536]{1,0:T(8,128)(2,1)} custom-call(s32[3]{0:T(128)} %add_add_fusion.2.info, bf16[1536,4096]{1,0:T(8,128)(2,1)} %bitcast.20, bf16[4096,1536]{1,0:T(8,128)(2,1)} %refs_1_.3, bf16[1,1536]{1,0:T(2,128)(2,1)} %reshape.22.refs_2_.refs_11_), custom_call_target="tpu_custom_call" | custom-call | flops 19327352832 | bytes 25165824 | tf_op jit(solution)/shard_map/qkv/pallas_call | solution.py:189
  199.2 25.9 %attention.5 = (bf16[768,512]{1,0:T(8,128)(2,1)}, bf16[768,512]{1,0:T(8,128)(2,1)}) custom-call(s32[3]{0:T(128)} %add_add_fusion.2.info, bf16[1536,1536]{1,0:T(8,128)(2,1)} %qkv.5.qkv_ref, f32[1536,128]{1,0:T(8,128)} %get-tuple-element.96.cos_ref, f32[1536,128]{1,0:T(8,128)} %get-tuple-element.93.sin_ref), custom_call_target="tpu_custom_call" | custom-call | flops 24000000000 | bytes 12582912 | tf_op jit(solution)/shard_map/attention/pallas_call | solution.py:84
  225.4 2.2 collective-permute-done.17.b_ref
  228.4 11.1 %shard_map.146 = bf16[768,4096]{1,0:T(8,128)(2,1)} custom-call(bf16[768,512]{1,0:T(8,128)(2,1)} %get-tuple-element.67.a_ref, bf16[768,512]{1,0:T(8,128)(2,1)} %copy-done.23, bf16[512,4096]{1,0:T(8,128)(2,1)} %wa_ref.9, bf16[512,4096]{1,0:T(8,128)(2,1)} %collective-permute-done.12.wb_ref), custom_call_target="tpu_custom_call" | custom-call | flops 6442450944 | bytes 8388608 | tf_op jit(solution)/shard_map/pallas_call | solution.py:321
  244.6 34.0 %collective-permute-done.5.refs_3_ = bf16[96,4096]{1,0:T(8,128)(2,1)} collective-permute-done((bf16[96,4096]{1,0:T(8,128)(2,1)S(1)}, bf16[96,4096]{1,0:T(8,128)(2,1)}, u32[]{:S(2)}, u32[]{:S(2)}) %collective-permute-start.5) | collective-permute-done | bytes 786464 | tf_op jit(solution)/shard_map/ppermute | solution.py:342
  282.4 4.1 norm_rows.7.refs_0_.x_ref
  286.5 1.6 collective-permute-start.13
  288.6 30.7 %qkv.4.qkv_ref = bf16[1536,1536]{1,0:T(8,128)(2,1)} custom-call(s32[3]{0:T(128)} %add_add_fusion.1.info, bf16[192,4096]{1,0:T(8,128)(2,1)} %get-tuple-element.49.refs_0_, bf16[192,4096]{1,0:T(8,128)(2,1)} %copy-done.1, bf16[192,4096]{1,0:T(8,128)(2,1)} %collective-permute-done.2.refs_2_, bf16[96,4096]{1,0:T(8,128)(2,1)} %collective-permute-done.5.refs_3_, ...), custom_call_target="tpu_custom_call" | custom-call | flops 19327352832 | bytes 25165824 | tf_op jit(solution)/shard_map/qkv/pallas_call | solution.py:189
  319.3 29.4 %attention.4 = (bf16[768,512]{1,0:T(8,128)(2,1)}, bf16[768,512]{1,0:T(8,128)(2,1)}) custom-call(s32[3]{0:T(128)} %add_add_fusion.1.info, bf16[1536,1536]{1,0:T(8,128)(2,1)} %qkv.4.qkv_ref, f32[1536,128]{1,0:T(8,128)} %get-tuple-element.97.cos_ref, f32[1536,128]{1,0:T(8,128)} %get-tuple-element.94.sin_ref), custom_call_target="tpu_custom_call" | custom-call | flops 24000000000 | bytes 12582912 | tf_op jit(solution)/shard_map/attention/pallas_call | solution.py:84
  348.8 2.5 collective-permute-done.23.b_ref
  352.1 10.9 %shard_map.147 = bf16[768,4096]{1,0:T(8,128)(2,1)} custom-call(bf16[768,512]{1,0:T(8,128)(2,1)} %get-tuple-element.78.a_ref, bf16[768,512]{1,0:T(8,128)(2,1)} %copy-done.21, bf16[512,4096]{1,0:T(8,128)(2,1)} %wa_ref.9, bf16[512,4096]{1,0:T(8,128)(2,1)} %collective-permute-done.12.wb_ref), custom_call_target="tpu_custom_call" | custom-call | flops 6442450944 | bytes 8388608 | tf_op jit(solution)/shard_map/pallas_call | solution.py:321
  368.6 4.1 norm_rows.8.refs_0_.x_ref
  372.7 27.5 %collective-permute-done.15.refs_3_ = bf16[96,4096]{1,0:T(8,128)(2,1)} collective-permute-done((bf16[96,4096]{1,0:T(8,128)(2,1)S(1)}, bf16[96,4096]{1,0:T(8,128)(2,1)}, u32[]{:S(2)}, u32[]{:S(2)}) %collective-permute-start.15) | collective-permute-done | bytes 786464 | tf_op jit(solution)/shard_map/ppermute | solution.py:342
  400.2 1.7 collective-permute-done.16.refs_4_
  402.7 2.1 collective-permute-start.20
  404.7 61.6 %up_glu.4.a_ref.b_ref = bf16[768,3584]{1,0:T(8,128)(2,1)} custom-call(s32[3]{0:T(128)} %add_add_fusion.info, bf16[192,4096]{1,0:T(8,128)(2,1)} %norm_rows.7.refs_0_.x_ref, bf16[192,4096]{1,0:T(8,128)(2,1)} %copy-done.2, bf16[192,4096]{1,0:T(8,128)(2,1)} %collective-permute-done.14.refs_2_, bf16[96,4096]{1,0:T(8,128)(2,1)} %collective-permute-done.15.refs_3_, ...), custom_call_target="tpu_custom_call" | custom-call | flops 45097156608 | bytes 58720256 | tf_op jit(solution)/shard_map/up_glu/pallas_call | solution.py:289
  466.4 29.4 %shard_map.151 = bf16[768,4096]{1,0:T(8,128)(2,1)} custom-call(bf16[768,3584]{1,0:T(8,128)(2,1)} %up_glu.4.a_ref.b_ref, bf16[768,3584]{1,0:T(8,128)(2,1)} %up_glu.4.a_ref.b_ref, bf16[1792,4096]{1,0:T(8,128)(2,1)} %wa_ref.13, bf16[1792,4096]{1,0:T(8,128)(2,1)} %collective-permute-done.10.wb_ref), custom_call_target="tpu_custom_call" | custom-call | flops 22548578304 | bytes 29360128 | tf_op jit(solution)/shard_map/pallas_call | solution.py:321
  497.9 1.8 collective-permute-start.22
  499.7 4.6 norm_rows.9.refs_0_.x_ref
  504.3 26.7 %collective-permute-done.21.refs_3_ = bf16[96,4096]{1,0:T(8,128)(2,1)} collective-permute-done((bf16[96,4096]{1,0:T(8,128)(2,1)S(1)}, bf16[96,4096]{1,0:T(8,128)(2,1)}, u32[]{:S(2)}, u32[]{:S(2)}) %collective-permute-start.21) | collective-permute-done | bytes 786464 | tf_op jit(solution)/shard_map/ppermute | solution.py:342
  531.0 2.0 collective-permute-done.22.refs_4_
  534.1 2.2 collective-permute-start.25
  536.3 61.5 %up_glu.5.a_ref.b_ref = bf16[768,3584]{1,0:T(8,128)(2,1)} custom-call(s32[3]{0:T(128)} %add_add_fusion.2.info, bf16[192,4096]{1,0:T(8,128)(2,1)} %norm_rows.8.refs_0_.x_ref, bf16[192,4096]{1,0:T(8,128)(2,1)} %copy-done.3, bf16[192,4096]{1,0:T(8,128)(2,1)} %collective-permute-done.20.refs_2_, bf16[96,4096]{1,0:T(8,128)(2,1)} %collective-permute-done.21.refs_3_, ...), custom_call_target="tpu_custom_call" | custom-call | flops 45097156608 | bytes 58720256 | tf_op jit(solution)/shard_map/up_glu/pallas_call | solution.py:289
  597.9 30.2 %shard_map.150 = bf16[768,4096]{1,0:T(8,128)(2,1)} custom-call(bf16[768,3584]{1,0:T(8,128)(2,1)} %up_glu.5.a_ref.b_ref, bf16[768,3584]{1,0:T(8,128)(2,1)} %up_glu.5.a_ref.b_ref, bf16[1792,4096]{1,0:T(8,128)(2,1)} %wa_ref.13, bf16[1792,4096]{1,0:T(8,128)(2,1)} %collective-permute-done.10.wb_ref), custom_call_target="tpu_custom_call" | custom-call | flops 22548578304 | bytes 29360128 | tf_op jit(solution)/shard_map/pallas_call | solution.py:321
  628.2 2.1 collective-permute-start.27
  630.3 24.2 %collective-permute-done.27.refs_3_ = bf16[96,4096]{1,0:T(8,128)(2,1)S(1)} collective-permute-done((bf16[96,4096]{1,0:T(8,128)(2,1)S(1)}, bf16[96,4096]{1,0:T(8,128)(2,1)S(1)}, u32[]{:S(2)}, u32[]{:S(2)}) %collective-permute-start.27) | collective-permute-done | bytes 786464 | tf_op jit(solution)/shard_map/ppermute | solution.py:342
  655.4 37.0 %up_glu.7.a_ref.b_ref = bf16[384,3584]{1,0:T(8,128)(2,1)} custom-call(s32[3]{0:T(128)} %add_add_fusion.1.info, bf16[192,4096]{1,0:T(8,128)(2,1)} %norm_rows.9.refs_0_.x_ref, bf16[192,4096]{1,0:T(8,128)(2,1)} %copy-done.4, bf16[192,4096]{1,0:T(8,128)(2,1)} %copy-done.6, bf16[96,4096]{1,0:T(8,128)(2,1)} %copy-done.24, bf16[4096,3584]{1,0:T(8,128)(2,1)} %refs_4_.3, ...), custom_call_target="tpu_custom_call" | custom-call | flops 22548578304 | bytes 58720256 | tf_op jit(solution)/shard_map/up_glu/pallas_call | solution.py:289
  692.4 18.8 %shard_map.149 = bf16[384,4096]{1,0:T(8,128)(2,1)} custom-call(bf16[384,3584]{1,0:T(8,128)(2,1)} %up_glu.7.a_ref.b_ref, bf16[384,3584]{1,0:T(8,128)(2,1)} %up_glu.7.a_ref.b_ref, bf16[1792,4096]{1,0:T(8,128)(2,1)} %wa_ref.13, bf16[1792,4096]{1,0:T(8,128)(2,1)} %collective-permute-done.10.wb_ref), custom_call_target="tpu_custom_call" | custom-call | flops 11274289152 | bytes 29360128 | tf_op jit(solution)/shard_map/pallas_call | solution.py:321
  712.6 25.9 %collective-permute-done.26.refs_3_ = bf16[96,4096]{1,0:T(8,128)(2,1)S(1)} collective-permute-done((bf16[96,4096]{1,0:T(8,128)(2,1)S(1)}, bf16[96,4096]{1,0:T(8,128)(2,1)S(1)}, u32[]{:S(2)}, u32[]{:S(2)}) %collective-permute-start.26) | collective-permute-done | bytes 786464 | tf_op jit(solution)/shard_map/ppermute | solution.py:342
  739.4 35.8 %up_glu.6.a_ref.b_ref = bf16[384,3584]{1,0:T(8,128)(2,1)} custom-call(s32[3]{0:T(128)} %add_add_fusion.1.info, bf16[192,4096]{1,0:T(8,128)(2,1)} %norm_rows.9.refs_0_.x_ref, bf16[192,4096]{1,0:T(8,128)(2,1)} %copy-done.4, bf16[192,4096]{1,0:T(8,128)(2,1)} %copy-done.6, bf16[96,4096]{1,0:T(8,128)(2,1)} %copy-done.22, bf16[4096,3584]{1,0:T(8,128)(2,1)} %refs_4_.3, ...), custom_call_target="tpu_custom_call" | custom-call | flops 22548578304 | bytes 58720256 | tf_op jit(solution)/shard_map/up_glu/pallas_call | solution.py:289
  775.2 18.7 %shard_map.148 = bf16[384,4096]{1,0:T(8,128)(2,1)} custom-call(bf16[384,3584]{1,0:T(8,128)(2,1)} %up_glu.6.a_ref.b_ref, bf16[384,3584]{1,0:T(8,128)(2,1)} %up_glu.6.a_ref.b_ref, bf16[1792,4096]{1,0:T(8,128)(2,1)} %wa_ref.13, bf16[1792,4096]{1,0:T(8,128)(2,1)} %collective-permute-done.10.wb_ref), custom_call_target="tpu_custom_call" | custom-call | flops 11274289152 | bytes 29360128 | tf_op jit(solution)/shard_map/pallas_call | solution.py:321
  796.5 4.1 norm_rows.10.out_refs_0_
  800.6 4.1 norm_rows.11.out_refs_0_
  804.7 3.3 norm_rows.12.out_refs_0_
  808.0 26.4 %reduce-scatter.14.cloned.1.call-done.part_ref = bf16[96,4096]{1,0:T(8,128)(2,1)} async-done(((bf16[384,4096]{1,0:T(8,128)(2,1)}), bf16[96,4096]{1,0:T(8,128)(2,1)}) %reduce-scatter.14.cloned.1.call-update) | async-done | bytes 786448 | tf_op jit(solution)/shard_map/reduce_scatter | solution.py:408
  834.4 3.2 norm_rows.13
  (143 shorter events, 36.5 us)
Async XLA Ops:
  6.5 73.1 %all-gather.5.cloned.1.call-start = ((), (), s32[]{:S(2)}) async-start(), calls=%async_computation.14 | async-start | bytes 14155776 | tf_op jit(solution)/shard_map/all_gather | solution.py:348
  9.3 161.9 %all-gather.7.cloned.1.call-start = ((), (), s32[]{:S(2)}) async-start(), calls=%async_computation.15 | async-start | bytes 14155776 | tf_op jit(solution)/shard_map/all_gather | solution.py:363
  9.4 11.1 %slice-start = ((s8[4718592]{0:T(1024)(128)(4,1)}), s8[4194304]{0:T(1024)(128)(4,1)S(1)}, s32[]{:S(2)}) async-start(s8[4718592]{0:T(1024)(128)(4,1)} %bitcast.18), calls=%async_computation.16 | async-start | bytes 8388608
  20.5 4.0 copy-start.15
  22.5 259.9 %reduce-scatter.8.cloned.1.call-start = ((), (), s32[]{:S(2)}) async-start(), calls=%async_computation.7 | async-start | bytes 7864320 | tf_op jit(solution)/shard_map/reduce_scatter | solution.py:392
  23.0 263.5 %collective-permute-start.9 = (bf16[4096,3584]{1,0:T(8,128)(2,1)}, bf16[4096,3584]{1,0:T(8,128)(2,1)}, u32[]{:S(2)}, u32[]{:S(2)}) collective-permute-start(bf16[4096,3584]{1,0:T(8,128)(2,1)} %refs_4_.3), channel_id=1, source_target_pairs={{0,1},{1,0},{2,3},{3,2},{4,5},{5,4},{6,7},{7,6}} | collective-permute-start | bytes 88080392 | tf_op jit(solution)/shard_map/ppermute | solution.py:342
  23.9 117.1 %collective-permute-start.12 = (bf16[512,4096]{1,0:T(8,128)(2,1)}, bf16[512,4096]{1,0:T(8,128)(2,1)}, u32[]{:S(2)}, u32[]{:S(2)}) collective-permute-start(bf16[512,4096]{1,0:T(8,128)(2,1)} %wa_ref.9), channel_id=1, source_target_pairs={{0,1},{1,0},{2,3},{3,2},{4,5},{5,4},{6,7},{7,6}} | collective-permute-start | bytes 12582920 | tf_op jit(solution)/shard_map/ppermute | solution.py:342
  79.6 58.8 %collective-permute-start.1 = (bf16[192,4096]{1,0:T(8,128)(2,1)}, bf16[192,4096]{1,0:T(8,128)(2,1)S(1)}, u32[]{:S(2)}, u32[]{:S(2)}) collective-permute-start(bf16[192,4096]{1,0:T(8,128)(2,1)} %get-tuple-element.49.refs_0_), channel_id=1, source_target_pairs={{0,2},{1,3},{2,0},{3,1},{4,6},{5,7},{6,4},{7,5}} | collective-permute-start | bytes 4718600 | tf_op jit(solution)/shard_map/ppermute | solution.py:342
  81.1 59.9 %collective-permute-start.2 = (bf16[192,4096]{1,0:T(8,128)(2,1)}, bf16[192,4096]{1,0:T(8,128)(2,1)}, u32[]{:S(2)}, u32[]{:S(2)}) collective-permute-start(bf16[192,4096]{1,0:T(8,128)(2,1)} %get-tuple-element.49.refs_0_), channel_id=1, source_target_pairs={{0,4},{1,5},{2,6},{3,7},{4,0},{5,1},{6,2},{7,3}} | collective-permute-start | bytes 4718600 | tf_op jit(solution)/shard_map/ppermute | solution.py:342
  137.2 3.8 collective-permute-start.11
  138.4 105.0 %copy-start.1 = (bf16[192,4096]{1,0:T(8,128)(2,1)}, bf16[192,4096]{1,0:T(8,128)(2,1)S(1)}, u32[]{:S(2)}) copy-start(bf16[192,4096]{1,0:T(8,128)(2,1)S(1)} %collective-permute-done.1.refs_1_) | copy-start | bytes 4718596
  152.8 215.8 %reduce-scatter.10.cloned.1.call-start = ((), (), s32[]{:S(2)}) async-start(), calls=%async_computation.8 | async-start | bytes 7864320 | tf_op jit(solution)/shard_map/reduce_scatter | solution.py:392
  153.0 90.4 %collective-permute-start.10 = (bf16[1792,4096]{1,0:T(8,128)(2,1)}, bf16[1792,4096]{1,0:T(8,128)(2,1)}, u32[]{:S(2)}, u32[]{:S(2)}) collective-permute-start(bf16[1792,4096]{1,0:T(8,128)(2,1)} %wa_ref.13), channel_id=1, source_target_pairs={{0,1},{1,0},{2,3},{3,2},{4,5},{5,4},{6,7},{7,6}} | collective-permute-start | bytes 44040200 | tf_op jit(solution)/shard_map/ppermute | solution.py:342
  225.1 2.5 collective-permute-start.17
  239.5 39.7 %copy-start.8 = (bf16[4096]{0:T(1024)(128)(2,1)S(1)}, bf16[4096]{0:T(1024)(128)(2,1)}, u32[]{:S(2)}) copy-start(bf16[4096]{0:T(1024)(128)(2,1)} %param.21) | copy-start | bytes 24580
  239.6 40.3 %copy-start.9 = (bf16[4096]{0:T(1024)(128)(2,1)S(1)}, bf16[4096]{0:T(1024)(128)(2,1)}, u32[]{:S(2)}) copy-start(bf16[4096]{0:T(1024)(128)(2,1)} %param.22) | copy-start | bytes 24580
  239.6 40.9 %copy-start.10 = (bf16[4096]{0:T(1024)(128)(2,1)S(1)}, bf16[4096]{0:T(1024)(128)(2,1)}, u32[]{:S(2)}) copy-start(bf16[4096]{0:T(1024)(128)(2,1)} %param.23) | copy-start | bytes 24580
  239.6 260.1 %reduce-scatter.12.cloned.1.call-start = ((), (), s32[]{:S(2)}) async-start(), calls=%async_computation.9 | async-start | bytes 7864320 | tf_op jit(solution)/shard_map/reduce_scatter | solution.py:392
  240.9 3.4 collective-permute-start
  242.3 36.3 %collective-permute-start.5 = (bf16[96,4096]{1,0:T(8,128)(2,1)S(1)}, bf16[96,4096]{1,0:T(8,128)(2,1)}, u32[]{:S(2)}, u32[]{:S(2)}) collective-permute-start(bf16[96,4096]{1,0:T(8,128)(2,1)S(1)} %slice.65), channel_id=1, source_target_pairs={{0,2},{1,3},{2,0},{3,1},{4,6},{5,7},{6,4},{7,5}} | collective-permute-start | bytes 2359304 | tf_op jit(solution)/shard_map/ppermute | solution.py:342
  243.0 36.3 %collective-permute-start.7 = (bf16[96,4096]{1,0:T(8,128)(2,1)S(1)}, bf16[96,4096]{1,0:T(8,128)(2,1)}, u32[]{:S(2)}, u32[]{:S(2)}) collective-permute-start(bf16[96,4096]{1,0:T(8,128)(2,1)S(1)} %slice.66), channel_id=1, source_target_pairs={{0,4},{1,5},{2,6},{3,7},{4,0},{5,1},{6,2},{7,3}} | collective-permute-start | bytes 2359304 | tf_op jit(solution)/shard_map/ppermute | solution.py:342
  243.4 43.1 %collective-permute-start.3 = (bf16[192,4096]{1,0:T(8,128)(2,1)S(1)}, bf16[192,4096]{1,0:T(8,128)(2,1)}, u32[]{:S(2)}, u32[]{:S(2)}) collective-permute-start(bf16[192,4096]{1,0:T(8,128)(2,1)S(1)} %collective-permute-done.1.refs_1_), channel_id=1, source_target_pairs={{0,1},{1,0},{2,3},{3,2},{4,5},{5,4},{6,7},{7,6}} | collective-permute-start | bytes 4718600 | tf_op jit(solution)/shard_map/ppermute | solution.py:342
  244.3 36.8 %copy-start.17 = (bf16[192,4096]{1,0:T(8,128)(2,1)}, bf16[192,4096]{1,0:T(8,128)(2,1)S(1)}, u32[]{:S(2)}) copy-start(bf16[192,4096]{1,0:T(8,128)(2,1)S(1)} %collective-permute-done.refs_5_) | copy-start | bytes 4718596
  244.3 42.2 %collective-permute-start.4 = (bf16[192,4096]{1,0:T(8,128)(2,1)}, bf16[192,4096]{1,0:T(8,128)(2,1)S(1)}, u32[]{:S(2)}, u32[]{:S(2)}) collective-permute-start(bf16[192,4096]{1,0:T(8,128)(2,1)} %collective-permute-done.2.refs_2_), channel_id=1, source_target_pairs={{0,1},{1,0},{2,3},{3,2},{4,5},{5,4},{6,7},{7,6}} | collective-permute-start | bytes 4718600 | tf_op jit(solution)/shard_map/ppermute | solution.py:342
  278.6 7.9 collective-permute-start.6
  279.3 7.2 collective-permute-start.8
  286.5 62.2 %collective-permute-start.13 = (bf16[192,4096]{1,0:T(8,128)(2,1)}, bf16[192,4096]{1,0:T(8,128)(2,1)S(1)}, u32[]{:S(2)}, u32[]{:S(2)}) collective-permute-start(bf16[192,4096]{1,0:T(8,128)(2,1)} %norm_rows.7.refs_0_.x_ref), channel_id=1, source_target_pairs={{0,2},{1,3},{2,0},{3,1},{4,6},{5,7},{6,4},{7,5}} | collective-permute-start | bytes 4718600 | tf_op jit(solution)/shard_map/ppermute | solution.py:342
  288.1 60.7 %collective-permute-start.14 = (bf16[192,4096]{1,0:T(8,128)(2,1)}, bf16[192,4096]{1,0:T(8,128)(2,1)}, u32[]{:S(2)}, u32[]{:S(2)}) collective-permute-start(bf16[192,4096]{1,0:T(8,128)(2,1)} %norm_rows.7.refs_0_.x_ref), channel_id=1, source_target_pairs={{0,4},{1,5},{2,6},{3,7},{4,0},{5,1},{6,2},{7,3}} | collective-permute-start | bytes 4718600 | tf_op jit(solution)/shard_map/ppermute | solution.py:342
  348.7 2.5 collective-permute-start.23
  348.7 16.7 %copy-start.2 = (bf16[192,4096]{1,0:T(8,128)(2,1)}, bf16[192,4096]{1,0:T(8,128)(2,1)S(1)}, u32[]{:S(2)}) copy-start(bf16[192,4096]{1,0:T(8,128)(2,1)S(1)} %collective-permute-done.13.refs_1_) | copy-start | bytes 4718596
  363.1 433.4 %reduce-scatter.20.cloned.1.call-start = ((), (), s32[]{:S(2)}) async-start(), calls=%async_computation.13 | async-start | bytes 7864320 | tf_op jit(solution)/shard_map/reduce_scatter | solution.py:408
  364.6 35.6 %collective-permute-start.15 = (bf16[96,4096]{1,0:T(8,128)(2,1)S(1)}, bf16[96,4096]{1,0:T(8,128)(2,1)}, u32[]{:S(2)}, u32[]{:S(2)}) collective-permute-start(bf16[96,4096]{1,0:T(8,128)(2,1)S(1)} %slice.70), channel_id=1, source_target_pairs={{0,2},{1,3},{2,0},{3,1},{4,6},{5,7},{6,4},{7,5}} | collective-permute-start | bytes 2359304 | tf_op jit(solution)/shard_map/ppermute | solution.py:342
  365.5 36.5 %collective-permute-start.16 = (bf16[96,4096]{1,0:T(8,128)(2,1)S(1)}, bf16[96,4096]{1,0:T(8,128)(2,1)}, u32[]{:S(2)}, u32[]{:S(2)}) collective-permute-start(bf16[96,4096]{1,0:T(8,128)(2,1)S(1)} %slice.71), channel_id=1, source_target_pairs={{0,4},{1,5},{2,6},{3,7},{4,0},{5,1},{6,2},{7,3}} | collective-permute-start | bytes 2359304 | tf_op jit(solution)/shard_map/ppermute | solution.py:342
  366.7 1.2 collective-permute-start.18
  401.9 64.4 %collective-permute-start.19 = (bf16[192,4096]{1,0:T(8,128)(2,1)}, bf16[192,4096]{1,0:T(8,128)(2,1)S(1)}, u32[]{:S(2)}, u32[]{:S(2)}) collective-permute-start(bf16[192,4096]{1,0:T(8,128)(2,1)} %norm_rows.8.refs_0_.x_ref), channel_id=1, source_target_pairs={{0,2},{1,3},{2,0},{3,1},{4,6},{5,7},{6,4},{7,5}} | collective-permute-start | bytes 4718600 | tf_op jit(solution)/shard_map/ppermute | solution.py:342
  402.7 63.8 %collective-permute-start.20 = (bf16[192,4096]{1,0:T(8,128)(2,1)}, bf16[192,4096]{1,0:T(8,128)(2,1)}, u32[]{:S(2)}, u32[]{:S(2)}) collective-permute-start(bf16[192,4096]{1,0:T(8,128)(2,1)} %norm_rows.8.refs_0_.x_ref), channel_id=1, source_target_pairs={{0,4},{1,5},{2,6},{3,7},{4,0},{5,1},{6,2},{7,3}} | collective-permute-start | bytes 4718600 | tf_op jit(solution)/shard_map/ppermute | solution.py:342
  466.4 31.5 %copy-start.3 = (bf16[192,4096]{1,0:T(8,128)(2,1)}, bf16[192,4096]{1,0:T(8,128)(2,1)S(1)}, u32[]{:S(2)}) copy-start(bf16[192,4096]{1,0:T(8,128)(2,1)S(1)} %collective-permute-done.19.refs_1_) | copy-start | bytes 4718596
  495.8 304.7 %reduce-scatter.18.cloned.1.call-start = ((), (), s32[]{:S(2)}) async-start(), calls=%async_computation.12 | async-start | bytes 7864320 | tf_op jit(solution)/shard_map/reduce_scatter | solution.py:408
  497.1 33.9 %collective-permute-start.21 = (bf16[96,4096]{1,0:T(8,128)(2,1)S(1)}, bf16[96,4096]{1,0:T(8,128)(2,1)}, u32[]{:S(2)}, u32[]{:S(2)}) collective-permute-start(bf16[96,4096]{1,0:T(8,128)(2,1)S(1)} %slice.76), channel_id=1, source_target_pairs={{0,2},{1,3},{2,0},{3,1},{4,6},{5,7},{6,4},{7,5}} | collective-permute-start | bytes 2359304 | tf_op jit(solution)/shard_map/ppermute | solution.py:342
  497.9 35.0 %collective-permute-start.22 = (bf16[96,4096]{1,0:T(8,128)(2,1)S(1)}, bf16[96,4096]{1,0:T(8,128)(2,1)S(1)}, u32[]{:S(2)}, u32[]{:S(2)}) collective-permute-start(bf16[96,4096]{1,0:T(8,128)(2,1)S(1)} %slice.77), channel_id=1, source_target_pairs={{0,4},{1,5},{2,6},{3,7},{4,0},{5,1},{6,2},{7,3}} | collective-permute-start | bytes 2359304 | tf_op jit(solution)/shard_map/ppermute | solution.py:342
  533.8 64.0 %collective-permute-start.24 = (bf16[192,4096]{1,0:T(8,128)(2,1)}, bf16[192,4096]{1,0:T(8,128)(2,1)S(1)}, u32[]{:S(2)}, u32[]{:S(2)}) collective-permute-start(bf16[192,4096]{1,0:T(8,128)(2,1)} %norm_rows.9.refs_0_.x_ref), channel_id=1, source_target_pairs={{0,2},{1,3},{2,0},{3,1},{4,6},{5,7},{6,4},{7,5}} | collective-permute-start | bytes 4718600 | tf_op jit(solution)/shard_map/ppermute | solution.py:342
  534.1 63.7 %collective-permute-start.25 = (bf16[192,4096]{1,0:T(8,128)(2,1)}, bf16[192,4096]{1,0:T(8,128)(2,1)S(1)}, u32[]{:S(2)}, u32[]{:S(2)}) collective-permute-start(bf16[192,4096]{1,0:T(8,128)(2,1)} %norm_rows.9.refs_0_.x_ref), channel_id=1, source_target_pairs={{0,4},{1,5},{2,6},{3,7},{4,0},{5,1},{6,2},{7,3}} | collective-permute-start | bytes 4718600 | tf_op jit(solution)/shard_map/ppermute | solution.py:342
  597.8 30.2 %copy-start.4 = (bf16[192,4096]{1,0:T(8,128)(2,1)}, bf16[192,4096]{1,0:T(8,128)(2,1)S(1)}, u32[]{:S(2)}) copy-start(bf16[192,4096]{1,0:T(8,128)(2,1)S(1)} %collective-permute-done.24.refs_1_) | copy-start | bytes 4718596
  597.9 30.3 %copy-start.6 = (bf16[192,4096]{1,0:T(8,128)(2,1)}, bf16[192,4096]{1,0:T(8,128)(2,1)S(1)}, u32[]{:S(2)}) copy-start(bf16[192,4096]{1,0:T(8,128)(2,1)S(1)} %collective-permute-done.25.refs_2_) | copy-start | bytes 4718596
  628.1 176.6 %reduce-scatter.16.cloned.1.call-start = ((), (), s32[]{:S(2)}) async-start(), calls=%async_computation.11 | async-start | bytes 3932160 | tf_op jit(solution)/shard_map/reduce_scatter | solution.py:408
  628.2 26.3 %collective-permute-start.27 = (bf16[96,4096]{1,0:T(8,128)(2,1)S(1)}, bf16[96,4096]{1,0:T(8,128)(2,1)S(1)}, u32[]{:S(2)}, u32[]{:S(2)}) collective-permute-start(bf16[96,4096]{1,0:T(8,128)(2,1)S(1)} %slice.79), channel_id=1, source_target_pairs={{0,2},{1,3},{2,0},{3,1},{4,6},{5,7},{6,4},{7,5}} | collective-permute-start | bytes 2359304 | tf_op jit(solution)/shard_map/ppermute | solution.py:342
  711.2 123.3 %reduce-scatter.14.cloned.1.call-start = ((), (), s32[]{:S(2)}) async-start(), calls=%async_computation.10 | async-start | bytes 3932160 | tf_op jit(solution)/shard_map/reduce_scatter | solution.py:408
  712.6 26.0 %collective-permute-start.26 = (bf16[96,4096]{1,0:T(8,128)(2,1)S(1)}, bf16[96,4096]{1,0:T(8,128)(2,1)S(1)}, u32[]{:S(2)}, u32[]{:S(2)}) collective-permute-start(bf16[96,4096]{1,0:T(8,128)(2,1)S(1)} %slice.78), channel_id=1, source_target_pairs={{0,4},{1,5},{2,6},{3,7},{4,0},{5,1},{6,2},{7,3}} | collective-permute-start | bytes 2359304 | tf_op jit(solution)/shard_map/ppermute | solution.py:342
  (16 other events, 26.7 us)
Sparse Core Ops, SparseCore 0:
  9.4 70.1 all-gather.4
  81.4 89.7 all-gather.6
  174.1 63.5 reduce-scatter.7
  240.5 103.2 reduce-scatter.9
  363.2 107.8 reduce-scatter.11
  496.0 105.3 reduce-scatter.19
  628.2 75.0 reduce-scatter.17
  711.3 46.3 reduce-scatter.15
  794.1 40.3 reduce-scatter.13
